TPU v7x, 256 devices: a whole 4x4x8 slice. The times are simulated.
256 devices in a mesh: dom: 32 (over y, x, core), col: 8 (over z).
Axes of the slice: x: 4, y: 4, z: 8, core: 2. Of those that a mesh axis runs over, the one named last changes fastest.
Arguments:
- features: bfloat16 [262144, 1024], P('dom', 'col'), may hold values from -6 to 6
- requests: int32 [32, 32, 8], P('dom'), may hold values from 0 to 63
- counts: int32 [32, 32], P(None, 'dom'), may hold values from 0 to 8, as said below
- tile_block: int32 [512, 32], P('dom'), may hold values from 0 to 127
- local_nbr: int32 [65536, 128], P('dom'), may hold values from 0 to 127
- tile_count: int32 [512], P('dom'), may hold values from 1 to 32, as said below
- w_self: bfloat16 [1024, 1024], P('col'), may hold values from -0.125 to 0.125
- w_neigh: bfloat16 [1024, 1024], P('col'), may hold values from -0.75 to 0.75
Outputs:
- embeddings: bfloat16 [65536, 1024], P('dom', 'col')
Inputs may be any that keep to these rules, and one draw needn't show every extreme that they name: Each shard's counts over all partitions sum to 128; for every shard some partition has exactly 8. `tile_count`: on every shard some destination block uses all 32 tiles.
All inputs are finite; a program needn't handle non-finite values.
Results may differ from a plain program's by a relative error of at most 0.014.
Values may be sent and summed in bfloat16 or wider, within the bound.
No kernel may reach another device: no remote copies, remote signals or barrier semaphores. Data moves between devices by JAX's collectives and lax.ppermute only.
A program may use at most 128 MiB of HBM per device.

v0:
```python
import jax
import jax.numpy as jnp
from jax import lax
from jax.experimental import pallas as pl
from jax.experimental.pallas import tpu as pltpu
from jax.sharding import PartitionSpec as P


D = 1024
ROWS = 128
CAP = 8
TILES = 32
FAN_T = 4
FRONT = 128
RING = 4
N_SRC = 2 * RING
DST = 16
N_ITEMS = DST * TILES
SECTION = N_ITEMS + ROWS
UNROLL = 4
BF = jnp.bfloat16
F32 = jnp.float32
I32 = jnp.int32

VMEM = pl.BlockSpec(memory_space=pltpu.VMEM)
SMEM = pl.BlockSpec(memory_space=pltpu.SMEM)
ANY = pl.BlockSpec(memory_space=pl.ANY)


def dom_of(y, x, core):
    return (y * RING + x) * 2 + core


def meet_pairs(d, e):
    pairs = []
    for y in range(RING):
        for x in range(RING):
            for core in range(2):
                if core ^ e == 0:
                    pairs.append((dom_of(y, x, core), dom_of((y + d) % RING, x, 0)))
                else:
                    pairs.append((dom_of(y, x, core), dom_of(y, (x + d) % RING, 1)))
    return pairs


def ring_pairs(m):
    pairs = []
    for y in range(RING):
        for x in range(RING):
            pairs.append((dom_of(y, x, 0), dom_of(y, (x + m) % RING, 0)))
            pairs.append((dom_of(y, x, 1), dom_of((y + m) % RING, x, 1)))
    return pairs


def wrapped(v):
    return lax.rem(v + 2 * RING, RING)


def pack_kernel(me, req, feat, *refs):
    outs, (ft, stage, sem) = refs[:N_SRC], refs[N_SRC:]
    core, x, y = lax.rem(me[0], 2), lax.rem(me[0] // 2, RING), me[0] // (2 * RING)

    def turn(b, _):
        for u in range(8):
            ft[b * 8 + u] = feat[pl.ds((b * 8 + u) * ROWS, ROWS), :].T
        return 0

    lax.fori_loop(0, feat.shape[0] // ROWS // 8, turn, 0)
    copies = []
    for q in range(N_SRC):
        d, e = q // 2, q % 2
        to_one = lax.rem(core + e, 2)
        for m in range(RING):
            shard0 = dom_of(wrapped(y + d), wrapped(x - m), 0)
            shard1 = dom_of(wrapped(y - m), wrapped(x + d), 1)
            shard = jnp.where(to_one == 1, shard1, shard0)
            for s in range(CAP):
                stage[q, m * CAP + s] = ft[req[shard, s]]
        copy = pltpu.make_async_copy(stage.at[q], outs[q], sem.at[q])
        copy.start()
        copies.append(copy)
    for copy in copies:
        copy.wait()


def pack(me, requests, features):
    n_blk = features.shape[0] // ROWS
    return pl.pallas_call(
        pack_kernel,
        out_shape=[jax.ShapeDtypeStruct((RING * CAP, ROWS, ROWS), BF)] * N_SRC,
        in_specs=[SMEM, SMEM, VMEM],
        out_specs=[ANY] * N_SRC,
        scratch_shapes=[
            pltpu.VMEM((n_blk, ROWS, ROWS), BF),
            pltpu.VMEM((N_SRC, RING * CAP, ROWS, ROWS), BF),
            pltpu.SemaphoreType.DMA((N_SRC,)),
        ],
        cost_estimate=pl.CostEstimate(flops=10**9, bytes_accessed=10**7, transcendentals=0),
        name="pack",
    )(me, requests, features)


def tables_kernel(me, nbr, ws, wn, nbr_t, w_t):
    half = ROWS // 2

    def turn_nbr(i, _):
        turned = nbr[pl.ds(i * ROWS, ROWS), :].T
        nbr_t[pl.ds(i * half, half), :] = turned[:half] + turned[half:] * 65536
        return 0

    lax.fori_loop(0, nbr.shape[0] // ROWS, turn_nbr, 0, unroll=2)
    for core, w in enumerate((ws, wn)):

        @pl.when(lax.rem(me[0], 2) == core)
        def _():
            for j in range(D // ROWS):
                w_t[j * ROWS : (j + 1) * ROWS, :] = w[:, j * ROWS : (j + 1) * ROWS].T


def tables(me, local_nbr, w_self, w_neigh):
    return pl.pallas_call(
        tables_kernel,
        out_shape=(
            jax.ShapeDtypeStruct((local_nbr.shape[0] // 2, ROWS), I32),
            jax.ShapeDtypeStruct((D, ROWS), BF),
        ),
        in_specs=[SMEM] + [VMEM] * 3,
        out_specs=(VMEM, VMEM),
        cost_estimate=pl.CostEstimate(flops=10**9, bytes_accessed=10**7, transcendentals=0),
        name="tables",
    )(me, local_nbr, w_self, w_neigh)


def plan_kernel(me, cnt, tile_block, tile_count, todo, slot, size):
    core, x, y = me[0] & 1, (me[0] >> 1) & (RING - 1), me[0] >> 3
    for m in range(RING + 1):
        size[m] = m * SECTION

    def owner(o, p):
        co, xo, yo = o & 1, (o >> 1) & (RING - 1), o >> 3
        q0 = ((y - yo) & (RING - 1)) * 2 + co
        q1 = ((x - xo) & (RING - 1)) * 2 + 1 - co
        q = jnp.where(core == 0, q0, q1)
        m = jnp.where(core == 0, xo - x, yo - y) & (RING - 1)
        first = q * 32 + m * CAP

        def one(s, p):
            slot[p] = first + s
            return p + 1

        return lax.fori_loop(0, cnt[o], one, p)

    lax.fori_loop(0, 2 * RING * RING, owner, jnp.int32(0))

    def block(i, _):
        v = slot[i]
        for m in range(RING):
            todo[m * SECTION + N_ITEMS + 1 + i] = jnp.where((v >> 3) & (RING - 1) == m, v, -1)
        used = tile_count[i]

        def tile(h, _):
            vs = [slot[tile_block[i, h * UNROLL + u]] for u in range(UNROLL)]
            for u, v in enumerate(vs):
                t = h * UNROLL + u
                m = jnp.where(t < used, (v >> 3) & (RING - 1), RING)
                n = size[m]
                todo[n] = v + 256 * i + 4096 * t
                size[m] = n + 1
            return 0

        lax.fori_loop(0, (used + UNROLL - 1) // UNROLL, tile, 0)
        return 0

    lax.fori_loop(0, DST, block, 0)
    for m in range(RING):
        todo[m * SECTION + N_ITEMS] = size[m] - m * SECTION


def plan(me, counts, tile_block, tile_count):
    return pl.pallas_call(
        plan_kernel,
        out_shape=jax.ShapeDtypeStruct(((RING + 1) * SECTION,), I32),
        in_specs=[SMEM] * 4,
        out_specs=SMEM,
        scratch_shapes=[pltpu.SMEM((FRONT,), I32), pltpu.SMEM((RING + 1,), I32)],
        cost_estimate=pl.CostEstimate(flops=2 * 10**9, bytes_accessed=10**6, transcendentals=0),
        name="plan",
    )(me, counts, tile_block, tile_count)


def own_kernel(*refs):
    lists, src, outs = refs[:RING], refs[RING : RING + N_SRC], refs[RING + N_SRC : 2 * RING + N_SRC]
    stage, sem, sem_out = refs[2 * RING + N_SRC :]

    def copy_of(q, n, v):
        return pltpu.make_async_copy(src[q].at[v & 31], stage.at[n], sem)

    for m in range(RING):

        def start(i, _):
            v = lists[m][m * SECTION + N_ITEMS + 1 + i]
            for q in range(N_SRC):

                @pl.when(v >> 5 == q)
                def _():
                    copy_of(q, m * DST + i, v).start()

            @pl.when(v < 0)
            def _():
                stage[m * DST + i] = jnp.zeros((ROWS, ROWS), BF)

            return 0

        lax.fori_loop(0, DST, start, 0)
    for m in range(RING):

        def finish(i, _):
            @pl.when(lists[m][m * SECTION + N_ITEMS + 1 + i] >= 0)
            def _():
                copy_of(0, 0, 0).wait()

            return 0

        lax.fori_loop(0, DST, finish, 0)
    copies = [
        pltpu.make_async_copy(stage.at[pl.ds(m * DST, DST)], outs[m], sem_out.at[m]) for m in range(RING)
    ]
    for copy in copies:
        copy.start()
    for copy in copies:
        copy.wait()


def own_rows(lists, sources):
    return pl.pallas_call(
        own_kernel,
        out_shape=[jax.ShapeDtypeStruct((DST, ROWS, ROWS), BF)] * RING,
        in_specs=[SMEM] * RING + [ANY] * N_SRC,
        out_specs=[ANY] * RING,
        scratch_shapes=[
            pltpu.VMEM((RING * DST, ROWS, ROWS), BF),
            pltpu.SemaphoreType.DMA,
            pltpu.SemaphoreType.DMA((RING,)),
        ],
        cost_estimate=pl.CostEstimate(flops=10**9, bytes_accessed=10**7, transcendentals=0),
        name="own_rows",
    )(*lists, *sources)


def agg_kernel(*refs):
    lists, src, nbr = refs[:RING], refs[RING : RING + N_SRC], refs[RING + N_SRC : 2 * RING + N_SRC]
    outs, (blocks, acc, sem) = refs[2 * RING + N_SRC : 3 * RING + N_SRC], refs[3 * RING + N_SRC :]
    fetch = [pltpu.make_async_copy(src[q], blocks.at[pl.ds(q * 32, 32)], sem.at[q]) for q in range(N_SRC)]
    for copy in fetch:
        copy.start()

    def clear(n, _):
        acc[n] = jnp.zeros((ROWS, ROWS), F32)
        return 0

    lax.fori_loop(0, RING * DST + 1, clear, 0, unroll=5)
    iota = lax.broadcasted_iota(I32, (ROWS, ROWS), 0).astype(F32).astype(BF)
    one, zero = jnp.ones((), BF), jnp.zeros((), BF)
    for copy in fetch:
        copy.wait()

    for m in (1, 2, 3, 0):
        todo = lists[m]
        n_item = todo[m * SECTION + N_ITEMS]

        def some(h, _):
            parts = []
            for u in range(UNROLL):
                n = h * UNROLL + u
                item = jnp.where(n < n_item, todo[m * SECTION + n], 0)
                blk = item & 255
                i = (item >> 8) & 15
                t = item >> 12
                dst = jnp.where(n < n_item, m * DST + i, RING * DST)
                row0 = i * (ROWS // 2) + (t & 15) * FAN_T
                shift = (t >> 4) * 16
                total = None
                for f in range(FAN_T):
                    row = (nbr[m][pl.ds(row0 + f, 1), :] >> shift) & 65535
                    hit = jnp.where(iota == row.astype(F32).astype(BF), one, zero)
                    total = hit if total is None else total + hit
                parts.append((dst, jnp.dot(blocks[blk], total, preferred_element_type=F32)))
            for dst, part in parts:
                acc[dst] += part
            return 0

        lax.fori_loop(0, (n_item + UNROLL - 1) // UNROLL, some, 0)
    for m in range(RING):

        def leave(n, _):
            outs[m][n] = acc[m * DST + n].astype(BF)
            return 0

        lax.fori_loop(0, DST, leave, 0, unroll=4)


def aggregate(lists, sources, nbrs):
    return pl.pallas_call(
        agg_kernel,
        out_shape=[jax.ShapeDtypeStruct((DST, ROWS, ROWS), BF)] * RING,
        in_specs=[SMEM] * RING + [ANY] * N_SRC + [VMEM] * RING,
        out_specs=[VMEM] * RING,
        scratch_shapes=[
            pltpu.VMEM((N_SRC * 32, ROWS, ROWS), BF),
            pltpu.VMEM((RING * DST + 1, ROWS, ROWS), F32),
            pltpu.SemaphoreType.DMA((N_SRC,)),
        ],
        cost_estimate=pl.CostEstimate(flops=10**10, bytes_accessed=2 * 10**7, transcendentals=0),
        name="agg",
    )(*lists, *sources, *nbrs)


def join_own_kernel(a, b, c, d, out):
    for n in range(DST):
        total = a[n].astype(F32) + b[n].astype(F32) + c[n].astype(F32) + d[n].astype(F32)
        out[n] = total.astype(BF)


def join_agg_kernel(tile_count, a, b, c, d, out):
    for n in range(DST):
        total = a[n].astype(F32) + b[n].astype(F32) + c[n].astype(F32) + d[n].astype(F32)
        out[n] = (total / (tile_count[n] * FAN_T).astype(F32)).astype(BF)


def join(kernel, scalars, parts):
    return pl.pallas_call(
        kernel,
        out_shape=jax.ShapeDtypeStruct((DST, ROWS, ROWS), BF),
        in_specs=[SMEM] * len(scalars) + [VMEM] * RING,
        out_specs=VMEM,
        cost_estimate=pl.CostEstimate(flops=10**9, bytes_accessed=5 * 10**6, transcendentals=0),
    )(*scalars, *parts)


def gather_kernel(*refs):
    *parts, out = refs
    for k, part in enumerate(parts):
        out[k] = part[...]


def gather_weights(parts):
    return pl.pallas_call(
        gather_kernel,
        out_shape=jax.ShapeDtypeStruct((len(parts), *parts[0].shape), BF),
        in_specs=[VMEM] * len(parts),
        out_specs=VMEM,
        cost_estimate=pl.CostEstimate(flops=10**9, bytes_accessed=5 * 10**6, transcendentals=0),
        name="gather_weights",
    )(*parts)


def project_kernel(me, column, xs, xa, w_mine, w_other, out, hid):
    n_col = xs.shape[0]
    self_first = me[0] & 1 == 0
    for b in range(xs.shape[1]):
        for n0 in range(0, D, 256):
            total = None
            for k in range(n_col):
                group = (column[0] + n_col - k) & (n_col - 1)
                s, a = xs[group, b], xa[group, b]
                x = jnp.concatenate([jnp.where(self_first, s, a), jnp.where(self_first, a, s)], axis=0)
                w = jnp.concatenate([w_mine[k, n0 : n0 + 256, :], w_other[k, n0 : n0 + 256, :]], axis=1)
                part = jnp.dot(w, x, preferred_element_type=F32)
                total = part if total is None else total + part
            hid[n0 : n0 + 256, :] = jnp.maximum(total, 0.0)
        h = hid[...]
        scale = jnp.sqrt(0.25 + jnp.sum(h * h, axis=0, keepdims=True) / D)
        for j in range(n_col):
            piece = hid[j * ROWS : (j + 1) * ROWS, :] / scale
            out[j, b * ROWS : (b + 1) * ROWS, :] = piece.T.astype(BF)


def project(me, column, xs, xa, w_mine, w_other):
    n_col, n_blk = xs.shape[:2]
    return pl.pallas_call(
        project_kernel,
        out_shape=jax.ShapeDtypeStruct((n_col, n_blk * ROWS, ROWS), BF),
        in_specs=[SMEM] * 2 + [VMEM] * 4,
        out_specs=VMEM,
        scratch_shapes=[pltpu.VMEM((D, ROWS), F32)],
        cost_estimate=pl.CostEstimate(flops=10**9, bytes_accessed=5 * 10**6, transcendentals=0),
        name="project",
    )(me, column, xs, xa, w_mine, w_other)


def body(features, requests, counts, tile_block, local_nbr, tile_count, w_self, w_neigh):
    n_col = lax.axis_size("col")
    me = lax.axis_index("dom").reshape(1).astype(I32)
    column = lax.axis_index("col").reshape(1).astype(I32)
    packed = pack(me, requests[0], features)
    sources = [packed[0]]
    for q in range(1, N_SRC):
        sources.append(lax.ppermute(packed[q], "dom", meet_pairs(q // 2, q % 2)))

    todo = plan(me, counts[:, 0], tile_block, tile_count)
    nbr_t, w_t = tables(me, local_nbr, w_self, w_neigh)
    lists, nbrs = [todo], [nbr_t]
    for m in range(1, RING):
        lists.append(lax.ppermute(todo, "dom", ring_pairs(m)))
        nbrs.append(lax.ppermute(nbr_t, "dom", ring_pairs(m)))
    w_all = [w_t]
    for k in range(1, n_col):
        w_all.append(lax.ppermute(w_t, "col", [(i, (i + k) % n_col) for i in range(n_col)]))
    w_mine = gather_weights(w_all)
    w_other = lax.ppermute(w_mine, "dom", [(i, i ^ 1) for i in range(lax.axis_size("dom"))])

    own_parts = own_rows(lists, sources)
    own_here = [own_parts[0]]
    for m in range(1, RING):
        own_here.append(lax.ppermute(own_parts[m], "dom", ring_pairs(RING - m)))
    agg_parts = aggregate(lists, sources, nbrs)
    agg_here = [agg_parts[0]]
    for m in range(1, RING):
        agg_here.append(lax.ppermute(agg_parts[m], "dom", ring_pairs(RING - m)))

    def to_rows(x):
        return lax.all_to_all(x.reshape(n_col, DST // n_col, ROWS, ROWS), "col", 0, 0, tiled=True)

    xs = to_rows(join(join_own_kernel, (), own_here))
    xa = to_rows(join(join_agg_kernel, (tile_count,), agg_here))
    y = project(me, column, xs, xa, w_mine, w_other)
    return lax.all_to_all(y, "col", 0, 0, tiled=True).reshape(-1, ROWS)


def solution(mesh):
    return jax.shard_map(
        body,
        mesh=mesh,
        in_specs=(
            P("dom", "col"),
            P("dom", None, None),
            P(None, "dom"),
            P("dom", None),
            P("dom", None),
            P("dom"),
            P("col", None),
            P("col", None),
        ),
        out_specs=P("dom", "col"),
        check_vma=False,
    )
```

profile of v0, /device:TPU:2, one launch (start us, length us, event | category | flops | bytes accessed | tf_op | source)
XLA Modules:
  0.0 230.2 jit_solution(4957710951046326589)
XLA Ops:
  1.4 6.1 %pack.1 = (bf16[32,128,128]{2,1,0:T(8,128)(2,1)}, bf16[32,128,128]{2,1,0:T(8,128)(2,1)}, bf16[32,128,128]{2,1,0:T(8,128)(2,1)}, bf16[32,128,128]{2,1,0:T(8,128)(...) custom-call(s32[1]{0:T(128)} %bitcast.me, ...), custom_call_target="tpu_custom_call" | custom-call | flops 1000000000 | bytes 10000000 | tf_op jit(solution)/shard_map/pack/pallas_call | solution.py:88
  9.2 5.4 %plan.1.refs_0_ = s32[3200]{0:T(1024)} custom-call(s32[1]{0:T(128)} %bitcast.me, s32[32]{0:T(128)} %bitcast.11, s32[16,32]{1,0:T(8,128)} %tile_block.1, s32[16]{0:T(128)} %tile_count.3), custom_call_target="tpu_custom_call" | custom-call | flops 2000000000 | bytes 1000000 | tf_op jit(solution)/shard_map/plan/pallas_call | solution.py:180
  18.1 3.2 %tables.1 = (s32[1024,128]{1,0:T(8,128)}, bf16[1024,128]{1,0:T(8,128)(2,1)}) custom-call(s32[1]{0:T(128)} %bitcast.me, s32[2048,128]{1,0:T(8,128)} %nbr.1, bf16[128,1024]{1,0:T(8,128)(2,1)} %ws.1, bf16[128,1024]{1,0:T(8,128)(2,1)} %wn.1), custom_call_target="tpu_custom_call" | custom-call | flops 1000000000 | bytes 10000000 | tf_op jit(solution)/shard_map/tables/pallas_call | solution.py:121
  21.6 4.2 %collective-permute-start.14 = (s32[1024,128]{1,0:T(8,128)}, s32[1024,128]{1,0:T(8,128)S(1)}, u32[]{:S(2)}, u32[]{:S(2)}) collective-permute-start(s32[1024,128]{1,0:T(8,128)} %get-tuple-element.35.refs_12_), channel_id=1, source_target_pairs={{0,32},{8,136},{16,48},{24,152},{32,0},{40,168},{48,16},{56,184},{... | collective-permute-start | bytes 1572872 | tf_op jit(solution)/shard_map/ppermute | solution.py:405
  25.8 5.3 %collective-permute-done.13.refs_13_ = s32[1024,128]{1,0:T(8,128)S(1)} collective-permute-done((s32[1024,128]{1,0:T(8,128)}, s32[1024,128]{1,0:T(8,128)S(1)}, u32[]{:S(2)}, u32[]{:S(2)}) %collective-permute-start.13) | collective-permute-done | bytes 524320 | tf_op jit(solution)/shard_map/ppermute | solution.py:405
  31.9 7.2 %collective-permute-start.5 = (bf16[32,128,128]{2,1,0:T(8,128)(2,1)}, bf16[32,128,128]{2,1,0:T(8,128)(2,1)S(1)}, u32[]{:S(2)}, u32[]{:S(2)}) collective-permute-start(bf16[32,128,128]{2,1,0:T(8,128)(2,1)} %get-tuple-element.26), channel_id=1, source_target_pairs={{0,24},{8,64},{16,40},{24,80},{32,56},{40,96},{48,8},{56,112},{64,... | collective-permute-start | bytes 3145736 | tf_op jit(solution)/shard_map/ppermute | solution.py:398
  42.3 2.8 %collective-permute-start.9 = (bf16[32,128,128]{2,1,0:T(8,128)(2,1)}, bf16[32,128,128]{2,1,0:T(8,128)(2,1)}, u32[]{:S(2)}, u32[]{:S(2)}) collective-permute-start(bf16[32,128,128]{2,1,0:T(8,128)(2,1)} %get-tuple-element.30), channel_id=1, source_target_pairs={{0,56},{8,192},{16,8},{24,208},{32,24},{40,224},{48,40},{56,240},{... | collective-permute-start | bytes 3145736 | tf_op jit(solution)/shard_map/ppermute | solution.py:398
  45.1 27.3 %collective-permute-done.5.refs_7_ = bf16[32,128,128]{2,1,0:T(8,128)(2,1)S(1)} collective-permute-done((bf16[32,128,128]{2,1,0:T(8,128)(2,1)}, bf16[32,128,128]{2,1,0:T(8,128)(2,1)S(1)}, u32[]{:S(2)}, u32[]{:S(2)}) %collective-permute-start.5) | collective-permute-done | bytes 1048608 | tf_op jit(solution)/shard_map/ppermute | solution.py:398
  72.4 1.9 collective-permute-start.19
  74.3 3.3 %collective-permute-start.20 = (bf16[1024,128]{1,0:T(8,128)(2,1)}, bf16[1024,128]{1,0:T(8,128)(2,1)}, u32[]{:S(2)}, u32[]{:S(2)}) collective-permute-start(bf16[1024,128]{1,0:T(8,128)(2,1)} %get-tuple-element.40.refs_0_), channel_id=1, source_target_pairs={{0,2},{1,3},{2,4},{3,5},{4,6},{5,7},{6,0},{7,1},{8,10},{9,11},{10,... | collective-permute-start | bytes 786440 | tf_op jit(solution)/shard_map/ppermute | solution.py:408
  77.6 4.0 %collective-permute-start.21 = (bf16[1024,128]{1,0:T(8,128)(2,1)}, bf16[1024,128]{1,0:T(8,128)(2,1)}, u32[]{:S(2)}, u32[]{:S(2)}) collective-permute-start(bf16[1024,128]{1,0:T(8,128)(2,1)} %get-tuple-element.40.refs_0_), channel_id=1, source_target_pairs={{0,3},{1,4},{2,5},{3,6},{4,7},{5,0},{6,1},{7,2},{8,11},{9,12},{10,... | collective-permute-start | bytes 786440 | tf_op jit(solution)/shard_map/ppermute | solution.py:408
  81.6 4.0 %collective-permute-done.8.refs_10_ = bf16[32,128,128]{2,1,0:T(8,128)(2,1)} collective-permute-done((bf16[32,128,128]{2,1,0:T(8,128)(2,1)}, bf16[32,128,128]{2,1,0:T(8,128)(2,1)}, u32[]{:S(2)}, u32[]{:S(2)}) %collective-permute-start.8) | collective-permute-done | bytes 1048608 | tf_op jit(solution)/shard_map/ppermute | solution.py:398
  85.7 7.2 %collective-permute-start.22 = (bf16[1024,128]{1,0:T(8,128)(2,1)}, bf16[1024,128]{1,0:T(8,128)(2,1)}, u32[]{:S(2)}, u32[]{:S(2)}) collective-permute-start(bf16[1024,128]{1,0:T(8,128)(2,1)} %get-tuple-element.40.refs_0_), channel_id=1, source_target_pairs={{0,4},{1,5},{2,6},{3,7},{4,0},{5,1},{6,2},{7,3},{8,12},{9,13},{10,... | collective-permute-start | bytes 786440 | tf_op jit(solution)/shard_map/ppermute | solution.py:408
  93.6 14.9 %agg.1 = (bf16[16,128,128]{2,1,0:T(8,128)(2,1)}, bf16[16,128,128]{2,1,0:T(8,128)(2,1)}, bf16[16,128,128]{2,1,0:T(8,128)(2,1)}, bf16[16,128,128]{2,1,0:T(8,128)(2,1)}) custom-call(s32[3200]{0:T(1024)} %plan.1.refs_0_, s32[3200]{0:T(1024)} %copy-done.9, s32[3200]{0:T(1024)} %copy-done.10, s32[3200]{0:T(1024)} %copy-done.11, ...), custom_call_target="tpu_custom_call" | custom-call | flops 10000000000 | bytes 20000000 | tf_op jit(solution)/shard_map/agg/pallas_call | solution.py:303
  108.6 4.9 %collective-permute-start.16 = (bf16[16,128,128]{2,1,0:T(8,128)(2,1)}, bf16[16,128,128]{2,1,0:T(8,128)(2,1)S(1)}, u32[]{:S(2)}, u32[]{:S(2)}) collective-permute-start(bf16[16,128,128]{2,1,0:T(8,128)(2,1)} %get-tuple-element.37), channel_id=1, source_target_pairs={{0,48},{8,200},{16,0},{24,216},{32,16},{40,232},{48,32},{56,248},{... | collective-permute-start | bytes 1572872 | tf_op jit(solution)/shard_map/ppermute | solution.py:419
  113.5 2.5 %collective-permute-start.17 = (bf16[16,128,128]{2,1,0:T(8,128)(2,1)}, bf16[16,128,128]{2,1,0:T(8,128)(2,1)S(1)}, u32[]{:S(2)}, u32[]{:S(2)}) collective-permute-start(bf16[16,128,128]{2,1,0:T(8,128)(2,1)} %get-tuple-element.38), channel_id=1, source_target_pairs={{0,32},{8,136},{16,48},{24,152},{32,0},{40,168},{48,16},{56,184},{... | collective-permute-start | bytes 1572872 | tf_op jit(solution)/shard_map/ppermute | solution.py:419
  116.0 7.1 %collective-permute-start.24 = (bf16[1024,128]{1,0:T(8,128)(2,1)S(1)}, bf16[1024,128]{1,0:T(8,128)(2,1)S(1)}, u32[]{:S(2)}, u32[]{:S(2)}) collective-permute-start(bf16[1024,128]{1,0:T(8,128)(2,1)S(1)} %copy-done.6), channel_id=1, source_target_pairs={{0,6},{1,7},{2,0},{3,1},{4,2},{5,3},{6,4},{7,5},{8,14},{9,15},{10,... | collective-permute-start | bytes 786440 | tf_op jit(solution)/shard_map/ppermute | solution.py:408
  124.9 9.5 %collective-permute-done.24.refs_6_ = bf16[1024,128]{1,0:T(8,128)(2,1)S(1)} collective-permute-done((bf16[1024,128]{1,0:T(8,128)(2,1)S(1)}, bf16[1024,128]{1,0:T(8,128)(2,1)S(1)}, u32[]{:S(2)}, u32[]{:S(2)}) %collective-permute-start.24) | collective-permute-done | bytes 262176 | tf_op jit(solution)/shard_map/ppermute | solution.py:408
  134.3 5.7 %collective-permute-done.25.refs_7_ = bf16[1024,128]{1,0:T(8,128)(2,1)S(1)} collective-permute-done((bf16[1024,128]{1,0:T(8,128)(2,1)S(1)}, bf16[1024,128]{1,0:T(8,128)(2,1)S(1)}, u32[]{:S(2)}, u32[]{:S(2)}) %collective-permute-start.25) | collective-permute-done | bytes 262176 | tf_op jit(solution)/shard_map/ppermute | solution.py:408
  140.7 3.0 %gather_weights.1.w_mine = bf16[8,1024,128]{2,1,0:T(8,128)(2,1)} custom-call(bf16[1024,128]{1,0:T(8,128)(2,1)} %get-tuple-element.40.refs_0_, bf16[1024,128]{1,0:T(8,128)(2,1)} %collective-permute-done.19.refs_1_, bf16[1024,128]{1,0:T(8,128)(2,1)} %collective-permute-done.20.refs_2_, bf16[1024,128]{1,0:T(8,128)(2,1)} %collective-permute-done.21.refs_3_, ...), custom_call_target="tpu_custom_call" | custom-call | flops 1000000000 | bytes 5000000 | tf_op jit(solution)/shard_map/gather_weights/pallas_call | solution.py:347
  145.1 2.6 %shard_map.83 = bf16[16,128,128]{2,1,0:T(8,128)(2,1)} custom-call(s32[16]{0:T(128)} %tile_count.3, bf16[16,128,128]{2,1,0:T(8,128)(2,1)} %get-tuple-element.36.a, bf16[16,128,128]{2,1,0:T(8,128)(2,1)} %copy-done.15, bf16[16,128,128]{2,1,0:T(8,128)(2,1)} %copy-done.16, bf16[16,128,128]{2,1,0:T(8,128)(2,1)} %collective-permute-done.18.d), custom_call_target="tpu_custom_call" | custom-call | flops 1000000000 | bytes 5000000 | tf_op jit(solution)/shard_map/pallas_call | solution.py:331
  147.7 4.1 %all-to-all-start.1 = ((bf16[8,2,128,128]{3,2,1,0:T(8,128)(2,1)}), bf16[8,2,128,128]{3,2,1,0:T(8,128)(2,1)S(1)}, u32[]{:S(2)}, u32[]{:S(2)}) async-start(bf16[8,2,128,128]{3,2,1,0:T(8,128)(2,1)} %bitcast.8), calls=%async_computation.1 | async-start | bytes 1048576 | tf_op jit(solution)/shard_map/all_to_all | solution.py:422
  151.8 5.1 %own_rows.1 = (bf16[16,128,128]{2,1,0:T(8,128)(2,1)}, bf16[16,128,128]{2,1,0:T(8,128)(2,1)}, bf16[16,128,128]{2,1,0:T(8,128)(2,1)}, bf16[16,128,128]{2,1,0:T(8,128)(2,1)}) custom-call(s32[3200]{0:T(1024)} %plan.1.refs_0_, s32[3200]{0:T(1024)} %copy-done.9, s32[3200]{0:T(1024)} %copy-done.10, s32[3200]{0:T(1024)} %copy-done.11, ...), custom_call_target="tpu_custom_call" | custom-call | flops 1000000000 | bytes 10000000 | tf_op jit(solution)/shard_map/own_rows/pallas_call | solution.py:235
  156.9 1.9 collective-permute-start.10
  159.7 2.5 %collective-permute-start.12 = (bf16[16,128,128]{2,1,0:T(8,128)(2,1)}, bf16[16,128,128]{2,1,0:T(8,128)(2,1)}, u32[]{:S(2)}, u32[]{:S(2)}) collective-permute-start(bf16[16,128,128]{2,1,0:T(8,128)(2,1)} %get-tuple-element.34), channel_id=1, source_target_pairs={{0,16},{8,72},{16,32},{24,88},{32,48},{40,104},{48,0},{56,120},{64... | collective-permute-start | bytes 1572872 | tf_op jit(solution)/shard_map/ppermute | solution.py:415
  162.2 4.1 %collective-permute-done.10.b = bf16[16,128,128]{2,1,0:T(8,128)(2,1)S(1)} collective-permute-done((bf16[16,128,128]{2,1,0:T(8,128)(2,1)}, bf16[16,128,128]{2,1,0:T(8,128)(2,1)S(1)}, u32[]{:S(2)}, u32[]{:S(2)}) %collective-permute-start.10) | collective-permute-done | bytes 524320 | tf_op jit(solution)/shard_map/ppermute | solution.py:415
  166.4 6.3 %collective-permute-done.11.c = bf16[16,128,128]{2,1,0:T(8,128)(2,1)} collective-permute-done((bf16[16,128,128]{2,1,0:T(8,128)(2,1)}, bf16[16,128,128]{2,1,0:T(8,128)(2,1)}, u32[]{:S(2)}, u32[]{:S(2)}) %collective-permute-start.11) | collective-permute-done | bytes 524320 | tf_op jit(solution)/shard_map/ppermute | solution.py:415
  174.2 2.6 %shard_map.82 = bf16[16,128,128]{2,1,0:T(8,128)(2,1)} custom-call(bf16[16,128,128]{2,1,0:T(8,128)(2,1)} %get-tuple-element.31.a, bf16[16,128,128]{2,1,0:T(8,128)(2,1)} %copy-done.17, bf16[16,128,128]{2,1,0:T(8,128)(2,1)} %collective-permute-done.11.c, bf16[16,128,128]{2,1,0:T(8,128)(2,1)} %collective-permute-done.12.d), custom_call_target="tpu_custom_call" | custom-call | flops 1000000000 | bytes 5000000 | tf_op jit(solution)/shard_map/pallas_call | solution.py:331
  176.8 7.2 %all-to-all-start = ((bf16[8,2,128,128]{3,2,1,0:T(8,128)(2,1)}), bf16[8,2,128,128]{3,2,1,0:T(8,128)(2,1)S(1)}, u32[]{:S(2)}, u32[]{:S(2)}) async-start(bf16[8,2,128,128]{3,2,1,0:T(8,128)(2,1)} %bitcast.9), calls=%async_computation | async-start | bytes 1048576 | tf_op jit(solution)/shard_map/all_to_all | solution.py:422
  184.0 17.4 %all-to-all-done.xs = bf16[8,2,128,128]{3,2,1,0:T(8,128)(2,1)S(1)} async-done(((bf16[8,2,128,128]{3,2,1,0:T(8,128)(2,1)}), bf16[8,2,128,128]{3,2,1,0:T(8,128)(2,1)S(1)}, u32[]{:S(2)}, u32[]{:S(2)}) %all-to-all-start) | async-done | bytes 524320 | tf_op jit(solution)/shard_map/all_to_all | solution.py:422
  202.2 5.9 %project.1 = bf16[8,256,128]{2,1,0:T(8,128)(2,1)} custom-call(s32[1]{0:T(128)} %bitcast.me, s32[1]{0:T(128)} %bitcast.1.column, bf16[8,2,128,128]{3,2,1,0:T(8,128)(2,1)} %copy-done.2, bf16[8,2,128,128]{3,2,1,0:T(8,128)(2,1)} %copy-done.1, bf16[8,1024,128]{2,1,0:T(8,128)(2,1)} %gather_weights.1.w_mine, bf16[8,1024,128]{2,1,0:T(8,128)(2,1)} %copy-done), custom_call_target="tpu_custom_call" | custom-call | flops 1000000000 | bytes 5000000 | tf_op jit(solution)/shard_map/project/pallas_call | solution.py:380
  208.1 21.3 %all_to_all.15 = bf16[8,256,128]{2,1,0:T(8,128)(2,1)S(1)} all-to-all(bf16[8,256,128]{2,1,0:T(8,128)(2,1)} %project.1), channel_id=1, replica_groups=mesh['dom'=32,'col'=8] {'col'}, dimensions={0} | all-to-all | bytes 1048576 | tf_op jit(solution)/shard_map/all_to_all | solution.py:427
  (74 shorter events, 19.4 us)
Async XLA Ops:
  7.5 33.6 %collective-permute-start.3 = (bf16[32,128,128]{2,1,0:T(8,128)(2,1)}, bf16[32,128,128]{2,1,0:T(8,128)(2,1)S(1)}, u32[]{:S(2)}, u32[]{:S(2)}) collective-permute-start(bf16[32,128,128]{2,1,0:T(8,128)(2,1)} %get-tuple-element.24), channel_id=1, source_target_pairs={{0,8},{8,0},{16,24},{24,16},{32,40},{40,32},{48,56},{56,48},{64,72... | collective-permute-start | bytes 3145736 | tf_op jit(solution)/shard_map/ppermute | solution.py:398
  7.6 34.8 %collective-permute-start.4 = (bf16[32,128,128]{2,1,0:T(8,128)(2,1)}, bf16[32,128,128]{2,1,0:T(8,128)(2,1)S(1)}, u32[]{:S(2)}, u32[]{:S(2)}) collective-permute-start(bf16[32,128,128]{2,1,0:T(8,128)(2,1)} %get-tuple-element.25), channel_id=1, source_target_pairs={{0,64},{8,24},{16,80},{24,40},{32,96},{40,56},{48,112},{56,8},{64,... | collective-permute-start | bytes 3145736 | tf_op jit(solution)/shard_map/ppermute | solution.py:398
  14.6 6.7 %collective-permute-start = (s32[3200]{0:T(1024)}, s32[3200]{0:T(1024)S(1)}, u32[]{:S(2)}, u32[]{:S(2)}) collective-permute-start(s32[3200]{0:T(1024)} %plan.1.refs_0_), channel_id=1, source_target_pairs={{0,16},{8,72},{16,32},{24,88},{32,48},{40,104},{48,0},{56,120},{64... | collective-permute-start | bytes 38408 | tf_op jit(solution)/shard_map/ppermute | solution.py:404
  15.8 5.8 %collective-permute-start.1 = (s32[3200]{0:T(1024)}, s32[3200]{0:T(1024)S(1)}, u32[]{:S(2)}, u32[]{:S(2)}) collective-permute-start(s32[3200]{0:T(1024)} %plan.1.refs_0_), channel_id=1, source_target_pairs={{0,32},{8,136},{16,48},{24,152},{32,0},{40,168},{48,16},{56,184},{... | collective-permute-start | bytes 38408 | tf_op jit(solution)/shard_map/ppermute | solution.py:404
  16.4 9.5 %collective-permute-start.2 = (s32[3200]{0:T(1024)}, s32[3200]{0:T(1024)S(1)}, u32[]{:S(2)}, u32[]{:S(2)}) collective-permute-start(s32[3200]{0:T(1024)} %plan.1.refs_0_), channel_id=1, source_target_pairs={{0,48},{8,200},{16,0},{24,216},{32,16},{40,232},{48,32},{56,248},{... | collective-permute-start | bytes 38408 | tf_op jit(solution)/shard_map/ppermute | solution.py:404
  21.3 72.3 %copy-start.9 = (s32[3200]{0:T(1024)}, s32[3200]{0:T(1024)S(1)}, u32[]{:S(2)}) copy-start(s32[3200]{0:T(1024)S(1)} %collective-permute-done.refs_1_) | copy-start | bytes 38404
  21.3 9.8 %collective-permute-start.13 = (s32[1024,128]{1,0:T(8,128)}, s32[1024,128]{1,0:T(8,128)S(1)}, u32[]{:S(2)}, u32[]{:S(2)}) collective-permute-start(s32[1024,128]{1,0:T(8,128)} %get-tuple-element.35.refs_12_), channel_id=1, source_target_pairs={{0,16},{8,72},{16,32},{24,88},{32,48},{40,104},{48,0},{56,120},{64... | collective-permute-start | bytes 1572872 | tf_op jit(solution)/shard_map/ppermute | solution.py:405
  21.6 72.0 %copy-start.10 = (s32[3200]{0:T(1024)}, s32[3200]{0:T(1024)S(1)}, u32[]{:S(2)}) copy-start(s32[3200]{0:T(1024)S(1)} %collective-permute-done.1.refs_2_) | copy-start | bytes 38404
  21.6 17.5 %collective-permute-start.14 = (s32[1024,128]{1,0:T(8,128)}, s32[1024,128]{1,0:T(8,128)S(1)}, u32[]{:S(2)}, u32[]{:S(2)}) collective-permute-start(s32[1024,128]{1,0:T(8,128)} %get-tuple-element.35.refs_12_), channel_id=1, source_target_pairs={{0,32},{8,136},{16,48},{24,152},{32,0},{40,168},{48,16},{56,184},{... | collective-permute-start | bytes 1572872 | tf_op jit(solution)/shard_map/ppermute | solution.py:405
  25.8 67.8 %copy-start.11 = (s32[3200]{0:T(1024)}, s32[3200]{0:T(1024)S(1)}, u32[]{:S(2)}) copy-start(s32[3200]{0:T(1024)S(1)} %collective-permute-done.2.refs_3_) | copy-start | bytes 38404
  25.8 13.3 %collective-permute-start.15 = (s32[1024,128]{1,0:T(8,128)}, s32[1024,128]{1,0:T(8,128)S(1)}, u32[]{:S(2)}, u32[]{:S(2)}) collective-permute-start(s32[1024,128]{1,0:T(8,128)} %get-tuple-element.35.refs_12_), channel_id=1, source_target_pairs={{0,48},{8,200},{16,0},{24,216},{32,16},{40,232},{48,32},{56,248},{... | collective-permute-start | bytes 1572872 | tf_op jit(solution)/shard_map/ppermute | solution.py:405
  31.9 40.5 %collective-permute-start.5 = (bf16[32,128,128]{2,1,0:T(8,128)(2,1)}, bf16[32,128,128]{2,1,0:T(8,128)(2,1)S(1)}, u32[]{:S(2)}, u32[]{:S(2)}) collective-permute-start(bf16[32,128,128]{2,1,0:T(8,128)(2,1)} %get-tuple-element.26), channel_id=1, source_target_pairs={{0,24},{8,64},{16,40},{24,80},{32,56},{40,96},{48,8},{56,112},{64,... | collective-permute-start | bytes 3145736 | tf_op jit(solution)/shard_map/ppermute | solution.py:398
  39.1 35.2 %collective-permute-start.6 = (bf16[32,128,128]{2,1,0:T(8,128)(2,1)}, bf16[32,128,128]{2,1,0:T(8,128)(2,1)}, u32[]{:S(2)}, u32[]{:S(2)}) collective-permute-start(bf16[32,128,128]{2,1,0:T(8,128)(2,1)} %get-tuple-element.27), channel_id=1, source_target_pairs={{0,128},{8,40},{16,144},{24,56},{32,160},{40,8},{48,176},{56,24},{... | collective-permute-start | bytes 3145736 | tf_op jit(solution)/shard_map/ppermute | solution.py:398
  39.2 38.4 %collective-permute-start.7 = (bf16[32,128,128]{2,1,0:T(8,128)(2,1)}, bf16[32,128,128]{2,1,0:T(8,128)(2,1)}, u32[]{:S(2)}, u32[]{:S(2)}) collective-permute-start(bf16[32,128,128]{2,1,0:T(8,128)(2,1)} %get-tuple-element.28), channel_id=1, source_target_pairs={{0,40},{8,128},{16,56},{24,144},{32,8},{40,160},{48,24},{56,176},{... | collective-permute-start | bytes 3145736 | tf_op jit(solution)/shard_map/ppermute | solution.py:398
  41.0 44.6 %collective-permute-start.8 = (bf16[32,128,128]{2,1,0:T(8,128)(2,1)}, bf16[32,128,128]{2,1,0:T(8,128)(2,1)}, u32[]{:S(2)}, u32[]{:S(2)}) collective-permute-start(bf16[32,128,128]{2,1,0:T(8,128)(2,1)} %get-tuple-element.29), channel_id=1, source_target_pairs={{0,192},{8,56},{16,208},{24,8},{32,224},{40,24},{48,240},{56,40},{... | collective-permute-start | bytes 3145736 | tf_op jit(solution)/shard_map/ppermute | solution.py:398
  42.3 50.5 %collective-permute-start.9 = (bf16[32,128,128]{2,1,0:T(8,128)(2,1)}, bf16[32,128,128]{2,1,0:T(8,128)(2,1)}, u32[]{:S(2)}, u32[]{:S(2)}) collective-permute-start(bf16[32,128,128]{2,1,0:T(8,128)(2,1)} %get-tuple-element.30), channel_id=1, source_target_pairs={{0,56},{8,192},{16,8},{24,208},{32,24},{40,224},{48,40},{56,240},{... | collective-permute-start | bytes 3145736 | tf_op jit(solution)/shard_map/ppermute | solution.py:398
  72.4 36.2 %collective-permute-start.19 = (bf16[1024,128]{1,0:T(8,128)(2,1)}, bf16[1024,128]{1,0:T(8,128)(2,1)}, u32[]{:S(2)}, u32[]{:S(2)}) collective-permute-start(bf16[1024,128]{1,0:T(8,128)(2,1)} %get-tuple-element.40.refs_0_), channel_id=1, source_target_pairs={{0,1},{1,2},{2,3},{3,4},{4,5},{5,6},{6,7},{7,0},{8,9},{9,10},{10,1... | collective-permute-start | bytes 786440 | tf_op jit(solution)/shard_map/ppermute | solution.py:408
  74.3 39.2 %collective-permute-start.20 = (bf16[1024,128]{1,0:T(8,128)(2,1)}, bf16[1024,128]{1,0:T(8,128)(2,1)}, u32[]{:S(2)}, u32[]{:S(2)}) collective-permute-start(bf16[1024,128]{1,0:T(8,128)(2,1)} %get-tuple-element.40.refs_0_), channel_id=1, source_target_pairs={{0,2},{1,3},{2,4},{3,5},{4,6},{5,7},{6,0},{7,1},{8,10},{9,11},{10,... | collective-permute-start | bytes 786440 | tf_op jit(solution)/shard_map/ppermute | solution.py:408
  77.6 38.4 %collective-permute-start.21 = (bf16[1024,128]{1,0:T(8,128)(2,1)}, bf16[1024,128]{1,0:T(8,128)(2,1)}, u32[]{:S(2)}, u32[]{:S(2)}) collective-permute-start(bf16[1024,128]{1,0:T(8,128)(2,1)} %get-tuple-element.40.refs_0_), channel_id=1, source_target_pairs={{0,3},{1,4},{2,5},{3,6},{4,7},{5,0},{6,1},{7,2},{8,11},{9,12},{10,... | collective-permute-start | bytes 786440 | tf_op jit(solution)/shard_map/ppermute | solution.py:408
  85.7 30.4 %collective-permute-start.22 = (bf16[1024,128]{1,0:T(8,128)(2,1)}, bf16[1024,128]{1,0:T(8,128)(2,1)}, u32[]{:S(2)}, u32[]{:S(2)}) collective-permute-start(bf16[1024,128]{1,0:T(8,128)(2,1)} %get-tuple-element.40.refs_0_), channel_id=1, source_target_pairs={{0,4},{1,5},{2,6},{3,7},{4,0},{5,1},{6,2},{7,3},{8,12},{9,13},{10,... | collective-permute-start | bytes 786440 | tf_op jit(solution)/shard_map/ppermute | solution.py:408
  92.8 30.4 %collective-permute-start.23 = (bf16[1024,128]{1,0:T(8,128)(2,1)}, bf16[1024,128]{1,0:T(8,128)(2,1)}, u32[]{:S(2)}, u32[]{:S(2)}) collective-permute-start(bf16[1024,128]{1,0:T(8,128)(2,1)} %get-tuple-element.40.refs_0_), channel_id=1, source_target_pairs={{0,5},{1,6},{2,7},{3,0},{4,1},{5,2},{6,3},{7,4},{8,13},{9,14},{10,... | collective-permute-start | bytes 786440 | tf_op jit(solution)/shard_map/ppermute | solution.py:408
  108.6 35.5 %collective-permute-start.16 = (bf16[16,128,128]{2,1,0:T(8,128)(2,1)}, bf16[16,128,128]{2,1,0:T(8,128)(2,1)S(1)}, u32[]{:S(2)}, u32[]{:S(2)}) collective-permute-start(bf16[16,128,128]{2,1,0:T(8,128)(2,1)} %get-tuple-element.37), channel_id=1, source_target_pairs={{0,48},{8,200},{16,0},{24,216},{32,16},{40,232},{48,32},{56,248},{... | collective-permute-start | bytes 1572872 | tf_op jit(solution)/shard_map/ppermute | solution.py:419
  113.5 30.6 %collective-permute-start.17 = (bf16[16,128,128]{2,1,0:T(8,128)(2,1)}, bf16[16,128,128]{2,1,0:T(8,128)(2,1)S(1)}, u32[]{:S(2)}, u32[]{:S(2)}) collective-permute-start(bf16[16,128,128]{2,1,0:T(8,128)(2,1)} %get-tuple-element.38), channel_id=1, source_target_pairs={{0,32},{8,136},{16,48},{24,152},{32,0},{40,168},{48,16},{56,184},{... | collective-permute-start | bytes 1572872 | tf_op jit(solution)/shard_map/ppermute | solution.py:419
  116.0 28.1 %collective-permute-start.18 = (bf16[16,128,128]{2,1,0:T(8,128)(2,1)}, bf16[16,128,128]{2,1,0:T(8,128)(2,1)}, u32[]{:S(2)}, u32[]{:S(2)}) collective-permute-start(bf16[16,128,128]{2,1,0:T(8,128)(2,1)} %get-tuple-element.39), channel_id=1, source_target_pairs={{0,16},{8,72},{16,32},{24,88},{32,48},{40,104},{48,0},{56,120},{64... | collective-permute-start | bytes 1572872 | tf_op jit(solution)/shard_map/ppermute | solution.py:419
  116.0 18.3 %collective-permute-start.24 = (bf16[1024,128]{1,0:T(8,128)(2,1)S(1)}, bf16[1024,128]{1,0:T(8,128)(2,1)S(1)}, u32[]{:S(2)}, u32[]{:S(2)}) collective-permute-start(bf16[1024,128]{1,0:T(8,128)(2,1)S(1)} %copy-done.6), channel_id=1, source_target_pairs={{0,6},{1,7},{2,0},{3,1},{4,2},{5,3},{6,4},{7,5},{8,14},{9,15},{10,... | collective-permute-start | bytes 786440 | tf_op jit(solution)/shard_map/ppermute | solution.py:408
  123.2 16.8 %collective-permute-start.25 = (bf16[1024,128]{1,0:T(8,128)(2,1)S(1)}, bf16[1024,128]{1,0:T(8,128)(2,1)S(1)}, u32[]{:S(2)}, u32[]{:S(2)}) collective-permute-start(bf16[1024,128]{1,0:T(8,128)(2,1)S(1)} %copy-done.6), channel_id=1, source_target_pairs={{0,7},{1,0},{2,1},{3,2},{4,3},{5,4},{6,5},{7,6},{8,15},{9,8},{10,9... | collective-permute-start | bytes 786440 | tf_op jit(solution)/shard_map/ppermute | solution.py:408
  143.7 40.3 %collective-permute-start.26 = (bf16[8,1024,128]{2,1,0:T(8,128)(2,1)}, bf16[8,1024,128]{2,1,0:T(8,128)(2,1)S(1)}, u32[]{:S(2)}, u32[]{:S(2)}) collective-permute-start(bf16[8,1024,128]{2,1,0:T(8,128)(2,1)} %gather_weights.1.w_mine), channel_id=1, source_target_pairs={{0,8},{8,0},{16,24},{24,16},{32,40},{40,32},{48,56},{56,48},{64,72... | collective-permute-start | bytes 6291464 | tf_op jit(solution)/shard_map/ppermute | solution.py:410
  147.7 29.1 %all-to-all-start.1 = ((bf16[8,2,128,128]{3,2,1,0:T(8,128)(2,1)}), bf16[8,2,128,128]{3,2,1,0:T(8,128)(2,1)S(1)}, u32[]{:S(2)}, u32[]{:S(2)}) async-start(bf16[8,2,128,128]{3,2,1,0:T(8,128)(2,1)} %bitcast.8), calls=%async_computation.1 | async-start | bytes 1048576 | tf_op jit(solution)/shard_map/all_to_all | solution.py:422
  156.9 9.5 %collective-permute-start.10 = (bf16[16,128,128]{2,1,0:T(8,128)(2,1)}, bf16[16,128,128]{2,1,0:T(8,128)(2,1)S(1)}, u32[]{:S(2)}, u32[]{:S(2)}) collective-permute-start(bf16[16,128,128]{2,1,0:T(8,128)(2,1)} %get-tuple-element.32), channel_id=1, source_target_pairs={{0,48},{8,200},{16,0},{24,216},{32,16},{40,232},{48,32},{56,248},{... | collective-permute-start | bytes 1572872 | tf_op jit(solution)/shard_map/ppermute | solution.py:415
  158.9 13.9 %collective-permute-start.11 = (bf16[16,128,128]{2,1,0:T(8,128)(2,1)}, bf16[16,128,128]{2,1,0:T(8,128)(2,1)}, u32[]{:S(2)}, u32[]{:S(2)}) collective-permute-start(bf16[16,128,128]{2,1,0:T(8,128)(2,1)} %get-tuple-element.33), channel_id=1, source_target_pairs={{0,32},{8,136},{16,48},{24,152},{32,0},{40,168},{48,16},{56,184},{... | collective-permute-start | bytes 1572872 | tf_op jit(solution)/shard_map/ppermute | solution.py:415
  159.7 14.5 %collective-permute-start.12 = (bf16[16,128,128]{2,1,0:T(8,128)(2,1)}, bf16[16,128,128]{2,1,0:T(8,128)(2,1)}, u32[]{:S(2)}, u32[]{:S(2)}) collective-permute-start(bf16[16,128,128]{2,1,0:T(8,128)(2,1)} %get-tuple-element.34), channel_id=1, source_target_pairs={{0,16},{8,72},{16,32},{24,88},{32,48},{40,104},{48,0},{56,120},{64... | collective-permute-start | bytes 1572872 | tf_op jit(solution)/shard_map/ppermute | solution.py:415
  176.8 24.6 %all-to-all-start = ((bf16[8,2,128,128]{3,2,1,0:T(8,128)(2,1)}), bf16[8,2,128,128]{3,2,1,0:T(8,128)(2,1)S(1)}, u32[]{:S(2)}, u32[]{:S(2)}) async-start(bf16[8,2,128,128]{3,2,1,0:T(8,128)(2,1)} %bitcast.9), calls=%async_computation | async-start | bytes 1048576 | tf_op jit(solution)/shard_map/all_to_all | solution.py:422
  (15 other events, 315.8 us)
where the time goes:
time: 232 us; the launch traced here: 230 us
  waiting for transfers between devices  81.2 us (35%)
  starting transfers between devices  73.2 us (32%)
  Pallas kernels  48.7 us (21%)
  blocking collectives  21.3 us (9%)
  local copies, waits for them, and re-layouts  5.48 us (2%)
    ppermute x7, waiting for transfers between devices, body(): sources.append(lax.ppermute(packed[q], 'dom', meet_pairs(q // 2, q % 2)))  31.3 us
    ppermute x7, starting transfers between devices, body(): lax.ppermute(w_t, 'col', [(i, (i + k) % n_col) for i in range(n_col)])  25.9 us
    all_to_all x1, blocking collectives, body(): return lax.all_to_all(y, 'col', 0, 0, tiled=True).reshape(-1, ROWS)  21.3 us
    all_to_all x2, waiting for transfers between devices, to_rows(): lax.all_to_all(x.reshape(n_col, DST // n_col, ROWS, ROWS), 'col', 0, 0, t...  17.4 us
    ppermute x7, waiting for transfers between devices, body(): lax.ppermute(w_t, 'col', [(i, (i + k) % n_col) for i in range(n_col)])  15.2 us
    pallas_call x1, Pallas kernels, aggregate(): pl.pallas_call(agg_kernel, out_shape=[jax.ShapeDtypeStruct((DST, ROWS, RO...  14.9 us
    ppermute x7, starting transfers between devices, body(): sources.append(lax.ppermute(packed[q], 'dom', meet_pairs(q // 2, q % 2)))  14.9 us
    ppermute x3, waiting for transfers between devices, body(): own_here.append(lax.ppermute(own_parts[m], 'dom', ring_pairs(RING - m)))  12 us
  transfers between devices with their start and end apart: 29, of which 10 were waited for; matrix products, arithmetic and copies ran while one was open for 0% of the time, Pallas kernels for 16%

commit v1 on v0

--- a/solution.py
+++ b/solution.py
@@ -1,3 +1,5 @@
+import functools
+
 import jax
 import jax.numpy as jnp
 from jax import lax
@@ -18,6 +20,7 @@
 N_ITEMS = DST * TILES
 SECTION = N_ITEMS + ROWS
 UNROLL = 4
+JOIN = 4
 BF = jnp.bfloat16
 F32 = jnp.float32
 I32 = jnp.int32
@@ -75,7 +78,7 @@
             shard1 = dom_of(wrapped(y - m), wrapped(x + d), 1)
             shard = jnp.where(to_one == 1, shard1, shard0)
             for s in range(CAP):
-                stage[q, m * CAP + s] = ft[req[shard, s]]
+                stage[q, m * CAP + s] = ft[req[s, shard]]
         copy = pltpu.make_async_copy(stage.at[q], outs[q], sem.at[q])
         copy.start()
         copies.append(copy)
@@ -199,11 +202,14 @@
 
         def start(i, _):
             v = lists[m][m * SECTION + N_ITEMS + 1 + i]
-            for q in range(N_SRC):
-
-                @pl.when(v >> 5 == q)
-                def _():
-                    copy_of(q, m * DST + i, v).start()
+
+            @pl.when(v >= 0)
+            def _():
+                for q in range(N_SRC):
+
+                    @pl.when(v >> 5 == q)
+                    def _():
+                        copy_of(q, m * DST + i, v).start()
 
             @pl.when(v < 0)
             def _():
@@ -247,10 +253,12 @@
     )(*lists, *sources)
 
 
-def agg_kernel(*refs):
-    lists, src, nbr = refs[:RING], refs[RING : RING + N_SRC], refs[RING + N_SRC : 2 * RING + N_SRC]
-    outs, (blocks, acc, sem) = refs[2 * RING + N_SRC : 3 * RING + N_SRC], refs[3 * RING + N_SRC :]
-    fetch = [pltpu.make_async_copy(src[q], blocks.at[pl.ds(q * 32, 32)], sem.at[q]) for q in range(N_SRC)]
+def agg_kernel(m, todo, *refs):
+    src, nbr, out, (blocks, acc, sem) = refs[:N_SRC], refs[N_SRC], refs[N_SRC + 1], refs[N_SRC + 2 :]
+    fetch = [
+        pltpu.make_async_copy(src[q].at[pl.ds(m * CAP, CAP)], blocks.at[pl.ds(q * CAP, CAP)], sem.at[q])
+        for q in range(N_SRC)
+    ]
     for copy in fetch:
         copy.start()
 
@@ -258,81 +266,78 @@
         acc[n] = jnp.zeros((ROWS, ROWS), F32)
         return 0
 
-    lax.fori_loop(0, RING * DST + 1, clear, 0, unroll=5)
+    lax.fori_loop(0, DST + 1, clear, 0)
     iota = lax.broadcasted_iota(I32, (ROWS, ROWS), 0).astype(F32).astype(BF)
     one, zero = jnp.ones((), BF), jnp.zeros((), BF)
+    n_item = todo[m * SECTION + N_ITEMS]
     for copy in fetch:
         copy.wait()
 
-    for m in (1, 2, 3, 0):
-        todo = lists[m]
-        n_item = todo[m * SECTION + N_ITEMS]
-
-        def some(h, _):
-            parts = []
-            for u in range(UNROLL):
-                n = h * UNROLL + u
-                item = jnp.where(n < n_item, todo[m * SECTION + n], 0)
-                blk = item & 255
-                i = (item >> 8) & 15
-                t = item >> 12
-                dst = jnp.where(n < n_item, m * DST + i, RING * DST)
-                row0 = i * (ROWS // 2) + (t & 15) * FAN_T
-                shift = (t >> 4) * 16
-                total = None
-                for f in range(FAN_T):
-                    row = (nbr[m][pl.ds(row0 + f, 1), :] >> shift) & 65535
-                    hit = jnp.where(iota == row.astype(F32).astype(BF), one, zero)
-                    total = hit if total is None else total + hit
-                parts.append((dst, jnp.dot(blocks[blk], total, preferred_element_type=F32)))
-            for dst, part in parts:
-                acc[dst] += part
-            return 0
-
-        lax.fori_loop(0, (n_item + UNROLL - 1) // UNROLL, some, 0)
-    for m in range(RING):
-
-        def leave(n, _):
-            outs[m][n] = acc[m * DST + n].astype(BF)
-            return 0
-
-        lax.fori_loop(0, DST, leave, 0, unroll=4)
-
-
-def aggregate(lists, sources, nbrs):
-    return pl.pallas_call(
-        agg_kernel,
-        out_shape=[jax.ShapeDtypeStruct((DST, ROWS, ROWS), BF)] * RING,
-        in_specs=[SMEM] * RING + [ANY] * N_SRC + [VMEM] * RING,
-        out_specs=[VMEM] * RING,
+    def some(h, _):
+        parts = []
+        for u in range(UNROLL):
+            n = h * UNROLL + u
+            item = jnp.where(n < n_item, todo[m * SECTION + n], 0)
+            blk = ((item >> 5) & 7) * CAP + (item & 7)
+            i = (item >> 8) & 15
+            t = item >> 12
+            row0 = i * (ROWS // 2) + (t & 15) * FAN_T
+            shift = (t >> 4) * 16
+            total = None
+            for f in range(FAN_T):
+                row = (nbr[pl.ds(row0 + f, 1), :] >> shift) & 65535
+                hit = jnp.where(iota == row.astype(F32).astype(BF), one, zero)
+                total = hit if total is None else total + hit
+            dst = jnp.where(n < n_item, i, DST)
+            parts.append((dst, jnp.dot(blocks[blk], total, preferred_element_type=F32)))
+        for dst, part in parts:
+            acc[dst] += part
+        return 0
+
+    lax.fori_loop(0, (n_item + UNROLL - 1) // UNROLL, some, 0)
+
+    def leave(n, _):
+        out[n] = acc[n].astype(BF)
+        return 0
+
+    lax.fori_loop(0, DST, leave, 0, unroll=4)
+
+
+def aggregate(m, todo, sources, nbr_t):
+    return pl.pallas_call(
+        functools.partial(agg_kernel, m),
+        out_shape=jax.ShapeDtypeStruct((DST, ROWS, ROWS), BF),
+        in_specs=[SMEM] + [ANY] * N_SRC + [VMEM],
+        out_specs=VMEM,
         scratch_shapes=[
-            pltpu.VMEM((N_SRC * 32, ROWS, ROWS), BF),
-            pltpu.VMEM((RING * DST + 1, ROWS, ROWS), F32),
+            pltpu.VMEM((N_SRC * CAP, ROWS, ROWS), BF),
+            pltpu.VMEM((DST + 1, ROWS, ROWS), F32),
             pltpu.SemaphoreType.DMA((N_SRC,)),
         ],
-        cost_estimate=pl.CostEstimate(flops=10**10, bytes_accessed=2 * 10**7, transcendentals=0),
-        name="agg",
-    )(*lists, *sources, *nbrs)
+        cost_estimate=pl.CostEstimate(flops=4 * 10**9, bytes_accessed=5 * 10**6, transcendentals=0),
+    )(todo, *sources, nbr_t)
 
 
 def join_own_kernel(a, b, c, d, out):
-    for n in range(DST):
+    total = a[...].astype(F32) + b[...].astype(F32) + c[...].astype(F32) + d[...].astype(F32)
+    out[...] = total.astype(BF)
+
+
+def join_agg_kernel(tile_count, a, b, c, d, out):
+    step = pl.program_id(0)
+    for n in range(JOIN):
         total = a[n].astype(F32) + b[n].astype(F32) + c[n].astype(F32) + d[n].astype(F32)
-        out[n] = total.astype(BF)
-
-
-def join_agg_kernel(tile_count, a, b, c, d, out):
-    for n in range(DST):
-        total = a[n].astype(F32) + b[n].astype(F32) + c[n].astype(F32) + d[n].astype(F32)
-        out[n] = (total / (tile_count[n] * FAN_T).astype(F32)).astype(BF)
+        out[n] = (total / (tile_count[step * JOIN + n] * FAN_T).astype(F32)).astype(BF)
 
 
 def join(kernel, scalars, parts):
+    some = pl.BlockSpec((JOIN, ROWS, ROWS), lambda g: (g, 0, 0))
     return pl.pallas_call(
         kernel,
+        grid=(DST // JOIN,),
         out_shape=jax.ShapeDtypeStruct((DST, ROWS, ROWS), BF),
-        in_specs=[SMEM] * len(scalars) + [VMEM] * RING,
-        out_specs=VMEM,
+        in_specs=[SMEM] * len(scalars) + [some] * RING,
+        out_specs=some,
         cost_estimate=pl.CostEstimate(flops=10**9, bytes_accessed=5 * 10**6, transcendentals=0),
     )(*scalars, *parts)
 
@@ -392,7 +397,7 @@
     n_col = lax.axis_size("col")
     me = lax.axis_index("dom").reshape(1).astype(I32)
     column = lax.axis_index("col").reshape(1).astype(I32)
-    packed = pack(me, requests[0], features)
+    packed = pack(me, requests[0].T, features)
     sources = [packed[0]]
     for q in range(1, N_SRC):
         sources.append(lax.ppermute(packed[q], "dom", meet_pairs(q // 2, q % 2)))
@@ -413,10 +418,10 @@
     own_here = [own_parts[0]]
     for m in range(1, RING):
         own_here.append(lax.ppermute(own_parts[m], "dom", ring_pairs(RING - m)))
-    agg_parts = aggregate(lists, sources, nbrs)
-    agg_here = [agg_parts[0]]
+    agg_here = [aggregate(0, lists[0], sources, nbrs[0])]
     for m in range(1, RING):
-        agg_here.append(lax.ppermute(agg_parts[m], "dom", ring_pairs(RING - m)))
+        part = aggregate(m, lists[m], sources, nbrs[m])
+        agg_here.append(lax.ppermute(part, "dom", ring_pairs(RING - m)))
 
     def to_rows(x):
         return lax.all_to_all(x.reshape(n_col, DST // n_col, ROWS, ROWS), "col", 0, 0, tiled=True)

time: 232 us -> 245 us (1.056)
  the two profiles are of different devices: /device:TPU:2 before, /device:TPU:1 now
where the time goes in v1:
time: 245 us; the launch traced here: 244 us
  waiting for transfers between devices  95.4 us (39%)
  starting transfers between devices  63.8 us (26%)
  Pallas kernels  60.8 us (25%)
  blocking collectives  21.3 us (9%)
    ppermute x7, waiting for transfers between devices, body(): sources.append(lax.ppermute(packed[q], 'dom', meet_pairs(q // 2, q % 2)))  38.2 us
    pallas_call x4, Pallas kernels, aggregate(): pl.pallas_call(functools.partial(agg_kernel, m), out_shape=jax.ShapeDtype...  25.1 us
    ppermute x7, waiting for transfers between devices, body(): lax.ppermute(w_t, 'col', [(i, (i + k) % n_col) for i in range(n_col)])  22.7 us
    all_to_all x1, blocking collectives, body(): return lax.all_to_all(y, 'col', 0, 0, tiled=True).reshape(-1, ROWS)  21.3 us
    all_to_all x2, waiting for transfers between devices, to_rows(): lax.all_to_all(x.reshape(n_col, DST // n_col, ROWS, ROWS), 'col', 0, 0, t...  18 us
    ppermute x7, starting transfers between devices, body(): lax.ppermute(w_t, 'col', [(i, (i + k) % n_col) for i in range(n_col)])  16.6 us
    ppermute x3, waiting for transfers between devices, body(): own_here.append(lax.ppermute(own_parts[m], 'dom', ring_pairs(RING - m)))  14.5 us
    all_to_all x2, starting transfers between devices, to_rows(): lax.all_to_all(x.reshape(n_col, DST // n_col, ROWS, ROWS), 'col', 0, 0, t...  12.1 us
  transfers between devices with their start and end apart: 29, of which 12 were waited for; matrix products, arithmetic and copies ran while one was open for 0% of the time, Pallas kernels for 20%

profile of v1, /device:TPU:1, one launch (start us, length us, event | category | flops | bytes accessed | tf_op | source)
XLA Modules:
  0.0 243.9 jit_solution(16162928615681980793)
XLA Ops:
  0.0 6.1 %pack.1 = (bf16[32,128,128]{2,1,0:T(8,128)(2,1)}, bf16[32,128,128]{2,1,0:T(8,128)(2,1)}, bf16[32,128,128]{2,1,0:T(8,128)(2,1)}, bf16[32,128,128]{2,1,0:T(8,128)(...) custom-call(s32[1]{0:T(128)} %bitcast.me, ...), custom_call_target="tpu_custom_call" | custom-call | flops 1000000000 | bytes 10000000 | tf_op jit(solution)/shard_map/pack/pallas_call | solution.py:91
  6.1 3.3 %collective-permute-start.3 = (bf16[32,128,128]{2,1,0:T(8,128)(2,1)}, bf16[32,128,128]{2,1,0:T(8,128)(2,1)S(1)}, u32[]{:S(2)}, u32[]{:S(2)}) collective-permute-start(bf16[32,128,128]{2,1,0:T(8,128)(2,1)} %get-tuple-element.20), channel_id=1, source_target_pairs={{0,8},{8,0},{16,24},{24,16},{32,40},{40,32},{48,56},{56,48},{64,72... | collective-permute-start | bytes 3145736 | tf_op jit(solution)/shard_map/ppermute | solution.py:403
  9.4 3.2 %tables.1 = (s32[1024,128]{1,0:T(8,128)}, bf16[1024,128]{1,0:T(8,128)(2,1)}) custom-call(s32[1]{0:T(128)} %bitcast.me, s32[2048,128]{1,0:T(8,128)} %nbr.1, bf16[128,1024]{1,0:T(8,128)(2,1)} %ws.1, bf16[128,1024]{1,0:T(8,128)(2,1)} %wn.1), custom_call_target="tpu_custom_call" | custom-call | flops 1000000000 | bytes 10000000 | tf_op jit(solution)/shard_map/tables/pallas_call | solution.py:124
  16.5 5.1 %plan.1.refs_0_.todo = s32[3200]{0:T(1024)} custom-call(s32[1]{0:T(128)} %bitcast.me, s32[32]{0:T(128)} %bitcast.13, s32[16,32]{1,0:T(8,128)} %tile_block.1, s32[16]{0:T(128)} %tile_count.3), custom_call_target="tpu_custom_call" | custom-call | flops 2000000000 | bytes 1000000 | tf_op jit(solution)/shard_map/plan/pallas_call | solution.py:183
  25.3 3.0 %collective-permute-start.7 = (bf16[32,128,128]{2,1,0:T(8,128)(2,1)}, bf16[32,128,128]{2,1,0:T(8,128)(2,1)}, u32[]{:S(2)}, u32[]{:S(2)}) collective-permute-start(bf16[32,128,128]{2,1,0:T(8,128)(2,1)} %get-tuple-element.24), channel_id=1, source_target_pairs={{0,40},{8,128},{16,56},{24,144},{32,8},{40,160},{48,24},{56,176},{... | collective-permute-start | bytes 3145736 | tf_op jit(solution)/shard_map/ppermute | solution.py:403
  31.3 27.3 %collective-permute-done.5.refs_7_.refs_3_ = bf16[32,128,128]{2,1,0:T(8,128)(2,1)S(1)} collective-permute-done((bf16[32,128,128]{2,1,0:T(8,128)(2,1)}, bf16[32,128,128]{2,1,0:T(8,128)(2,1)S(1)}, u32[]{:S(2)}, u32[]{:S(2)}) %collective-permute-start.5) | collective-permute-done | bytes 1048608 | tf_op jit(solution)/shard_map/ppermute | solution.py:403
  61.6 10.4 %collective-permute-done.8.refs_10_.refs_6_ = bf16[32,128,128]{2,1,0:T(8,128)(2,1)} collective-permute-done((bf16[32,128,128]{2,1,0:T(8,128)(2,1)}, bf16[32,128,128]{2,1,0:T(8,128)(2,1)}, u32[]{:S(2)}, u32[]{:S(2)}) %collective-permute-start.8) | collective-permute-done | bytes 1048608 | tf_op jit(solution)/shard_map/ppermute | solution.py:403
  74.6 7.0 %shard_map.86 = bf16[16,128,128]{2,1,0:T(8,128)(2,1)} custom-call(s32[3200]{0:T(1024)} %copy-done.13, bf16[32,128,128]{2,1,0:T(8,128)(2,1)} %get-tuple-element.19.refs_4_.refs_0_, bf16[32,128,128]{2,1,0:T(8,128)(2,1)} %copy-done.3, bf16[32,128,128]{2,1,0:T(8,128)(2,1)} %copy-done.4, bf16[32,128,128]{2,1,0:T(8,128)(2,1)} %copy-done.5, ...), custom_call_target="tpu_custom_call" | custom-call | flops 4000000000 | bytes 5000000 | tf_op jit(solution)/shard_map/pallas_call | solution.py:307
  81.6 3.1 %collective-permute-start.20 = (bf16[1024,128]{1,0:T(8,128)(2,1)S(1)}, bf16[1024,128]{1,0:T(8,128)(2,1)S(1)}, u32[]{:S(2)}, u32[]{:S(2)}) collective-permute-start(bf16[1024,128]{1,0:T(8,128)(2,1)S(1)} %copy-done.6), channel_id=1, source_target_pairs={{0,2},{1,3},{2,4},{3,5},{4,6},{5,7},{6,0},{7,1},{8,10},{9,11},{10,... | collective-permute-start | bytes 786440 | tf_op jit(solution)/shard_map/ppermute | solution.py:413
  84.7 3.8 %collective-permute-start.21 = (bf16[1024,128]{1,0:T(8,128)(2,1)S(1)}, bf16[1024,128]{1,0:T(8,128)(2,1)S(1)}, u32[]{:S(2)}, u32[]{:S(2)}) collective-permute-start(bf16[1024,128]{1,0:T(8,128)(2,1)S(1)} %copy-done.6), channel_id=1, source_target_pairs={{0,3},{1,4},{2,5},{3,6},{4,7},{5,0},{6,1},{7,2},{8,11},{9,12},{10,... | collective-permute-start | bytes 786440 | tf_op jit(solution)/shard_map/ppermute | solution.py:413
  88.5 6.8 %shard_map.85 = bf16[16,128,128]{2,1,0:T(8,128)(2,1)} custom-call(s32[3200]{0:T(1024)} %copy-done.14, bf16[32,128,128]{2,1,0:T(8,128)(2,1)} %get-tuple-element.19.refs_4_.refs_0_, bf16[32,128,128]{2,1,0:T(8,128)(2,1)} %copy-done.3, bf16[32,128,128]{2,1,0:T(8,128)(2,1)} %copy-done.4, bf16[32,128,128]{2,1,0:T(8,128)(2,1)} %copy-done.5, ...), custom_call_target="tpu_custom_call" | custom-call | flops 4000000000 | bytes 5000000 | tf_op jit(solution)/shard_map/pallas_call | solution.py:307
  95.8 4.5 %collective-permute-start.23 = (bf16[1024,128]{1,0:T(8,128)(2,1)S(1)}, bf16[1024,128]{1,0:T(8,128)(2,1)S(1)}, u32[]{:S(2)}, u32[]{:S(2)}) collective-permute-start(bf16[1024,128]{1,0:T(8,128)(2,1)S(1)} %copy-done.6), channel_id=1, source_target_pairs={{0,5},{1,6},{2,7},{3,0},{4,1},{5,2},{6,3},{7,4},{8,13},{9,14},{10,... | collective-permute-start | bytes 786440 | tf_op jit(solution)/shard_map/ppermute | solution.py:413
  103.4 5.2 %shard_map.84 = bf16[16,128,128]{2,1,0:T(8,128)(2,1)} custom-call(s32[3200]{0:T(1024)} %copy-done.15, bf16[32,128,128]{2,1,0:T(8,128)(2,1)} %get-tuple-element.19.refs_4_.refs_0_, bf16[32,128,128]{2,1,0:T(8,128)(2,1)} %copy-done.3, bf16[32,128,128]{2,1,0:T(8,128)(2,1)} %copy-done.4, bf16[32,128,128]{2,1,0:T(8,128)(2,1)} %copy-done.5, ...), custom_call_target="tpu_custom_call" | custom-call | flops 4000000000 | bytes 5000000 | tf_op jit(solution)/shard_map/pallas_call | solution.py:307
  108.7 4.9 %collective-permute-done.21.refs_3_ = bf16[1024,128]{1,0:T(8,128)(2,1)S(1)} collective-permute-done((bf16[1024,128]{1,0:T(8,128)(2,1)S(1)}, bf16[1024,128]{1,0:T(8,128)(2,1)S(1)}, u32[]{:S(2)}, u32[]{:S(2)}) %collective-permute-start.21) | collective-permute-done | bytes 262176 | tf_op jit(solution)/shard_map/ppermute | solution.py:413
  113.5 3.5 %collective-permute-start.18 = (bf16[16,128,128]{2,1,0:T(8,128)(2,1)S(1)}, bf16[16,128,128]{2,1,0:T(8,128)(2,1)}, u32[]{:S(2)}, u32[]{:S(2)}) collective-permute-start(bf16[16,128,128]{2,1,0:T(8,128)(2,1)S(1)} %copy-done.16), channel_id=1, source_target_pairs={{0,16},{8,72},{16,32},{24,88},{32,48},{40,104},{48,0},{56,120},{64... | collective-permute-start | bytes 1572872 | tf_op jit(solution)/shard_map/ppermute | solution.py:424
  117.1 6.5 %collective-permute-done.22.refs_4_ = bf16[1024,128]{1,0:T(8,128)(2,1)S(1)} collective-permute-done((bf16[1024,128]{1,0:T(8,128)(2,1)S(1)}, bf16[1024,128]{1,0:T(8,128)(2,1)S(1)}, u32[]{:S(2)}, u32[]{:S(2)}) %collective-permute-start.22) | collective-permute-done | bytes 262176 | tf_op jit(solution)/shard_map/ppermute | solution.py:413
  123.6 4.1 %collective-permute-done.23.refs_5_ = bf16[1024,128]{1,0:T(8,128)(2,1)S(1)} collective-permute-done((bf16[1024,128]{1,0:T(8,128)(2,1)S(1)}, bf16[1024,128]{1,0:T(8,128)(2,1)S(1)}, u32[]{:S(2)}, u32[]{:S(2)}) %collective-permute-start.23) | collective-permute-done | bytes 262176 | tf_op jit(solution)/shard_map/ppermute | solution.py:413
  127.7 7.4 %collective-permute-start.14 = (bf16[16,128,128]{2,1,0:T(8,128)(2,1)}, bf16[16,128,128]{2,1,0:T(8,128)(2,1)}, u32[]{:S(2)}, u32[]{:S(2)}) collective-permute-start(bf16[16,128,128]{2,1,0:T(8,128)(2,1)} %shard_map.84), channel_id=1, source_target_pairs={{0,48},{8,200},{16,0},{24,216},{32,16},{40,232},{48,32},{56,248},{... | collective-permute-start | bytes 1572872 | tf_op jit(solution)/shard_map/ppermute | solution.py:424
  135.1 4.8 %collective-permute-done.24.refs_6_ = bf16[1024,128]{1,0:T(8,128)(2,1)S(1)} collective-permute-done((bf16[1024,128]{1,0:T(8,128)(2,1)S(1)}, bf16[1024,128]{1,0:T(8,128)(2,1)S(1)}, u32[]{:S(2)}, u32[]{:S(2)}) %collective-permute-start.24) | collective-permute-done | bytes 262176 | tf_op jit(solution)/shard_map/ppermute | solution.py:413
  143.1 3.0 %gather_weights.1.w_mine = bf16[8,1024,128]{2,1,0:T(8,128)(2,1)} custom-call(bf16[1024,128]{1,0:T(8,128)(2,1)} %get-tuple-element.32.refs_0_, bf16[1024,128]{1,0:T(8,128)(2,1)} %collective-permute-done.19.refs_1_, bf16[1024,128]{1,0:T(8,128)(2,1)} %copy-done.7, bf16[1024,128]{1,0:T(8,128)(2,1)} %copy-done.8, bf16[1024,128]{1,0:T(8,128)(2,1)} %copy-done.9, ...), custom_call_target="tpu_custom_call" | custom-call | flops 1000000000 | bytes 5000000 | tf_op jit(solution)/shard_map/gather_weights/pallas_call | solution.py:352
  147.6 6.1 %shard_map.83.a = bf16[16,128,128]{2,1,0:T(8,128)(2,1)} custom-call(s32[3200]{0:T(1024)} %plan.1.refs_0_.todo, bf16[32,128,128]{2,1,0:T(8,128)(2,1)} %get-tuple-element.19.refs_4_.refs_0_, bf16[32,128,128]{2,1,0:T(8,128)(2,1)} %copy-done.3, bf16[32,128,128]{2,1,0:T(8,128)(2,1)} %copy-done.4, bf16[32,128,128]{2,1,0:T(8,128)(2,1)} %copy-done.5, ...), custom_call_target="tpu_custom_call" | custom-call | flops 4000000000 | bytes 5000000 | tf_op jit(solution)/shard_map/pallas_call | solution.py:307
  153.8 3.6 %shard_map.87 = bf16[16,128,128]{2,1,0:T(8,128)(2,1)} custom-call(s32[16]{0:T(128)} %tile_count.3, bf16[16,128,128]{2,1,0:T(8,128)(2,1)} %shard_map.83.a, bf16[16,128,128]{2,1,0:T(8,128)(2,1)} %collective-permute-done.14.b, bf16[16,128,128]{2,1,0:T(8,128)(2,1)} %collective-permute-done.16.c, bf16[16,128,128]{2,1,0:T(8,128)(2,1)} %collective-permute-done.18.d), custom_call_target="tpu_custom_call" | custom-call | flops 1000000000 | bytes 5000000 | tf_op jit(solution)/shard_map/pallas_call | solution.py:335
  157.4 5.4 %all-to-all-start.1 = ((bf16[8,2,128,128]{3,2,1,0:T(8,128)(2,1)}), bf16[8,2,128,128]{3,2,1,0:T(8,128)(2,1)S(1)}, u32[]{:S(2)}, u32[]{:S(2)}) async-start(bf16[8,2,128,128]{3,2,1,0:T(8,128)(2,1)} %bitcast.10), calls=%async_computation.1 | async-start | bytes 1048576 | tf_op jit(solution)/shard_map/all_to_all | solution.py:427
  162.9 5.2 %own_rows.1 = (bf16[16,128,128]{2,1,0:T(8,128)(2,1)}, bf16[16,128,128]{2,1,0:T(8,128)(2,1)}, bf16[16,128,128]{2,1,0:T(8,128)(2,1)}, bf16[16,128,128]{2,1,0:T(8,128)(2,1)}) custom-call(s32[3200]{0:T(1024)} %plan.1.refs_0_.todo, s32[3200]{0:T(1024)} %copy-done.15, s32[3200]{0:T(1024)} %copy-done.14, s32[3200]{0:T(1024)} %copy-done.13, ...), custom_call_target="tpu_custom_call" | custom-call | flops 1000000000 | bytes 10000000 | tf_op jit(solution)/shard_map/own_rows/pallas_call | solution.py:241
  168.1 3.6 %collective-permute-start.10 = (bf16[16,128,128]{2,1,0:T(8,128)(2,1)}, bf16[16,128,128]{2,1,0:T(8,128)(2,1)S(1)}, u32[]{:S(2)}, u32[]{:S(2)}) collective-permute-start(bf16[16,128,128]{2,1,0:T(8,128)(2,1)} %get-tuple-element.28), channel_id=1, source_target_pairs={{0,48},{8,200},{16,0},{24,216},{32,16},{40,232},{48,32},{56,248},{... | collective-permute-start | bytes 1572872 | tf_op jit(solution)/shard_map/ppermute | solution.py:420
  172.4 11.4 %collective-permute-done.10.b = bf16[16,128,128]{2,1,0:T(8,128)(2,1)S(1)} collective-permute-done((bf16[16,128,128]{2,1,0:T(8,128)(2,1)}, bf16[16,128,128]{2,1,0:T(8,128)(2,1)S(1)}, u32[]{:S(2)}, u32[]{:S(2)}) %collective-permute-start.10) | collective-permute-done | bytes 524320 | tf_op jit(solution)/shard_map/ppermute | solution.py:420
  183.7 3.1 %collective-permute-done.12.d = bf16[16,128,128]{2,1,0:T(8,128)(2,1)} collective-permute-done((bf16[16,128,128]{2,1,0:T(8,128)(2,1)}, bf16[16,128,128]{2,1,0:T(8,128)(2,1)}, u32[]{:S(2)}, u32[]{:S(2)}) %collective-permute-start.12) | collective-permute-done | bytes 524320 | tf_op jit(solution)/shard_map/ppermute | solution.py:420
  186.9 3.6 %shard_map.82 = bf16[16,128,128]{2,1,0:T(8,128)(2,1)} custom-call(bf16[16,128,128]{2,1,0:T(8,128)(2,1)} %get-tuple-element.27.a, bf16[16,128,128]{2,1,0:T(8,128)(2,1)} %copy-done.18, bf16[16,128,128]{2,1,0:T(8,128)(2,1)} %collective-permute-done.11.c, bf16[16,128,128]{2,1,0:T(8,128)(2,1)} %collective-permute-done.12.d), custom_call_target="tpu_custom_call" | custom-call | flops 1000000000 | bytes 5000000 | tf_op jit(solution)/shard_map/pallas_call | solution.py:335
  190.5 6.7 %all-to-all-start = ((bf16[8,2,128,128]{3,2,1,0:T(8,128)(2,1)}), bf16[8,2,128,128]{3,2,1,0:T(8,128)(2,1)S(1)}, u32[]{:S(2)}, u32[]{:S(2)}) async-start(bf16[8,2,128,128]{3,2,1,0:T(8,128)(2,1)} %bitcast.11), calls=%async_computation | async-start | bytes 1048576 | tf_op jit(solution)/shard_map/all_to_all | solution.py:427
  197.2 18.0 %all-to-all-done.xs = bf16[8,2,128,128]{3,2,1,0:T(8,128)(2,1)S(1)} async-done(((bf16[8,2,128,128]{3,2,1,0:T(8,128)(2,1)}), bf16[8,2,128,128]{3,2,1,0:T(8,128)(2,1)S(1)}, u32[]{:S(2)}, u32[]{:S(2)}) %all-to-all-start) | async-done | bytes 524320 | tf_op jit(solution)/shard_map/all_to_all | solution.py:427
  215.9 5.9 %project.1 = bf16[8,256,128]{2,1,0:T(8,128)(2,1)} custom-call(s32[1]{0:T(128)} %bitcast.me, s32[1]{0:T(128)} %bitcast.1.column, bf16[8,2,128,128]{3,2,1,0:T(8,128)(2,1)} %copy-done.2, bf16[8,2,128,128]{3,2,1,0:T(8,128)(2,1)} %copy-done.1, bf16[8,1024,128]{2,1,0:T(8,128)(2,1)} %gather_weights.1.w_mine, bf16[8,1024,128]{2,1,0:T(8,128)(2,1)} %copy-done), custom_call_target="tpu_custom_call" | custom-call | flops 1000000000 | bytes 5000000 | tf_op jit(solution)/shard_map/project/pallas_call | solution.py:385
  221.8 21.3 %all_to_all.15 = bf16[8,256,128]{2,1,0:T(8,128)(2,1)S(1)} all-to-all(bf16[8,256,128]{2,1,0:T(8,128)(2,1)} %project.1), channel_id=1, replica_groups=mesh['dom'=32,'col'=8] {'col'}, dimensions={0} | all-to-all | bytes 1048576 | tf_op jit(solution)/shard_map/all_to_all | solution.py:432
  (78 shorter events, 27.0 us)
Async XLA Ops:
  6.1 22.2 %collective-permute-start.3 = (bf16[32,128,128]{2,1,0:T(8,128)(2,1)}, bf16[32,128,128]{2,1,0:T(8,128)(2,1)S(1)}, u32[]{:S(2)}, u32[]{:S(2)}) collective-permute-start(bf16[32,128,128]{2,1,0:T(8,128)(2,1)} %get-tuple-element.20), channel_id=1, source_target_pairs={{0,8},{8,0},{16,24},{24,16},{32,40},{40,32},{48,56},{56,48},{64,72... | collective-permute-start | bytes 3145736 | tf_op jit(solution)/shard_map/ppermute | solution.py:403
  9.4 21.5 %collective-permute-start.4 = (bf16[32,128,128]{2,1,0:T(8,128)(2,1)}, bf16[32,128,128]{2,1,0:T(8,128)(2,1)S(1)}, u32[]{:S(2)}, u32[]{:S(2)}) collective-permute-start(bf16[32,128,128]{2,1,0:T(8,128)(2,1)} %get-tuple-element.21), channel_id=1, source_target_pairs={{0,64},{8,24},{16,80},{24,40},{32,96},{40,56},{48,112},{56,8},{64,... | collective-permute-start | bytes 3145736 | tf_op jit(solution)/shard_map/ppermute | solution.py:403
  12.6 12.8 %collective-permute-start.17 = (s32[1024,128]{1,0:T(8,128)}, s32[1024,128]{1,0:T(8,128)}, u32[]{:S(2)}, u32[]{:S(2)}) collective-permute-start(s32[1024,128]{1,0:T(8,128)} %get-tuple-element.31.refs_8_), channel_id=1, source_target_pairs={{0,48},{8,200},{16,0},{24,216},{32,16},{40,232},{48,32},{56,248},{... | collective-permute-start | bytes 1572872 | tf_op jit(solution)/shard_map/ppermute | solution.py:410
  14.8 43.8 %collective-permute-start.5 = (bf16[32,128,128]{2,1,0:T(8,128)(2,1)}, bf16[32,128,128]{2,1,0:T(8,128)(2,1)S(1)}, u32[]{:S(2)}, u32[]{:S(2)}) collective-permute-start(bf16[32,128,128]{2,1,0:T(8,128)(2,1)} %get-tuple-element.22), channel_id=1, source_target_pairs={{0,24},{8,64},{16,40},{24,80},{32,56},{40,96},{48,8},{56,112},{64,... | collective-permute-start | bytes 3145736 | tf_op jit(solution)/shard_map/ppermute | solution.py:403
  16.5 56.5 %copy-start.6 = (bf16[1024,128]{1,0:T(8,128)(2,1)S(1)}, bf16[1024,128]{1,0:T(8,128)(2,1)}, u32[]{:S(2)}) copy-start(bf16[1024,128]{1,0:T(8,128)(2,1)} %get-tuple-element.32.refs_0_) | copy-start | bytes 786436
  21.6 3.2 %collective-permute-start.2 = (s32[3200]{0:T(1024)}, s32[3200]{0:T(1024)S(1)}, u32[]{:S(2)}, u32[]{:S(2)}) collective-permute-start(s32[3200]{0:T(1024)} %plan.1.refs_0_.todo), channel_id=1, source_target_pairs={{0,48},{8,200},{16,0},{24,216},{32,16},{40,232},{48,32},{56,248},{... | collective-permute-start | bytes 38408 | tf_op jit(solution)/shard_map/ppermute | solution.py:409
  24.8 49.8 %copy-start.13 = (s32[3200]{0:T(1024)}, s32[3200]{0:T(1024)S(1)}, u32[]{:S(2)}) copy-start(s32[3200]{0:T(1024)S(1)} %collective-permute-done.2.refs_3_.todo) | copy-start | bytes 38404
  24.8 33.8 %collective-permute-start.6 = (bf16[32,128,128]{2,1,0:T(8,128)(2,1)}, bf16[32,128,128]{2,1,0:T(8,128)(2,1)}, u32[]{:S(2)}, u32[]{:S(2)}) collective-permute-start(bf16[32,128,128]{2,1,0:T(8,128)(2,1)} %get-tuple-element.23), channel_id=1, source_target_pairs={{0,128},{8,40},{16,144},{24,56},{32,160},{40,8},{48,176},{56,24},{... | collective-permute-start | bytes 3145736 | tf_op jit(solution)/shard_map/ppermute | solution.py:403
  25.3 36.2 %collective-permute-start.7 = (bf16[32,128,128]{2,1,0:T(8,128)(2,1)}, bf16[32,128,128]{2,1,0:T(8,128)(2,1)}, u32[]{:S(2)}, u32[]{:S(2)}) collective-permute-start(bf16[32,128,128]{2,1,0:T(8,128)(2,1)} %get-tuple-element.24), channel_id=1, source_target_pairs={{0,40},{8,128},{16,56},{24,144},{32,8},{40,160},{48,24},{56,176},{... | collective-permute-start | bytes 3145736 | tf_op jit(solution)/shard_map/ppermute | solution.py:403
  28.3 46.3 %copy-start.3 = (bf16[32,128,128]{2,1,0:T(8,128)(2,1)}, bf16[32,128,128]{2,1,0:T(8,128)(2,1)S(1)}, u32[]{:S(2)}) copy-start(bf16[32,128,128]{2,1,0:T(8,128)(2,1)S(1)} %collective-permute-done.3.refs_5_.refs_1_) | copy-start | bytes 3145732
  28.3 43.6 %collective-permute-start.8 = (bf16[32,128,128]{2,1,0:T(8,128)(2,1)}, bf16[32,128,128]{2,1,0:T(8,128)(2,1)}, u32[]{:S(2)}, u32[]{:S(2)}) collective-permute-start(bf16[32,128,128]{2,1,0:T(8,128)(2,1)} %get-tuple-element.25), channel_id=1, source_target_pairs={{0,192},{8,56},{16,208},{24,8},{32,224},{40,24},{48,240},{56,40},{... | collective-permute-start | bytes 3145736 | tf_op jit(solution)/shard_map/ppermute | solution.py:403
  30.9 42.0 %collective-permute-start.9 = (bf16[32,128,128]{2,1,0:T(8,128)(2,1)}, bf16[32,128,128]{2,1,0:T(8,128)(2,1)}, u32[]{:S(2)}, u32[]{:S(2)}) collective-permute-start(bf16[32,128,128]{2,1,0:T(8,128)(2,1)} %get-tuple-element.26), channel_id=1, source_target_pairs={{0,56},{8,192},{16,8},{24,208},{32,24},{40,224},{48,40},{56,240},{... | collective-permute-start | bytes 3145736 | tf_op jit(solution)/shard_map/ppermute | solution.py:403
  58.6 26.1 %collective-permute-start.15 = (s32[1024,128]{1,0:T(8,128)}, s32[1024,128]{1,0:T(8,128)}, u32[]{:S(2)}, u32[]{:S(2)}) collective-permute-start(s32[1024,128]{1,0:T(8,128)} %get-tuple-element.31.refs_8_), channel_id=1, source_target_pairs={{0,32},{8,136},{16,48},{24,152},{32,0},{40,168},{48,16},{56,184},{... | collective-permute-start | bytes 1572872 | tf_op jit(solution)/shard_map/ppermute | solution.py:410
  58.6 23.0 %collective-permute-start.1 = (s32[3200]{0:T(1024)}, s32[3200]{0:T(1024)S(1)}, u32[]{:S(2)}, u32[]{:S(2)}) collective-permute-start(s32[3200]{0:T(1024)} %plan.1.refs_0_.todo), channel_id=1, source_target_pairs={{0,32},{8,136},{16,48},{24,152},{32,0},{40,168},{48,16},{56,184},{... | collective-permute-start | bytes 38408 | tf_op jit(solution)/shard_map/ppermute | solution.py:409
  61.6 33.7 %collective-permute-start = (s32[3200]{0:T(1024)}, s32[3200]{0:T(1024)S(1)}, u32[]{:S(2)}, u32[]{:S(2)}) collective-permute-start(s32[3200]{0:T(1024)} %plan.1.refs_0_.todo), channel_id=1, source_target_pairs={{0,16},{8,72},{16,32},{24,88},{32,48},{40,104},{48,0},{56,120},{64... | collective-permute-start | bytes 38408 | tf_op jit(solution)/shard_map/ppermute | solution.py:409
  72.0 30.7 %collective-permute-start.13 = (s32[1024,128]{1,0:T(8,128)}, s32[1024,128]{1,0:T(8,128)}, u32[]{:S(2)}, u32[]{:S(2)}) collective-permute-start(s32[1024,128]{1,0:T(8,128)} %get-tuple-element.31.refs_8_), channel_id=1, source_target_pairs={{0,16},{8,72},{16,32},{24,88},{32,48},{40,104},{48,0},{56,120},{64... | collective-permute-start | bytes 1572872 | tf_op jit(solution)/shard_map/ppermute | solution.py:410
  73.0 22.9 %collective-permute-start.19 = (bf16[1024,128]{1,0:T(8,128)(2,1)S(1)}, bf16[1024,128]{1,0:T(8,128)(2,1)}, u32[]{:S(2)}, u32[]{:S(2)}) collective-permute-start(bf16[1024,128]{1,0:T(8,128)(2,1)S(1)} %copy-done.6), channel_id=1, source_target_pairs={{0,1},{1,2},{2,3},{3,4},{4,5},{5,6},{6,7},{7,0},{8,9},{9,10},{10,1... | collective-permute-start | bytes 786440 | tf_op jit(solution)/shard_map/ppermute | solution.py:413
  81.6 18.7 %collective-permute-start.20 = (bf16[1024,128]{1,0:T(8,128)(2,1)S(1)}, bf16[1024,128]{1,0:T(8,128)(2,1)S(1)}, u32[]{:S(2)}, u32[]{:S(2)}) collective-permute-start(bf16[1024,128]{1,0:T(8,128)(2,1)S(1)} %copy-done.6), channel_id=1, source_target_pairs={{0,2},{1,3},{2,4},{3,5},{4,6},{5,7},{6,0},{7,1},{8,10},{9,11},{10,... | collective-permute-start | bytes 786440 | tf_op jit(solution)/shard_map/ppermute | solution.py:413
  84.7 28.8 %collective-permute-start.21 = (bf16[1024,128]{1,0:T(8,128)(2,1)S(1)}, bf16[1024,128]{1,0:T(8,128)(2,1)S(1)}, u32[]{:S(2)}, u32[]{:S(2)}) collective-permute-start(bf16[1024,128]{1,0:T(8,128)(2,1)S(1)} %copy-done.6), channel_id=1, source_target_pairs={{0,3},{1,4},{2,5},{3,6},{4,7},{5,0},{6,1},{7,2},{8,11},{9,12},{10,... | collective-permute-start | bytes 786440 | tf_op jit(solution)/shard_map/ppermute | solution.py:413
  95.3 28.3 %collective-permute-start.22 = (bf16[1024,128]{1,0:T(8,128)(2,1)S(1)}, bf16[1024,128]{1,0:T(8,128)(2,1)S(1)}, u32[]{:S(2)}, u32[]{:S(2)}) collective-permute-start(bf16[1024,128]{1,0:T(8,128)(2,1)S(1)} %copy-done.6), channel_id=1, source_target_pairs={{0,4},{1,5},{2,6},{3,7},{4,0},{5,1},{6,2},{7,3},{8,12},{9,13},{10,... | collective-permute-start | bytes 786440 | tf_op jit(solution)/shard_map/ppermute | solution.py:413
  95.8 31.8 %collective-permute-start.23 = (bf16[1024,128]{1,0:T(8,128)(2,1)S(1)}, bf16[1024,128]{1,0:T(8,128)(2,1)S(1)}, u32[]{:S(2)}, u32[]{:S(2)}) collective-permute-start(bf16[1024,128]{1,0:T(8,128)(2,1)S(1)} %copy-done.6), channel_id=1, source_target_pairs={{0,5},{1,6},{2,7},{3,0},{4,1},{5,2},{6,3},{7,4},{8,13},{9,14},{10,... | collective-permute-start | bytes 786440 | tf_op jit(solution)/shard_map/ppermute | solution.py:413
  100.3 39.6 %collective-permute-start.24 = (bf16[1024,128]{1,0:T(8,128)(2,1)S(1)}, bf16[1024,128]{1,0:T(8,128)(2,1)S(1)}, u32[]{:S(2)}, u32[]{:S(2)}) collective-permute-start(bf16[1024,128]{1,0:T(8,128)(2,1)S(1)} %copy-done.6), channel_id=1, source_target_pairs={{0,6},{1,7},{2,0},{3,1},{4,2},{5,3},{6,4},{7,5},{8,14},{9,15},{10,... | collective-permute-start | bytes 786440 | tf_op jit(solution)/shard_map/ppermute | solution.py:413
  102.7 39.7 %collective-permute-start.25 = (bf16[1024,128]{1,0:T(8,128)(2,1)S(1)}, bf16[1024,128]{1,0:T(8,128)(2,1)S(1)}, u32[]{:S(2)}, u32[]{:S(2)}) collective-permute-start(bf16[1024,128]{1,0:T(8,128)(2,1)S(1)} %copy-done.6), channel_id=1, source_target_pairs={{0,7},{1,0},{2,1},{3,2},{4,3},{5,4},{6,5},{7,6},{8,15},{9,8},{10,9... | collective-permute-start | bytes 786440 | tf_op jit(solution)/shard_map/ppermute | solution.py:413
  113.5 40.2 %collective-permute-start.18 = (bf16[16,128,128]{2,1,0:T(8,128)(2,1)S(1)}, bf16[16,128,128]{2,1,0:T(8,128)(2,1)}, u32[]{:S(2)}, u32[]{:S(2)}) collective-permute-start(bf16[16,128,128]{2,1,0:T(8,128)(2,1)S(1)} %copy-done.16), channel_id=1, source_target_pairs={{0,16},{8,72},{16,32},{24,88},{32,48},{40,104},{48,0},{56,120},{64... | collective-permute-start | bytes 1572872 | tf_op jit(solution)/shard_map/ppermute | solution.py:424
  123.6 30.2 %collective-permute-start.16 = (bf16[16,128,128]{2,1,0:T(8,128)(2,1)S(1)}, bf16[16,128,128]{2,1,0:T(8,128)(2,1)}, u32[]{:S(2)}, u32[]{:S(2)}) collective-permute-start(bf16[16,128,128]{2,1,0:T(8,128)(2,1)S(1)} %copy-done.17), channel_id=1, source_target_pairs={{0,32},{8,136},{16,48},{24,152},{32,0},{40,168},{48,16},{56,184},{... | collective-permute-start | bytes 1572872 | tf_op jit(solution)/shard_map/ppermute | solution.py:424
  127.7 26.1 %collective-permute-start.14 = (bf16[16,128,128]{2,1,0:T(8,128)(2,1)}, bf16[16,128,128]{2,1,0:T(8,128)(2,1)}, u32[]{:S(2)}, u32[]{:S(2)}) collective-permute-start(bf16[16,128,128]{2,1,0:T(8,128)(2,1)} %shard_map.84), channel_id=1, source_target_pairs={{0,48},{8,200},{16,0},{24,216},{32,16},{40,232},{48,32},{56,248},{... | collective-permute-start | bytes 1572872 | tf_op jit(solution)/shard_map/ppermute | solution.py:424
  146.1 51.1 %collective-permute-start.26 = (bf16[8,1024,128]{2,1,0:T(8,128)(2,1)}, bf16[8,1024,128]{2,1,0:T(8,128)(2,1)S(1)}, u32[]{:S(2)}, u32[]{:S(2)}) collective-permute-start(bf16[8,1024,128]{2,1,0:T(8,128)(2,1)} %gather_weights.1.w_mine), channel_id=1, source_target_pairs={{0,8},{8,0},{16,24},{24,16},{32,40},{40,32},{48,56},{56,48},{64,72... | collective-permute-start | bytes 6291464 | tf_op jit(solution)/shard_map/ppermute | solution.py:415
  157.4 33.0 %all-to-all-start.1 = ((bf16[8,2,128,128]{3,2,1,0:T(8,128)(2,1)}), bf16[8,2,128,128]{3,2,1,0:T(8,128)(2,1)S(1)}, u32[]{:S(2)}, u32[]{:S(2)}) async-start(bf16[8,2,128,128]{3,2,1,0:T(8,128)(2,1)} %bitcast.10), calls=%async_computation.1 | async-start | bytes 1048576 | tf_op jit(solution)/shard_map/all_to_all | solution.py:427
  168.1 15.6 %collective-permute-start.10 = (bf16[16,128,128]{2,1,0:T(8,128)(2,1)}, bf16[16,128,128]{2,1,0:T(8,128)(2,1)S(1)}, u32[]{:S(2)}, u32[]{:S(2)}) collective-permute-start(bf16[16,128,128]{2,1,0:T(8,128)(2,1)} %get-tuple-element.28), channel_id=1, source_target_pairs={{0,48},{8,200},{16,0},{24,216},{32,16},{40,232},{48,32},{56,248},{... | collective-permute-start | bytes 1572872 | tf_op jit(solution)/shard_map/ppermute | solution.py:420
  171.7 12.1 %collective-permute-start.11 = (bf16[16,128,128]{2,1,0:T(8,128)(2,1)}, bf16[16,128,128]{2,1,0:T(8,128)(2,1)}, u32[]{:S(2)}, u32[]{:S(2)}) collective-permute-start(bf16[16,128,128]{2,1,0:T(8,128)(2,1)} %get-tuple-element.29), channel_id=1, source_target_pairs={{0,32},{8,136},{16,48},{24,152},{32,0},{40,168},{48,16},{56,184},{... | collective-permute-start | bytes 1572872 | tf_op jit(solution)/shard_map/ppermute | solution.py:420
  171.7 15.2 %collective-permute-start.12 = (bf16[16,128,128]{2,1,0:T(8,128)(2,1)}, bf16[16,128,128]{2,1,0:T(8,128)(2,1)}, u32[]{:S(2)}, u32[]{:S(2)}) collective-permute-start(bf16[16,128,128]{2,1,0:T(8,128)(2,1)} %get-tuple-element.30), channel_id=1, source_target_pairs={{0,16},{8,72},{16,32},{24,88},{32,48},{40,104},{48,0},{56,120},{64... | collective-permute-start | bytes 1572872 | tf_op jit(solution)/shard_map/ppermute | solution.py:420
  190.5 24.7 %all-to-all-start = ((bf16[8,2,128,128]{3,2,1,0:T(8,128)(2,1)}), bf16[8,2,128,128]{3,2,1,0:T(8,128)(2,1)S(1)}, u32[]{:S(2)}, u32[]{:S(2)}) async-start(bf16[8,2,128,128]{3,2,1,0:T(8,128)(2,1)} %bitcast.11), calls=%async_computation | async-start | bytes 1048576 | tf_op jit(solution)/shard_map/all_to_all | solution.py:427
  (16 other events, 241.8 us)

commit v2 on v0

--- a/solution.py
+++ b/solution.py
@@ -18,6 +18,8 @@
 N_ITEMS = DST * TILES
 SECTION = N_ITEMS + ROWS
 UNROLL = 4
+EARLY = (0, 1, 2, 3, 6, 7)
+LATE = (4, 5)
 BF = jnp.bfloat16
 F32 = jnp.float32
 I32 = jnp.int32
@@ -25,6 +27,7 @@
 VMEM = pl.BlockSpec(memory_space=pltpu.VMEM)
 SMEM = pl.BlockSpec(memory_space=pltpu.SMEM)
 ANY = pl.BlockSpec(memory_space=pl.ANY)
+LIMIT = pltpu.CompilerParams(vmem_limit_bytes=24 * 2**20)
 
 
 def dom_of(y, x, core):
@@ -75,7 +78,7 @@
             shard1 = dom_of(wrapped(y - m), wrapped(x + d), 1)
             shard = jnp.where(to_one == 1, shard1, shard0)
             for s in range(CAP):
-                stage[q, m * CAP + s] = ft[req[shard, s]]
+                stage[q, m * CAP + s] = ft[req[s, shard]]
         copy = pltpu.make_async_copy(stage.at[q], outs[q], sem.at[q])
         copy.start()
         copies.append(copy)
@@ -96,6 +99,7 @@
             pltpu.SemaphoreType.DMA((N_SRC,)),
         ],
         cost_estimate=pl.CostEstimate(flops=10**9, bytes_accessed=10**7, transcendentals=0),
+        compiler_params=LIMIT,
         name="pack",
     )(me, requests, features)
 
@@ -127,14 +131,17 @@
         in_specs=[SMEM] + [VMEM] * 3,
         out_specs=(VMEM, VMEM),
         cost_estimate=pl.CostEstimate(flops=10**9, bytes_accessed=10**7, transcendentals=0),
+        compiler_params=LIMIT,
         name="tables",
     )(me, local_nbr, w_self, w_neigh)
 
 
 def plan_kernel(me, cnt, tile_block, tile_count, todo, slot, size):
     core, x, y = me[0] & 1, (me[0] >> 1) & (RING - 1), me[0] >> 3
-    for m in range(RING + 1):
+    for m in range(RING):
         size[m] = m * SECTION
+        size[RING + m] = m * SECTION + N_ITEMS - 1
+    size[2 * RING] = RING * SECTION + SECTION // 2
 
     def owner(o, p):
         co, xo, yo = o & 1, (o >> 1) & (RING - 1), o >> 3
@@ -155,17 +162,19 @@
     def block(i, _):
         v = slot[i]
         for m in range(RING):
-            todo[m * SECTION + N_ITEMS + 1 + i] = jnp.where((v >> 3) & (RING - 1) == m, v, -1)
+            todo[m * SECTION + N_ITEMS + 2 + i] = jnp.where((v >> 3) & (RING - 1) == m, v, -1)
         used = tile_count[i]
 
         def tile(h, _):
             vs = [slot[tile_block[i, h * UNROLL + u]] for u in range(UNROLL)]
             for u, v in enumerate(vs):
                 t = h * UNROLL + u
-                m = jnp.where(t < used, (v >> 3) & (RING - 1), RING)
+                late = v >> 6 == 2
+                m = jnp.where(late, RING, 0) + ((v >> 3) & (RING - 1))
+                m = jnp.where(t < used, m, 2 * RING)
                 n = size[m]
                 todo[n] = v + 256 * i + 4096 * t
-                size[m] = n + 1
+                size[m] = n + jnp.where(late, -1, 1)
             return 0
 
         lax.fori_loop(0, (used + UNROLL - 1) // UNROLL, tile, 0)
@@ -174,6 +183,7 @@
     lax.fori_loop(0, DST, block, 0)
     for m in range(RING):
         todo[m * SECTION + N_ITEMS] = size[m] - m * SECTION
+        todo[m * SECTION + N_ITEMS + 1] = m * SECTION + N_ITEMS - 1 - size[RING + m]
 
 
 def plan(me, counts, tile_block, tile_count):
@@ -182,8 +192,9 @@
         out_shape=jax.ShapeDtypeStruct(((RING + 1) * SECTION,), I32),
         in_specs=[SMEM] * 4,
         out_specs=SMEM,
-        scratch_shapes=[pltpu.SMEM((FRONT,), I32), pltpu.SMEM((RING + 1,), I32)],
+        scratch_shapes=[pltpu.SMEM((FRONT,), I32), pltpu.SMEM((2 * RING + 1,), I32)],
         cost_estimate=pl.CostEstimate(flops=2 * 10**9, bytes_accessed=10**6, transcendentals=0),
+        compiler_params=LIMIT,
         name="plan",
     )(me, counts, tile_block, tile_count)
 
@@ -198,12 +209,15 @@
     for m in range(RING):
 
         def start(i, _):
-            v = lists[m][m * SECTION + N_ITEMS + 1 + i]
-            for q in range(N_SRC):
-
-                @pl.when(v >> 5 == q)
-                def _():
-                    copy_of(q, m * DST + i, v).start()
+            v = lists[m][m * SECTION + N_ITEMS + 2 + i]
+
+            @pl.when(v >= 0)
+            def _():
+                for q in range(N_SRC):
+
+                    @pl.when(v >> 5 == q)
+                    def _():
+                        copy_of(q, m * DST + i, v).start()
 
             @pl.when(v < 0)
             def _():
@@ -215,7 +229,7 @@
     for m in range(RING):
 
         def finish(i, _):
-            @pl.when(lists[m][m * SECTION + N_ITEMS + 1 + i] >= 0)
+            @pl.when(lists[m][m * SECTION + N_ITEMS + 2 + i] >= 0)
             def _():
                 copy_of(0, 0, 0).wait()
 
@@ -243,40 +257,29 @@
             pltpu.SemaphoreType.DMA((RING,)),
         ],
         cost_estimate=pl.CostEstimate(flops=10**9, bytes_accessed=10**7, transcendentals=0),
+        compiler_params=LIMIT,
         name="own_rows",
     )(*lists, *sources)
 
 
-def agg_kernel(*refs):
-    lists, src, nbr = refs[:RING], refs[RING : RING + N_SRC], refs[RING + N_SRC : 2 * RING + N_SRC]
-    outs, (blocks, acc, sem) = refs[2 * RING + N_SRC : 3 * RING + N_SRC], refs[3 * RING + N_SRC :]
-    fetch = [pltpu.make_async_copy(src[q], blocks.at[pl.ds(q * 32, 32)], sem.at[q]) for q in range(N_SRC)]
-    for copy in fetch:
-        copy.start()
-
-    def clear(n, _):
-        acc[n] = jnp.zeros((ROWS, ROWS), F32)
-        return 0
-
-    lax.fori_loop(0, RING * DST + 1, clear, 0, unroll=5)
+def add_sums(lists, nbr, blocks, acc, late):
     iota = lax.broadcasted_iota(I32, (ROWS, ROWS), 0).astype(F32).astype(BF)
     one, zero = jnp.ones((), BF), jnp.zeros((), BF)
-    for copy in fetch:
-        copy.wait()
-
-    for m in (1, 2, 3, 0):
+    for m in range(RING):
         todo = lists[m]
-        n_item = todo[m * SECTION + N_ITEMS]
-
-        def some(h, _):
+        n_item = todo[m * SECTION + N_ITEMS + late]
+
+        def some(h, _, m=m, todo=todo, n_item=n_item):
             parts = []
             for u in range(UNROLL):
                 n = h * UNROLL + u
-                item = jnp.where(n < n_item, todo[m * SECTION + n], 0)
-                blk = item & 255
+                place = m * SECTION + (N_ITEMS - 1 - n if late else n)
+                item = jnp.where(n < n_item, todo[place], 128 * late)
+                q = (item >> 5) & 7
+                q = q - 4 if late else jnp.where(q > 3, q - 2, q)
+                blk = q * (RING * CAP) + (item & 31)
                 i = (item >> 8) & 15
                 t = item >> 12
-                dst = jnp.where(n < n_item, m * DST + i, RING * DST)
                 row0 = i * (ROWS // 2) + (t & 15) * FAN_T
                 shift = (t >> 4) * 16
                 total = None
@@ -284,12 +287,69 @@
                     row = (nbr[m][pl.ds(row0 + f, 1), :] >> shift) & 65535
                     hit = jnp.where(iota == row.astype(F32).astype(BF), one, zero)
                     total = hit if total is None else total + hit
+                dst = jnp.where(n < n_item, m * DST + i, RING * DST)
                 parts.append((dst, jnp.dot(blocks[blk], total, preferred_element_type=F32)))
             for dst, part in parts:
                 acc[dst] += part
             return 0
 
         lax.fori_loop(0, (n_item + UNROLL - 1) // UNROLL, some, 0)
+
+
+def fetched(src, blocks, sem):
+    some = RING * CAP
+    copies = [pltpu.make_async_copy(s, blocks.at[pl.ds(q * some, some)], sem.at[q]) for q, s in enumerate(src)]
+    for copy in copies:
+        copy.start()
+    return copies
+
+
+def early_kernel(*refs):
+    lists, src, nbr = refs[:RING], refs[RING : RING + len(EARLY)], refs[RING + len(EARLY) : 2 * RING + len(EARLY)]
+    out, blocks, acc, sem, sem_out = refs[2 * RING + len(EARLY) :]
+    copies = fetched(src, blocks, sem)
+
+    def clear(n, _):
+        acc[n] = jnp.zeros((ROWS, ROWS), F32)
+        return 0
+
+    lax.fori_loop(0, RING * DST + 1, clear, 0)
+    for copy in copies:
+        copy.wait()
+    add_sums(lists, nbr, blocks, acc, 0)
+    leave = pltpu.make_async_copy(acc.at[pl.ds(0, RING * DST)], out, sem_out)
+    leave.start()
+    leave.wait()
+
+
+def early_sums(lists, sources, nbrs):
+    return pl.pallas_call(
+        early_kernel,
+        out_shape=jax.ShapeDtypeStruct((RING * DST, ROWS, ROWS), F32),
+        in_specs=[SMEM] * RING + [ANY] * len(EARLY) + [VMEM] * RING,
+        out_specs=ANY,
+        scratch_shapes=[
+            pltpu.VMEM((len(EARLY) * RING * CAP, ROWS, ROWS), BF),
+            pltpu.VMEM((RING * DST + 1, ROWS, ROWS), F32),
+            pltpu.SemaphoreType.DMA((len(EARLY),)),
+            pltpu.SemaphoreType.DMA,
+        ],
+        cost_estimate=pl.CostEstimate(flops=10**10, bytes_accessed=2 * 10**7, transcendentals=0),
+        compiler_params=LIMIT,
+        name="early",
+    )(*lists, *sources, *nbrs)
+
+
+def late_kernel(*refs):
+    lists, src, nbr = refs[:RING], refs[RING : RING + len(LATE)], refs[RING + len(LATE) : 2 * RING + len(LATE)]
+    early, outs = refs[2 * RING + len(LATE)], refs[2 * RING + len(LATE) + 1 : 3 * RING + len(LATE) + 1]
+    blocks, acc, sem, sem_in = refs[3 * RING + len(LATE) + 1 :]
+    begin = pltpu.make_async_copy(early, acc.at[pl.ds(0, RING * DST)], sem_in)
+    begin.start()
+    for copy in fetched(src, blocks, sem):
+        copy.wait()
+    begin.wait()
+    add_sums(lists, nbr, blocks, acc, 1)
     for m in range(RING):
 
         def leave(n, _):
@@ -299,20 +359,22 @@
         lax.fori_loop(0, DST, leave, 0, unroll=4)
 
 
-def aggregate(lists, sources, nbrs):
-    return pl.pallas_call(
-        agg_kernel,
+def late_sums(lists, sources, nbrs, early):
+    return pl.pallas_call(
+        late_kernel,
         out_shape=[jax.ShapeDtypeStruct((DST, ROWS, ROWS), BF)] * RING,
-        in_specs=[SMEM] * RING + [ANY] * N_SRC + [VMEM] * RING,
+        in_specs=[SMEM] * RING + [ANY] * len(LATE) + [VMEM] * RING + [ANY],
         out_specs=[VMEM] * RING,
         scratch_shapes=[
-            pltpu.VMEM((N_SRC * 32, ROWS, ROWS), BF),
+            pltpu.VMEM((len(LATE) * RING * CAP, ROWS, ROWS), BF),
             pltpu.VMEM((RING * DST + 1, ROWS, ROWS), F32),
-            pltpu.SemaphoreType.DMA((N_SRC,)),
+            pltpu.SemaphoreType.DMA((len(LATE),)),
+            pltpu.SemaphoreType.DMA,
         ],
         cost_estimate=pl.CostEstimate(flops=10**10, bytes_accessed=2 * 10**7, transcendentals=0),
-        name="agg",
-    )(*lists, *sources, *nbrs)
+        compiler_params=LIMIT,
+        name="late",
+    )(*lists, *sources, *nbrs, early)
 
 
 def join_own_kernel(a, b, c, d, out):
@@ -334,6 +396,7 @@
         in_specs=[SMEM] * len(scalars) + [VMEM] * RING,
         out_specs=VMEM,
         cost_estimate=pl.CostEstimate(flops=10**9, bytes_accessed=5 * 10**6, transcendentals=0),
+        compiler_params=LIMIT,
     )(*scalars, *parts)
 
 
@@ -350,6 +413,7 @@
         in_specs=[VMEM] * len(parts),
         out_specs=VMEM,
         cost_estimate=pl.CostEstimate(flops=10**9, bytes_accessed=5 * 10**6, transcendentals=0),
+        compiler_params=LIMIT,
         name="gather_weights",
     )(*parts)
 
@@ -384,6 +448,7 @@
         out_specs=VMEM,
         scratch_shapes=[pltpu.VMEM((D, ROWS), F32)],
         cost_estimate=pl.CostEstimate(flops=10**9, bytes_accessed=5 * 10**6, transcendentals=0),
+        compiler_params=LIMIT,
         name="project",
     )(me, column, xs, xa, w_mine, w_other)
 
@@ -392,7 +457,7 @@
     n_col = lax.axis_size("col")
     me = lax.axis_index("dom").reshape(1).astype(I32)
     column = lax.axis_index("col").reshape(1).astype(I32)
-    packed = pack(me, requests[0], features)
+    packed = pack(me, requests[0].T, features)
     sources = [packed[0]]
     for q in range(1, N_SRC):
         sources.append(lax.ppermute(packed[q], "dom", meet_pairs(q // 2, q % 2)))
@@ -413,7 +478,8 @@
     own_here = [own_parts[0]]
     for m in range(1, RING):
         own_here.append(lax.ppermute(own_parts[m], "dom", ring_pairs(RING - m)))
-    agg_parts = aggregate(lists, sources, nbrs)
+    early = early_sums(lists, [sources[q] for q in EARLY], nbrs)
+    agg_parts = late_sums(lists, [sources[q] for q in LATE], nbrs, early)
     agg_here = [agg_parts[0]]
     for m in range(1, RING):
         agg_here.append(lax.ppermute(agg_parts[m], "dom", ring_pairs(RING - m)))

time: 232 us -> 241 us (1.039)
  the two profiles are of different devices: /device:TPU:2 before, /device:TPU:25 now
where the time goes in v2:
time: 241 us
  waiting for transfers between devices  97.7 us (41%)
  starting transfers between devices  69 us (29%)
  Pallas kernels  38.8 us (16%)
  blocking collectives  20.3 us (8%)
  local copies, waits for them, and re-layouts  14.6 us (6%)
    ppermute x7, waiting for transfers between devices, body(): sources.append(lax.ppermute(packed[q], 'dom', meet_pairs(q // 2, q % 2)))  34.7 us
    ppermute x7, waiting for transfers between devices, body(): lax.ppermute(w_t, 'col', [(i, (i + k) % n_col) for i in range(n_col)])  29.6 us
    all_to_all x1, blocking collectives, body(): return lax.all_to_all(y, 'col', 0, 0, tiled=True).reshape(-1, ROWS)  20.3 us
    all_to_all x2, waiting for transfers between devices, to_rows(): lax.all_to_all(x.reshape(n_col, DST // n_col, ROWS, ROWS), 'col', 0, 0, t...  18.1 us
    ppermute x7, starting transfers between devices, body(): lax.ppermute(w_t, 'col', [(i, (i + k) % n_col) for i in range(n_col)])  17.8 us
    ppermute x7, starting transfers between devices, body(): sources.append(lax.ppermute(packed[q], 'dom', meet_pairs(q // 2, q % 2)))  16.7 us
    all_to_all x2, starting transfers between devices, to_rows(): lax.all_to_all(x.reshape(n_col, DST // n_col, ROWS, ROWS), 'col', 0, 0, t...  15.9 us
    unnamed x43, local copies, waits for them, and re-layouts  14.6 us
  transfers between devices with their start and end apart: 29, of which 14 were waited for; matrix products, arithmetic and copies ran while one was open for 0% of the time, Pallas kernels for 14%

profile of v2, /device:TPU:25, one launch (start us, length us, event | category | flops | bytes accessed | tf_op | source)
XLA Modules:
  0.0 240.7 jit_solution(10767439176171241481)
XLA Ops:
  4.3 1.7 collective-permute-start.19
  6.0 2.9 %pack.1 = (bf16[32,128,128]{2,1,0:T(8,128)(2,1)S(1)}, bf16[32,128,128]{2,1,0:T(8,128)(2,1)S(1)}, bf16[32,128,128]{2,1,0:T(8,128)(2,1)S(1)}, bf16[32,128,128]{2,1...) custom-call(s32[1]{0:T(128)} %bitcast.me, ...), custom_call_target="tpu_custom_call" | custom-call | flops 1000000000 | bytes 10000000 | tf_op jit(solution)/shard_map/pack/pallas_call | solution.py:91
  11.2 4.8 %plan.1.refs_0_ = s32[3200]{0:T(1024)S(1)} custom-call(s32[1]{0:T(128)} %bitcast.me, s32[32]{0:T(128)S(1)} %bitcast.11, s32[16,32]{1,0:T(8,128)S(1)} %copy-done.15, s32[16]{0:T(128)S(1)} %copy-done.18), custom_call_target="tpu_custom_call" | custom-call | flops 2000000000 | bytes 1000000 | tf_op jit(solution)/shard_map/plan/pallas_call | solution.py:190
  16.4 2.3 collective-permute-start.1
  20.5 3.0 %collective-permute-start.20 = (bf16[1024,128]{1,0:T(8,128)(2,1)S(1)}, bf16[1024,128]{1,0:T(8,128)(2,1)S(1)}, u32[]{:S(2)}, u32[]{:S(2)}) collective-permute-start(bf16[1024,128]{1,0:T(8,128)(2,1)S(1)} %get-tuple-element.40.refs_0_), channel_id=1, source_target_pairs={{0,2},{1,3},{2,4},{3,5},{4,6},{5,7},{6,0},{7,1},{8,10},{9,11},{10,... | collective-permute-start | bytes 786440 | tf_op jit(solution)/shard_map/ppermute | solution.py:473
  23.5 5.1 %collective-permute-start.21 = (bf16[1024,128]{1,0:T(8,128)(2,1)S(1)}, bf16[1024,128]{1,0:T(8,128)(2,1)S(1)}, u32[]{:S(2)}, u32[]{:S(2)}) collective-permute-start(bf16[1024,128]{1,0:T(8,128)(2,1)S(1)} %get-tuple-element.40.refs_0_), channel_id=1, source_target_pairs={{0,3},{1,4},{2,5},{3,6},{4,7},{5,0},{6,1},{7,2},{8,11},{9,12},{10,... | collective-permute-start | bytes 786440 | tf_op jit(solution)/shard_map/ppermute | solution.py:473
  29.6 6.3 %collective-permute-done.20.refs_2_ = bf16[1024,128]{1,0:T(8,128)(2,1)S(1)} collective-permute-done((bf16[1024,128]{1,0:T(8,128)(2,1)S(1)}, bf16[1024,128]{1,0:T(8,128)(2,1)S(1)}, u32[]{:S(2)}, u32[]{:S(2)}) %collective-permute-start.20) | collective-permute-done | bytes 262176 | tf_op jit(solution)/shard_map/ppermute | solution.py:473
  36.0 4.6 %collective-permute-start.23 = (bf16[1024,128]{1,0:T(8,128)(2,1)S(1)}, bf16[1024,128]{1,0:T(8,128)(2,1)S(1)}, u32[]{:S(2)}, u32[]{:S(2)}) collective-permute-start(bf16[1024,128]{1,0:T(8,128)(2,1)S(1)} %get-tuple-element.40.refs_0_), channel_id=1, source_target_pairs={{0,5},{1,6},{2,7},{3,0},{4,1},{5,2},{6,3},{7,4},{8,13},{9,14},{10,... | collective-permute-start | bytes 786440 | tf_op jit(solution)/shard_map/ppermute | solution.py:473
  40.5 8.5 %collective-permute-done.21.refs_3_ = bf16[1024,128]{1,0:T(8,128)(2,1)S(1)} collective-permute-done((bf16[1024,128]{1,0:T(8,128)(2,1)S(1)}, bf16[1024,128]{1,0:T(8,128)(2,1)S(1)}, u32[]{:S(2)}, u32[]{:S(2)}) %collective-permute-start.21) | collective-permute-done | bytes 262176 | tf_op jit(solution)/shard_map/ppermute | solution.py:473
  49.1 2.3 collective-permute-start.24
  51.4 10.7 %collective-permute-done.22.refs_4_ = bf16[1024,128]{1,0:T(8,128)(2,1)S(1)} collective-permute-done((bf16[1024,128]{1,0:T(8,128)(2,1)S(1)}, bf16[1024,128]{1,0:T(8,128)(2,1)S(1)}, u32[]{:S(2)}, u32[]{:S(2)}) %collective-permute-start.22) | collective-permute-done | bytes 262176 | tf_op jit(solution)/shard_map/ppermute | solution.py:473
  62.1 5.5 %collective-permute-start.5 = (bf16[32,128,128]{2,1,0:T(8,128)(2,1)S(1)}, bf16[32,128,128]{2,1,0:T(8,128)(2,1)S(1)}, u32[]{:S(2)}, u32[]{:S(2)}) collective-permute-start(bf16[32,128,128]{2,1,0:T(8,128)(2,1)S(1)} %get-tuple-element.26), channel_id=1, source_target_pairs={{0,24},{8,64},{16,40},{24,80},{32,56},{40,96},{48,8},{56,112},{64,... | collective-permute-start | bytes 3145736 | tf_op jit(solution)/shard_map/ppermute | solution.py:463
  67.6 3.2 %collective-permute-done.24.refs_6_ = bf16[1024,128]{1,0:T(8,128)(2,1)S(1)} collective-permute-done((bf16[1024,128]{1,0:T(8,128)(2,1)S(1)}, bf16[1024,128]{1,0:T(8,128)(2,1)S(1)}, u32[]{:S(2)}, u32[]{:S(2)}) %collective-permute-start.24) | collective-permute-done | bytes 262176 | tf_op jit(solution)/shard_map/ppermute | solution.py:473
  70.8 2.7 %collective-permute-start.6 = (bf16[32,128,128]{2,1,0:T(8,128)(2,1)S(1)}, bf16[32,128,128]{2,1,0:T(8,128)(2,1)S(1)}, u32[]{:S(2)}, u32[]{:S(2)}) collective-permute-start(bf16[32,128,128]{2,1,0:T(8,128)(2,1)S(1)} %get-tuple-element.27), channel_id=1, source_target_pairs={{0,128},{8,40},{16,144},{24,56},{32,160},{40,8},{48,176},{56,24},{... | collective-permute-start | bytes 3145736 | tf_op jit(solution)/shard_map/ppermute | solution.py:463
  74.4 5.0 %collective-permute-start.7 = (bf16[32,128,128]{2,1,0:T(8,128)(2,1)S(1)}, bf16[32,128,128]{2,1,0:T(8,128)(2,1)S(1)}, u32[]{:S(2)}, u32[]{:S(2)}) collective-permute-start(bf16[32,128,128]{2,1,0:T(8,128)(2,1)S(1)} %get-tuple-element.28), channel_id=1, source_target_pairs={{0,40},{8,128},{16,56},{24,144},{32,8},{40,160},{48,24},{56,176},{... | collective-permute-start | bytes 3145736 | tf_op jit(solution)/shard_map/ppermute | solution.py:463
  80.6 21.2 %collective-permute-done.5.refs_7_ = bf16[32,128,128]{2,1,0:T(8,128)(2,1)S(1)} collective-permute-done((bf16[32,128,128]{2,1,0:T(8,128)(2,1)S(1)}, bf16[32,128,128]{2,1,0:T(8,128)(2,1)S(1)}, u32[]{:S(2)}, u32[]{:S(2)}) %collective-permute-start.5) | collective-permute-done | bytes 1048608 | tf_op jit(solution)/shard_map/ppermute | solution.py:463
  104.1 12.8 %collective-permute-done.8.refs_10_.refs_8_ = bf16[32,128,128]{2,1,0:T(8,128)(2,1)S(1)} collective-permute-done((bf16[32,128,128]{2,1,0:T(8,128)(2,1)S(1)}, bf16[32,128,128]{2,1,0:T(8,128)(2,1)S(1)}, u32[]{:S(2)}, u32[]{:S(2)}) %collective-permute-start.8) | collective-permute-done | bytes 1048608 | tf_op jit(solution)/shard_map/ppermute | solution.py:463
  116.9 5.5 %collective-permute-start.26 = (bf16[8,1024,128]{2,1,0:T(8,128)(2,1)S(1)}, bf16[8,1024,128]{2,1,0:T(8,128)(2,1)}, u32[]{:S(2)}, u32[]{:S(2)}) collective-permute-start(bf16[8,1024,128]{2,1,0:T(8,128)(2,1)S(1)} %gather_weights.1.w_mine), channel_id=1, source_target_pairs={{0,8},{8,0},{16,24},{24,16},{32,40},{40,32},{48,56},{56,48},{64,72... | collective-permute-start | bytes 6291464 | tf_op jit(solution)/shard_map/ppermute | solution.py:475
  122.4 3.6 %own_rows.1 = (bf16[16,128,128]{2,1,0:T(8,128)(2,1)S(1)}, bf16[16,128,128]{2,1,0:T(8,128)(2,1)S(1)}, bf16[16,128,128]{2,1,0:T(8,128)(2,1)S(1)}, bf16[16,128,128]{2,1,0:T(8,128)(2,1)S(1)}) custom-call(s32[3200]{0:T(1024)S(1)} %plan.1.refs_0_, s32[3200]{0:T(1024)S(1)} %collective-permute-done.refs_1_, s32[3200]{0:T(1024)S(1)} %collective-permute-done.1.refs_2_, ...), custom_call_target="tpu_custom_call" | custom-call | flops 1000000000 | bytes 10000000 | tf_op jit(solution)/shard_map/own_rows/pallas_call | solution.py:249
  126.6 4.9 %collective-permute-start.11 = (bf16[16,128,128]{2,1,0:T(8,128)(2,1)S(1)}, bf16[16,128,128]{2,1,0:T(8,128)(2,1)S(1)}, u32[]{:S(2)}, u32[]{:S(2)}) collective-permute-start(bf16[16,128,128]{2,1,0:T(8,128)(2,1)S(1)} %get-tuple-element.33), channel_id=1, source_target_pairs={{0,32},{8,136},{16,48},{24,152},{32,0},{40,168},{48,16},{56,184},{... | collective-permute-start | bytes 1572872 | tf_op jit(solution)/shard_map/ppermute | solution.py:480
  131.4 1.5 collective-permute-done.15.refs_13_.refs_9_
  133.0 13.7 %early.1.refs_10_ = f32[64,128,128]{2,1,0:T(8,128)S(1)} custom-call(s32[3200]{0:T(1024)S(1)} %plan.1.refs_0_, s32[3200]{0:T(1024)S(1)} %collective-permute-done.refs_1_, s32[3200]{0:T(1024)S(1)} %collective-permute-done.1.refs_2_, s32[3200]{0:T(1024)S(1)} %collective-permute-done.2.refs_3_, bf16[32,128,128]{2,1,0:T(8,128)(2,1)S(1)} %get-tuple-element.23.refs_4_, ...), custom_call_target="tpu_custom_call" | custom-call | flops 10000000000 | bytes 20000000 | tf_op jit(solution)/shard_map/early/pallas_call | solution.py:326
  146.8 2.0 copy-done.19
  149.8 9.2 %all-to-all-start = ((bf16[8,2,128,128]{3,2,1,0:T(8,128)(2,1)}), bf16[8,2,128,128]{3,2,1,0:T(8,128)(2,1)S(1)}, u32[]{:S(2)}, u32[]{:S(2)}) async-start(bf16[8,2,128,128]{3,2,1,0:T(8,128)(2,1)} %bitcast.5), calls=%async_computation | async-start | bytes 1048576 | tf_op jit(solution)/shard_map/all_to_all | solution.py:488
  164.6 2.2 copy-done.20
  166.8 6.7 %late.1 = (bf16[16,128,128]{2,1,0:T(8,128)(2,1)S(1)}, bf16[16,128,128]{2,1,0:T(8,128)(2,1)S(1)}, bf16[16,128,128]{2,1,0:T(8,128)(2,1)S(1)}, bf16[16,128,128]{2,1,0:T(8,128)(2,1)S(1)}) custom-call(s32[3200]{0:T(1024)S(1)} %plan.1.refs_0_, s32[3200]{0:T(1024)S(1)} %collective-permute-done.refs_1_, s32[3200]{0:T(1024)S(1)} %collective-permute-done.1.refs_2_, ...), custom_call_target="tpu_custom_call" | custom-call | flops 10000000000 | bytes 20000000 | tf_op jit(solution)/shard_map/late/pallas_call | solution.py:363
  173.7 2.6 %collective-permute-start.18 = (bf16[16,128,128]{2,1,0:T(8,128)(2,1)S(1)}, bf16[16,128,128]{2,1,0:T(8,128)(2,1)S(1)}, u32[]{:S(2)}, u32[]{:S(2)}) collective-permute-start(bf16[16,128,128]{2,1,0:T(8,128)(2,1)S(1)} %get-tuple-element.39), channel_id=1, source_target_pairs={{0,16},{8,72},{16,32},{24,88},{32,48},{40,104},{48,0},{56,120},{64... | collective-permute-start | bytes 1572872 | tf_op jit(solution)/shard_map/ppermute | solution.py:485
  176.2 12.2 %collective-permute-done.16.b = bf16[16,128,128]{2,1,0:T(8,128)(2,1)S(1)} collective-permute-done((bf16[16,128,128]{2,1,0:T(8,128)(2,1)S(1)}, bf16[16,128,128]{2,1,0:T(8,128)(2,1)S(1)}, u32[]{:S(2)}, u32[]{:S(2)}) %collective-permute-start.16) | collective-permute-done | bytes 524320 | tf_op jit(solution)/shard_map/ppermute | solution.py:485
  190.7 6.7 %all-to-all-start.1 = ((bf16[8,2,128,128]{3,2,1,0:T(8,128)(2,1)}), bf16[8,2,128,128]{3,2,1,0:T(8,128)(2,1)S(1)}, u32[]{:S(2)}, u32[]{:S(2)}) async-start(bf16[8,2,128,128]{3,2,1,0:T(8,128)(2,1)} %bitcast.9), calls=%async_computation.1 | async-start | bytes 1048576 | tf_op jit(solution)/shard_map/all_to_all | solution.py:488
  197.3 18.1 %all-to-all-done.1.xa = bf16[8,2,128,128]{3,2,1,0:T(8,128)(2,1)S(1)} async-done(((bf16[8,2,128,128]{3,2,1,0:T(8,128)(2,1)}), bf16[8,2,128,128]{3,2,1,0:T(8,128)(2,1)S(1)}, u32[]{:S(2)}, u32[]{:S(2)}) %all-to-all-start.1) | async-done | bytes 524320 | tf_op jit(solution)/shard_map/all_to_all | solution.py:488
  215.4 4.1 %project.1 = bf16[8,256,128]{2,1,0:T(8,128)(2,1)S(1)} custom-call(s32[1]{0:T(128)} %bitcast.me, s32[1]{0:T(128)} %bitcast.1.column, bf16[8,2,128,128]{3,2,1,0:T(8,128)(2,1)S(1)} %all-to-all-done.xs, bf16[8,2,128,128]{3,2,1,0:T(8,128)(2,1)S(1)} %all-to-all-done.1.xa, bf16[8,1024,128]{2,1,0:T(8,128)(2,1)S(1)} %gather_weights.1.w_mine, ...), custom_call_target="tpu_custom_call" | custom-call | flops 1000000000 | bytes 5000000 | tf_op jit(solution)/shard_map/project/pallas_call | solution.py:444
  219.5 20.3 %all_to_all.15 = bf16[8,256,128]{2,1,0:T(8,128)(2,1)S(1)} all-to-all(bf16[8,256,128]{2,1,0:T(8,128)(2,1)S(1)} %project.1), channel_id=1, replica_groups=mesh['dom'=32,'col'=8] {'col'}, dimensions={0} | all-to-all | bytes 1048576 | tf_op jit(solution)/shard_map/all_to_all | solution.py:493
  (80 shorter events, 24.6 us)
Async XLA Ops:
  4.3 24.3 %collective-permute-start.19 = (bf16[1024,128]{1,0:T(8,128)(2,1)S(1)}, bf16[1024,128]{1,0:T(8,128)(2,1)S(1)}, u32[]{:S(2)}, u32[]{:S(2)}) collective-permute-start(bf16[1024,128]{1,0:T(8,128)(2,1)S(1)} %get-tuple-element.40.refs_0_), channel_id=1, source_target_pairs={{0,1},{1,2},{2,3},{3,4},{4,5},{5,6},{6,7},{7,0},{8,9},{9,10},{10,1... | collective-permute-start | bytes 786440 | tf_op jit(solution)/shard_map/ppermute | solution.py:473
  8.9 70.4 %collective-permute-start.3 = (bf16[32,128,128]{2,1,0:T(8,128)(2,1)S(1)}, bf16[32,128,128]{2,1,0:T(8,128)(2,1)S(1)}, u32[]{:S(2)}, u32[]{:S(2)}) collective-permute-start(bf16[32,128,128]{2,1,0:T(8,128)(2,1)S(1)} %get-tuple-element.24), channel_id=1, source_target_pairs={{0,8},{8,0},{16,24},{24,16},{32,40},{40,32},{48,56},{56,48},{64,72... | collective-permute-start | bytes 3145736 | tf_op jit(solution)/shard_map/ppermute | solution.py:463
  10.0 70.6 %collective-permute-start.4 = (bf16[32,128,128]{2,1,0:T(8,128)(2,1)S(1)}, bf16[32,128,128]{2,1,0:T(8,128)(2,1)S(1)}, u32[]{:S(2)}, u32[]{:S(2)}) collective-permute-start(bf16[32,128,128]{2,1,0:T(8,128)(2,1)S(1)} %get-tuple-element.25), channel_id=1, source_target_pairs={{0,64},{8,24},{16,80},{24,40},{32,96},{40,56},{48,112},{56,8},{64,... | collective-permute-start | bytes 3145736 | tf_op jit(solution)/shard_map/ppermute | solution.py:463
  16.0 3.1 %collective-permute-start = (s32[3200]{0:T(1024)S(1)}, s32[3200]{0:T(1024)S(1)}, u32[]{:S(2)}, u32[]{:S(2)}) collective-permute-start(s32[3200]{0:T(1024)S(1)} %plan.1.refs_0_), channel_id=1, source_target_pairs={{0,16},{8,72},{16,32},{24,88},{32,48},{40,104},{48,0},{56,120},{64... | collective-permute-start | bytes 38408 | tf_op jit(solution)/shard_map/ppermute | solution.py:469
  16.4 4.1 %collective-permute-start.1 = (s32[3200]{0:T(1024)S(1)}, s32[3200]{0:T(1024)S(1)}, u32[]{:S(2)}, u32[]{:S(2)}) collective-permute-start(s32[3200]{0:T(1024)S(1)} %plan.1.refs_0_), channel_id=1, source_target_pairs={{0,32},{8,136},{16,48},{24,152},{32,0},{40,168},{48,16},{56,184},{... | collective-permute-start | bytes 38408 | tf_op jit(solution)/shard_map/ppermute | solution.py:469
  19.2 4.3 %collective-permute-start.2 = (s32[3200]{0:T(1024)S(1)}, s32[3200]{0:T(1024)S(1)}, u32[]{:S(2)}, u32[]{:S(2)}) collective-permute-start(s32[3200]{0:T(1024)S(1)} %plan.1.refs_0_), channel_id=1, source_target_pairs={{0,48},{8,200},{16,0},{24,216},{32,16},{40,232},{48,32},{56,248},{... | collective-permute-start | bytes 38408 | tf_op jit(solution)/shard_map/ppermute | solution.py:469
  20.5 15.5 %collective-permute-start.20 = (bf16[1024,128]{1,0:T(8,128)(2,1)S(1)}, bf16[1024,128]{1,0:T(8,128)(2,1)S(1)}, u32[]{:S(2)}, u32[]{:S(2)}) collective-permute-start(bf16[1024,128]{1,0:T(8,128)(2,1)S(1)} %get-tuple-element.40.refs_0_), channel_id=1, source_target_pairs={{0,2},{1,3},{2,4},{3,5},{4,6},{5,7},{6,0},{7,1},{8,10},{9,11},{10,... | collective-permute-start | bytes 786440 | tf_op jit(solution)/shard_map/ppermute | solution.py:473
  23.5 25.6 %collective-permute-start.21 = (bf16[1024,128]{1,0:T(8,128)(2,1)S(1)}, bf16[1024,128]{1,0:T(8,128)(2,1)S(1)}, u32[]{:S(2)}, u32[]{:S(2)}) collective-permute-start(bf16[1024,128]{1,0:T(8,128)(2,1)S(1)} %get-tuple-element.40.refs_0_), channel_id=1, source_target_pairs={{0,3},{1,4},{2,5},{3,6},{4,7},{5,0},{6,1},{7,2},{8,11},{9,12},{10,... | collective-permute-start | bytes 786440 | tf_op jit(solution)/shard_map/ppermute | solution.py:473
  28.5 33.6 %collective-permute-start.22 = (bf16[1024,128]{1,0:T(8,128)(2,1)S(1)}, bf16[1024,128]{1,0:T(8,128)(2,1)S(1)}, u32[]{:S(2)}, u32[]{:S(2)}) collective-permute-start(bf16[1024,128]{1,0:T(8,128)(2,1)S(1)} %get-tuple-element.40.refs_0_), channel_id=1, source_target_pairs={{0,4},{1,5},{2,6},{3,7},{4,0},{5,1},{6,2},{7,3},{8,12},{9,13},{10,... | collective-permute-start | bytes 786440 | tf_op jit(solution)/shard_map/ppermute | solution.py:473
  36.0 26.1 %collective-permute-start.23 = (bf16[1024,128]{1,0:T(8,128)(2,1)S(1)}, bf16[1024,128]{1,0:T(8,128)(2,1)S(1)}, u32[]{:S(2)}, u32[]{:S(2)}) collective-permute-start(bf16[1024,128]{1,0:T(8,128)(2,1)S(1)} %get-tuple-element.40.refs_0_), channel_id=1, source_target_pairs={{0,5},{1,6},{2,7},{3,0},{4,1},{5,2},{6,3},{7,4},{8,13},{9,14},{10,... | collective-permute-start | bytes 786440 | tf_op jit(solution)/shard_map/ppermute | solution.py:473
  49.1 21.8 %collective-permute-start.24 = (bf16[1024,128]{1,0:T(8,128)(2,1)S(1)}, bf16[1024,128]{1,0:T(8,128)(2,1)S(1)}, u32[]{:S(2)}, u32[]{:S(2)}) collective-permute-start(bf16[1024,128]{1,0:T(8,128)(2,1)S(1)} %get-tuple-element.40.refs_0_), channel_id=1, source_target_pairs={{0,6},{1,7},{2,0},{3,1},{4,2},{5,3},{6,4},{7,5},{8,14},{9,15},{10,... | collective-permute-start | bytes 786440 | tf_op jit(solution)/shard_map/ppermute | solution.py:473
  62.1 12.3 %collective-permute-start.25 = (bf16[1024,128]{1,0:T(8,128)(2,1)S(1)}, bf16[1024,128]{1,0:T(8,128)(2,1)S(1)}, u32[]{:S(2)}, u32[]{:S(2)}) collective-permute-start(bf16[1024,128]{1,0:T(8,128)(2,1)S(1)} %get-tuple-element.40.refs_0_), channel_id=1, source_target_pairs={{0,7},{1,0},{2,1},{3,2},{4,3},{5,4},{6,5},{7,6},{8,15},{9,8},{10,9... | collective-permute-start | bytes 786440 | tf_op jit(solution)/shard_map/ppermute | solution.py:473
  62.1 39.7 %collective-permute-start.5 = (bf16[32,128,128]{2,1,0:T(8,128)(2,1)S(1)}, bf16[32,128,128]{2,1,0:T(8,128)(2,1)S(1)}, u32[]{:S(2)}, u32[]{:S(2)}) collective-permute-start(bf16[32,128,128]{2,1,0:T(8,128)(2,1)S(1)} %get-tuple-element.26), channel_id=1, source_target_pairs={{0,24},{8,64},{16,40},{24,80},{32,56},{40,96},{48,8},{56,112},{64,... | collective-permute-start | bytes 3145736 | tf_op jit(solution)/shard_map/ppermute | solution.py:463
  70.8 31.0 %collective-permute-start.6 = (bf16[32,128,128]{2,1,0:T(8,128)(2,1)S(1)}, bf16[32,128,128]{2,1,0:T(8,128)(2,1)S(1)}, u32[]{:S(2)}, u32[]{:S(2)}) collective-permute-start(bf16[32,128,128]{2,1,0:T(8,128)(2,1)S(1)} %get-tuple-element.27), channel_id=1, source_target_pairs={{0,128},{8,40},{16,144},{24,56},{32,160},{40,8},{48,176},{56,24},{... | collective-permute-start | bytes 3145736 | tf_op jit(solution)/shard_map/ppermute | solution.py:463
  74.4 28.2 %collective-permute-start.7 = (bf16[32,128,128]{2,1,0:T(8,128)(2,1)S(1)}, bf16[32,128,128]{2,1,0:T(8,128)(2,1)S(1)}, u32[]{:S(2)}, u32[]{:S(2)}) collective-permute-start(bf16[32,128,128]{2,1,0:T(8,128)(2,1)S(1)} %get-tuple-element.28), channel_id=1, source_target_pairs={{0,40},{8,128},{16,56},{24,144},{32,8},{40,160},{48,24},{56,176},{... | collective-permute-start | bytes 3145736 | tf_op jit(solution)/shard_map/ppermute | solution.py:463
  79.4 37.5 %collective-permute-start.8 = (bf16[32,128,128]{2,1,0:T(8,128)(2,1)S(1)}, bf16[32,128,128]{2,1,0:T(8,128)(2,1)S(1)}, u32[]{:S(2)}, u32[]{:S(2)}) collective-permute-start(bf16[32,128,128]{2,1,0:T(8,128)(2,1)S(1)} %get-tuple-element.29), channel_id=1, source_target_pairs={{0,192},{8,56},{16,208},{24,8},{32,224},{40,24},{48,240},{56,40},{... | collective-permute-start | bytes 3145736 | tf_op jit(solution)/shard_map/ppermute | solution.py:463
  80.6 41.8 %collective-permute-start.9 = (bf16[32,128,128]{2,1,0:T(8,128)(2,1)S(1)}, bf16[32,128,128]{2,1,0:T(8,128)(2,1)S(1)}, u32[]{:S(2)}, u32[]{:S(2)}) collective-permute-start(bf16[32,128,128]{2,1,0:T(8,128)(2,1)S(1)} %get-tuple-element.30), channel_id=1, source_target_pairs={{0,56},{8,192},{16,8},{24,208},{32,24},{40,224},{48,40},{56,240},{... | collective-permute-start | bytes 3145736 | tf_op jit(solution)/shard_map/ppermute | solution.py:463
  101.8 24.7 %collective-permute-start.13 = (s32[1024,128]{1,0:T(8,128)S(1)}, s32[1024,128]{1,0:T(8,128)S(1)}, u32[]{:S(2)}, u32[]{:S(2)}) collective-permute-start(s32[1024,128]{1,0:T(8,128)S(1)} %get-tuple-element.35.refs_10_.refs_6_), channel_id=1, source_target_pairs={{0,16},{8,72},{16,32},{24,88},{32,48},{40,104},{48,0},{56,120},{64... | collective-permute-start | bytes 1572872 | tf_op jit(solution)/shard_map/ppermute | solution.py:470
  101.8 20.5 %copy-start = (bf16[32,128,128]{2,1,0:T(8,128)(2,1)}, bf16[32,128,128]{2,1,0:T(8,128)(2,1)S(1)}, u32[]{:S(2)}) copy-start(bf16[32,128,128]{2,1,0:T(8,128)(2,1)S(1)} %collective-permute-done.6.refs_8_.refs_4_) | copy-start | bytes 3145732
  101.8 29.6 %collective-permute-start.14 = (s32[1024,128]{1,0:T(8,128)S(1)}, s32[1024,128]{1,0:T(8,128)S(1)}, u32[]{:S(2)}, u32[]{:S(2)}) collective-permute-start(s32[1024,128]{1,0:T(8,128)S(1)} %get-tuple-element.35.refs_10_.refs_6_), channel_id=1, source_target_pairs={{0,32},{8,136},{16,48},{24,152},{32,0},{40,168},{48,16},{56,184},{... | collective-permute-start | bytes 1572872 | tf_op jit(solution)/shard_map/ppermute | solution.py:470
  102.6 19.8 %copy-start.2 = (bf16[32,128,128]{2,1,0:T(8,128)(2,1)}, bf16[32,128,128]{2,1,0:T(8,128)(2,1)S(1)}, u32[]{:S(2)}) copy-start(bf16[32,128,128]{2,1,0:T(8,128)(2,1)S(1)} %collective-permute-done.7.refs_9_.refs_5_) | copy-start | bytes 3145732
  102.6 30.4 %collective-permute-start.15 = (s32[1024,128]{1,0:T(8,128)S(1)}, s32[1024,128]{1,0:T(8,128)S(1)}, u32[]{:S(2)}, u32[]{:S(2)}) collective-permute-start(s32[1024,128]{1,0:T(8,128)S(1)} %get-tuple-element.35.refs_10_.refs_6_), channel_id=1, source_target_pairs={{0,48},{8,200},{16,0},{24,216},{32,16},{40,232},{48,32},{56,248},{... | collective-permute-start | bytes 1572872 | tf_op jit(solution)/shard_map/ppermute | solution.py:470
  116.9 80.5 %collective-permute-start.26 = (bf16[8,1024,128]{2,1,0:T(8,128)(2,1)S(1)}, bf16[8,1024,128]{2,1,0:T(8,128)(2,1)}, u32[]{:S(2)}, u32[]{:S(2)}) collective-permute-start(bf16[8,1024,128]{2,1,0:T(8,128)(2,1)S(1)} %gather_weights.1.w_mine), channel_id=1, source_target_pairs={{0,8},{8,0},{16,24},{24,16},{32,40},{40,32},{48,56},{56,48},{64,72... | collective-permute-start | bytes 6291464 | tf_op jit(solution)/shard_map/ppermute | solution.py:475
  125.9 22.8 %collective-permute-start.10 = (bf16[16,128,128]{2,1,0:T(8,128)(2,1)S(1)}, bf16[16,128,128]{2,1,0:T(8,128)(2,1)S(1)}, u32[]{:S(2)}, u32[]{:S(2)}) collective-permute-start(bf16[16,128,128]{2,1,0:T(8,128)(2,1)S(1)} %get-tuple-element.32), channel_id=1, source_target_pairs={{0,48},{8,200},{16,0},{24,216},{32,16},{40,232},{48,32},{56,248},{... | collective-permute-start | bytes 1572872 | tf_op jit(solution)/shard_map/ppermute | solution.py:480
  126.6 20.2 %copy-start.7 = (s32[1024,128]{1,0:T(8,128)}, s32[1024,128]{1,0:T(8,128)S(1)}, u32[]{:S(2)}) copy-start(s32[1024,128]{1,0:T(8,128)S(1)} %collective-permute-done.13.refs_11_.refs_7_) | copy-start | bytes 1572868
  126.6 22.2 %collective-permute-start.11 = (bf16[16,128,128]{2,1,0:T(8,128)(2,1)S(1)}, bf16[16,128,128]{2,1,0:T(8,128)(2,1)S(1)}, u32[]{:S(2)}, u32[]{:S(2)}) collective-permute-start(bf16[16,128,128]{2,1,0:T(8,128)(2,1)S(1)} %get-tuple-element.33), channel_id=1, source_target_pairs={{0,32},{8,136},{16,48},{24,152},{32,0},{40,168},{48,16},{56,184},{... | collective-permute-start | bytes 1572872 | tf_op jit(solution)/shard_map/ppermute | solution.py:480
  131.4 17.3 %collective-permute-start.12 = (bf16[16,128,128]{2,1,0:T(8,128)(2,1)S(1)}, bf16[16,128,128]{2,1,0:T(8,128)(2,1)S(1)}, u32[]{:S(2)}, u32[]{:S(2)}) collective-permute-start(bf16[16,128,128]{2,1,0:T(8,128)(2,1)S(1)} %get-tuple-element.34), channel_id=1, source_target_pairs={{0,16},{8,72},{16,32},{24,88},{32,48},{40,104},{48,0},{56,120},{64... | collective-permute-start | bytes 1572872 | tf_op jit(solution)/shard_map/ppermute | solution.py:480
  149.8 40.9 %all-to-all-start = ((bf16[8,2,128,128]{3,2,1,0:T(8,128)(2,1)}), bf16[8,2,128,128]{3,2,1,0:T(8,128)(2,1)S(1)}, u32[]{:S(2)}, u32[]{:S(2)}) async-start(bf16[8,2,128,128]{3,2,1,0:T(8,128)(2,1)} %bitcast.5), calls=%async_computation | async-start | bytes 1048576 | tf_op jit(solution)/shard_map/all_to_all | solution.py:488
  173.5 14.9 %collective-permute-start.16 = (bf16[16,128,128]{2,1,0:T(8,128)(2,1)S(1)}, bf16[16,128,128]{2,1,0:T(8,128)(2,1)S(1)}, u32[]{:S(2)}, u32[]{:S(2)}) collective-permute-start(bf16[16,128,128]{2,1,0:T(8,128)(2,1)S(1)} %get-tuple-element.37), channel_id=1, source_target_pairs={{0,48},{8,200},{16,0},{24,216},{32,16},{40,232},{48,32},{56,248},{... | collective-permute-start | bytes 1572872 | tf_op jit(solution)/shard_map/ppermute | solution.py:485
  173.6 14.8 %collective-permute-start.17 = (bf16[16,128,128]{2,1,0:T(8,128)(2,1)S(1)}, bf16[16,128,128]{2,1,0:T(8,128)(2,1)S(1)}, u32[]{:S(2)}, u32[]{:S(2)}) collective-permute-start(bf16[16,128,128]{2,1,0:T(8,128)(2,1)S(1)} %get-tuple-element.38), channel_id=1, source_target_pairs={{0,32},{8,136},{16,48},{24,152},{32,0},{40,168},{48,16},{56,184},{... | collective-permute-start | bytes 1572872 | tf_op jit(solution)/shard_map/ppermute | solution.py:485
  173.7 15.4 %collective-permute-start.18 = (bf16[16,128,128]{2,1,0:T(8,128)(2,1)S(1)}, bf16[16,128,128]{2,1,0:T(8,128)(2,1)S(1)}, u32[]{:S(2)}, u32[]{:S(2)}) collective-permute-start(bf16[16,128,128]{2,1,0:T(8,128)(2,1)S(1)} %get-tuple-element.39), channel_id=1, source_target_pairs={{0,16},{8,72},{16,32},{24,88},{32,48},{40,104},{48,0},{56,120},{64... | collective-permute-start | bytes 1572872 | tf_op jit(solution)/shard_map/ppermute | solution.py:485
  190.7 24.7 %all-to-all-start.1 = ((bf16[8,2,128,128]{3,2,1,0:T(8,128)(2,1)}), bf16[8,2,128,128]{3,2,1,0:T(8,128)(2,1)S(1)}, u32[]{:S(2)}, u32[]{:S(2)}) async-start(bf16[8,2,128,128]{3,2,1,0:T(8,128)(2,1)} %bitcast.9), calls=%async_computation.1 | async-start | bytes 1048576 | tf_op jit(solution)/shard_map/all_to_all | solution.py:488
  (18 other events, 72.4 us)

commit v3 on v2

--- a/solution.py
+++ b/solution.py
@@ -27,7 +27,13 @@
 VMEM = pl.BlockSpec(memory_space=pltpu.VMEM)
 SMEM = pl.BlockSpec(memory_space=pltpu.SMEM)
 ANY = pl.BlockSpec(memory_space=pl.ANY)
-LIMIT = pltpu.CompilerParams(vmem_limit_bytes=24 * 2**20)
+
+
+def grant(mib):
+    return pltpu.CompilerParams(vmem_limit_bytes=mib * 2**20)
+
+
+LIMIT = grant(8)
 
 
 def dom_of(y, x, core):
@@ -99,7 +105,7 @@
             pltpu.SemaphoreType.DMA((N_SRC,)),
         ],
         cost_estimate=pl.CostEstimate(flops=10**9, bytes_accessed=10**7, transcendentals=0),
-        compiler_params=LIMIT,
+        compiler_params=grant(14),
         name="pack",
     )(me, requests, features)
 
@@ -335,7 +341,7 @@
             pltpu.SemaphoreType.DMA,
         ],
         cost_estimate=pl.CostEstimate(flops=10**10, bytes_accessed=2 * 10**7, transcendentals=0),
-        compiler_params=LIMIT,
+        compiler_params=grant(15),
         name="early",
     )(*lists, *sources, *nbrs)
 
@@ -372,7 +378,7 @@
             pltpu.SemaphoreType.DMA,
         ],
         cost_estimate=pl.CostEstimate(flops=10**10, bytes_accessed=2 * 10**7, transcendentals=0),
-        compiler_params=LIMIT,
+        compiler_params=grant(12),
         name="late",
     )(*lists, *sources, *nbrs, early)
 

time: 241 us -> 241 us (level)
  no operation moved by 1% of the time
where the time goes in v3:
time: 241 us
  waiting for transfers between devices  97.7 us (41%)
  starting transfers between devices  69 us (29%)
  Pallas kernels  38.9 us (16%)
  blocking collectives  20.3 us (8%)
  local copies, waits for them, and re-layouts  14.6 us (6%)
    ppermute x7, waiting for transfers between devices, body(): sources.append(lax.ppermute(packed[q], 'dom', meet_pairs(q // 2, q % 2)))  34.7 us
    ppermute x7, waiting for transfers between devices, body(): lax.ppermute(w_t, 'col', [(i, (i + k) % n_col) for i in range(n_col)])  29.6 us
    all_to_all x1, blocking collectives, body(): return lax.all_to_all(y, 'col', 0, 0, tiled=True).reshape(-1, ROWS)  20.3 us
    all_to_all x2, waiting for transfers between devices, to_rows(): lax.all_to_all(x.reshape(n_col, DST // n_col, ROWS, ROWS), 'col', 0, 0, t...  18.1 us
    ppermute x7, starting transfers between devices, body(): lax.ppermute(w_t, 'col', [(i, (i + k) % n_col) for i in range(n_col)])  17.8 us
    ppermute x7, starting transfers between devices, body(): sources.append(lax.ppermute(packed[q], 'dom', meet_pairs(q // 2, q % 2)))  16.7 us
    all_to_all x2, starting transfers between devices, to_rows(): lax.all_to_all(x.reshape(n_col, DST // n_col, ROWS, ROWS), 'col', 0, 0, t...  15.9 us
    unnamed x43, local copies, waits for them, and re-layouts  14.6 us
  transfers between devices with their start and end apart: 29, of which 14 were waited for; matrix products, arithmetic and copies ran while one was open for 0% of the time, Pallas kernels for 14%

profile of v3, /device:TPU:25, one launch (start us, length us, event | category | flops | bytes accessed | tf_op | source)
XLA Modules:
  0.0 240.7 jit_solution(13897058051619502559)
XLA Ops:
  4.3 1.7 collective-permute-start.19
  6.0 2.9 %pack.1 = (bf16[32,128,128]{2,1,0:T(8,128)(2,1)S(1)}, bf16[32,128,128]{2,1,0:T(8,128)(2,1)S(1)}, bf16[32,128,128]{2,1,0:T(8,128)(2,1)S(1)}, bf16[32,128,128]{2,1...) custom-call(s32[1]{0:T(128)} %bitcast.me, ...), custom_call_target="tpu_custom_call" | custom-call | flops 1000000000 | bytes 10000000 | tf_op jit(solution)/shard_map/pack/pallas_call | solution.py:97
  11.2 4.8 %plan.1.refs_0_ = s32[3200]{0:T(1024)S(1)} custom-call(s32[1]{0:T(128)} %bitcast.me, s32[32]{0:T(128)S(1)} %bitcast.11, s32[16,32]{1,0:T(8,128)S(1)} %copy-done.15, s32[16]{0:T(128)S(1)} %copy-done.18), custom_call_target="tpu_custom_call" | custom-call | flops 2000000000 | bytes 1000000 | tf_op jit(solution)/shard_map/plan/pallas_call | solution.py:196
  16.4 2.3 collective-permute-start.1
  20.5 3.0 %collective-permute-start.20 = (bf16[1024,128]{1,0:T(8,128)(2,1)S(1)}, bf16[1024,128]{1,0:T(8,128)(2,1)S(1)}, u32[]{:S(2)}, u32[]{:S(2)}) collective-permute-start(bf16[1024,128]{1,0:T(8,128)(2,1)S(1)} %get-tuple-element.40.refs_0_), channel_id=1, source_target_pairs={{0,2},{1,3},{2,4},{3,5},{4,6},{5,7},{6,0},{7,1},{8,10},{9,11},{10,... | collective-permute-start | bytes 786440 | tf_op jit(solution)/shard_map/ppermute | solution.py:479
  23.5 5.1 %collective-permute-start.21 = (bf16[1024,128]{1,0:T(8,128)(2,1)S(1)}, bf16[1024,128]{1,0:T(8,128)(2,1)S(1)}, u32[]{:S(2)}, u32[]{:S(2)}) collective-permute-start(bf16[1024,128]{1,0:T(8,128)(2,1)S(1)} %get-tuple-element.40.refs_0_), channel_id=1, source_target_pairs={{0,3},{1,4},{2,5},{3,6},{4,7},{5,0},{6,1},{7,2},{8,11},{9,12},{10,... | collective-permute-start | bytes 786440 | tf_op jit(solution)/shard_map/ppermute | solution.py:479
  29.6 6.3 %collective-permute-done.20.refs_2_ = bf16[1024,128]{1,0:T(8,128)(2,1)S(1)} collective-permute-done((bf16[1024,128]{1,0:T(8,128)(2,1)S(1)}, bf16[1024,128]{1,0:T(8,128)(2,1)S(1)}, u32[]{:S(2)}, u32[]{:S(2)}) %collective-permute-start.20) | collective-permute-done | bytes 262176 | tf_op jit(solution)/shard_map/ppermute | solution.py:479
  36.0 4.6 %collective-permute-start.23 = (bf16[1024,128]{1,0:T(8,128)(2,1)S(1)}, bf16[1024,128]{1,0:T(8,128)(2,1)S(1)}, u32[]{:S(2)}, u32[]{:S(2)}) collective-permute-start(bf16[1024,128]{1,0:T(8,128)(2,1)S(1)} %get-tuple-element.40.refs_0_), channel_id=1, source_target_pairs={{0,5},{1,6},{2,7},{3,0},{4,1},{5,2},{6,3},{7,4},{8,13},{9,14},{10,... | collective-permute-start | bytes 786440 | tf_op jit(solution)/shard_map/ppermute | solution.py:479
  40.5 8.5 %collective-permute-done.21.refs_3_ = bf16[1024,128]{1,0:T(8,128)(2,1)S(1)} collective-permute-done((bf16[1024,128]{1,0:T(8,128)(2,1)S(1)}, bf16[1024,128]{1,0:T(8,128)(2,1)S(1)}, u32[]{:S(2)}, u32[]{:S(2)}) %collective-permute-start.21) | collective-permute-done | bytes 262176 | tf_op jit(solution)/shard_map/ppermute | solution.py:479
  49.1 2.3 collective-permute-start.24
  51.4 10.7 %collective-permute-done.22.refs_4_ = bf16[1024,128]{1,0:T(8,128)(2,1)S(1)} collective-permute-done((bf16[1024,128]{1,0:T(8,128)(2,1)S(1)}, bf16[1024,128]{1,0:T(8,128)(2,1)S(1)}, u32[]{:S(2)}, u32[]{:S(2)}) %collective-permute-start.22) | collective-permute-done | bytes 262176 | tf_op jit(solution)/shard_map/ppermute | solution.py:479
  62.1 5.5 %collective-permute-start.5 = (bf16[32,128,128]{2,1,0:T(8,128)(2,1)S(1)}, bf16[32,128,128]{2,1,0:T(8,128)(2,1)S(1)}, u32[]{:S(2)}, u32[]{:S(2)}) collective-permute-start(bf16[32,128,128]{2,1,0:T(8,128)(2,1)S(1)} %get-tuple-element.26), channel_id=1, source_target_pairs={{0,24},{8,64},{16,40},{24,80},{32,56},{40,96},{48,8},{56,112},{64,... | collective-permute-start | bytes 3145736 | tf_op jit(solution)/shard_map/ppermute | solution.py:469
  67.6 3.2 %collective-permute-done.24.refs_6_ = bf16[1024,128]{1,0:T(8,128)(2,1)S(1)} collective-permute-done((bf16[1024,128]{1,0:T(8,128)(2,1)S(1)}, bf16[1024,128]{1,0:T(8,128)(2,1)S(1)}, u32[]{:S(2)}, u32[]{:S(2)}) %collective-permute-start.24) | collective-permute-done | bytes 262176 | tf_op jit(solution)/shard_map/ppermute | solution.py:479
  70.8 2.7 %collective-permute-start.6 = (bf16[32,128,128]{2,1,0:T(8,128)(2,1)S(1)}, bf16[32,128,128]{2,1,0:T(8,128)(2,1)S(1)}, u32[]{:S(2)}, u32[]{:S(2)}) collective-permute-start(bf16[32,128,128]{2,1,0:T(8,128)(2,1)S(1)} %get-tuple-element.27), channel_id=1, source_target_pairs={{0,128},{8,40},{16,144},{24,56},{32,160},{40,8},{48,176},{56,24},{... | collective-permute-start | bytes 3145736 | tf_op jit(solution)/shard_map/ppermute | solution.py:469
  74.4 5.0 %collective-permute-start.7 = (bf16[32,128,128]{2,1,0:T(8,128)(2,1)S(1)}, bf16[32,128,128]{2,1,0:T(8,128)(2,1)S(1)}, u32[]{:S(2)}, u32[]{:S(2)}) collective-permute-start(bf16[32,128,128]{2,1,0:T(8,128)(2,1)S(1)} %get-tuple-element.28), channel_id=1, source_target_pairs={{0,40},{8,128},{16,56},{24,144},{32,8},{40,160},{48,24},{56,176},{... | collective-permute-start | bytes 3145736 | tf_op jit(solution)/shard_map/ppermute | solution.py:469
  80.6 21.2 %collective-permute-done.5.refs_7_ = bf16[32,128,128]{2,1,0:T(8,128)(2,1)S(1)} collective-permute-done((bf16[32,128,128]{2,1,0:T(8,128)(2,1)S(1)}, bf16[32,128,128]{2,1,0:T(8,128)(2,1)S(1)}, u32[]{:S(2)}, u32[]{:S(2)}) %collective-permute-start.5) | collective-permute-done | bytes 1048608 | tf_op jit(solution)/shard_map/ppermute | solution.py:469
  104.1 12.8 %collective-permute-done.8.refs_10_.refs_8_ = bf16[32,128,128]{2,1,0:T(8,128)(2,1)S(1)} collective-permute-done((bf16[32,128,128]{2,1,0:T(8,128)(2,1)S(1)}, bf16[32,128,128]{2,1,0:T(8,128)(2,1)S(1)}, u32[]{:S(2)}, u32[]{:S(2)}) %collective-permute-start.8) | collective-permute-done | bytes 1048608 | tf_op jit(solution)/shard_map/ppermute | solution.py:469
  116.9 5.5 %collective-permute-start.26 = (bf16[8,1024,128]{2,1,0:T(8,128)(2,1)S(1)}, bf16[8,1024,128]{2,1,0:T(8,128)(2,1)}, u32[]{:S(2)}, u32[]{:S(2)}) collective-permute-start(bf16[8,1024,128]{2,1,0:T(8,128)(2,1)S(1)} %gather_weights.1.w_mine), channel_id=1, source_target_pairs={{0,8},{8,0},{16,24},{24,16},{32,40},{40,32},{48,56},{56,48},{64,72... | collective-permute-start | bytes 6291464 | tf_op jit(solution)/shard_map/ppermute | solution.py:481
  122.4 3.6 %own_rows.1 = (bf16[16,128,128]{2,1,0:T(8,128)(2,1)S(1)}, bf16[16,128,128]{2,1,0:T(8,128)(2,1)S(1)}, bf16[16,128,128]{2,1,0:T(8,128)(2,1)S(1)}, bf16[16,128,128]{2,1,0:T(8,128)(2,1)S(1)}) custom-call(s32[3200]{0:T(1024)S(1)} %plan.1.refs_0_, s32[3200]{0:T(1024)S(1)} %collective-permute-done.refs_1_, s32[3200]{0:T(1024)S(1)} %collective-permute-done.1.refs_2_, ...), custom_call_target="tpu_custom_call" | custom-call | flops 1000000000 | bytes 10000000 | tf_op jit(solution)/shard_map/own_rows/pallas_call | solution.py:255
  126.6 4.9 %collective-permute-start.11 = (bf16[16,128,128]{2,1,0:T(8,128)(2,1)S(1)}, bf16[16,128,128]{2,1,0:T(8,128)(2,1)S(1)}, u32[]{:S(2)}, u32[]{:S(2)}) collective-permute-start(bf16[16,128,128]{2,1,0:T(8,128)(2,1)S(1)} %get-tuple-element.33), channel_id=1, source_target_pairs={{0,32},{8,136},{16,48},{24,152},{32,0},{40,168},{48,16},{56,184},{... | collective-permute-start | bytes 1572872 | tf_op jit(solution)/shard_map/ppermute | solution.py:486
  131.4 1.5 collective-permute-done.15.refs_13_.refs_9_
  133.0 13.7 %early.1.refs_10_ = f32[64,128,128]{2,1,0:T(8,128)S(1)} custom-call(s32[3200]{0:T(1024)S(1)} %plan.1.refs_0_, s32[3200]{0:T(1024)S(1)} %collective-permute-done.refs_1_, s32[3200]{0:T(1024)S(1)} %collective-permute-done.1.refs_2_, s32[3200]{0:T(1024)S(1)} %collective-permute-done.2.refs_3_, bf16[32,128,128]{2,1,0:T(8,128)(2,1)S(1)} %get-tuple-element.23.refs_4_, ...), custom_call_target="tpu_custom_call" | custom-call | flops 10000000000 | bytes 20000000 | tf_op jit(solution)/shard_map/early/pallas_call | solution.py:332
  146.8 2.0 copy-done.19
  149.8 9.2 %all-to-all-start = ((bf16[8,2,128,128]{3,2,1,0:T(8,128)(2,1)}), bf16[8,2,128,128]{3,2,1,0:T(8,128)(2,1)S(1)}, u32[]{:S(2)}, u32[]{:S(2)}) async-start(bf16[8,2,128,128]{3,2,1,0:T(8,128)(2,1)} %bitcast.5), calls=%async_computation | async-start | bytes 1048576 | tf_op jit(solution)/shard_map/all_to_all | solution.py:494
  164.6 2.2 copy-done.20
  166.8 6.7 %late.1 = (bf16[16,128,128]{2,1,0:T(8,128)(2,1)S(1)}, bf16[16,128,128]{2,1,0:T(8,128)(2,1)S(1)}, bf16[16,128,128]{2,1,0:T(8,128)(2,1)S(1)}, bf16[16,128,128]{2,1,0:T(8,128)(2,1)S(1)}) custom-call(s32[3200]{0:T(1024)S(1)} %plan.1.refs_0_, s32[3200]{0:T(1024)S(1)} %collective-permute-done.refs_1_, s32[3200]{0:T(1024)S(1)} %collective-permute-done.1.refs_2_, ...), custom_call_target="tpu_custom_call" | custom-call | flops 10000000000 | bytes 20000000 | tf_op jit(solution)/shard_map/late/pallas_call | solution.py:369
  173.7 2.6 %collective-permute-start.18 = (bf16[16,128,128]{2,1,0:T(8,128)(2,1)S(1)}, bf16[16,128,128]{2,1,0:T(8,128)(2,1)S(1)}, u32[]{:S(2)}, u32[]{:S(2)}) collective-permute-start(bf16[16,128,128]{2,1,0:T(8,128)(2,1)S(1)} %get-tuple-element.39), channel_id=1, source_target_pairs={{0,16},{8,72},{16,32},{24,88},{32,48},{40,104},{48,0},{56,120},{64... | collective-permute-start | bytes 1572872 | tf_op jit(solution)/shard_map/ppermute | solution.py:491
  176.2 12.2 %collective-permute-done.16.b = bf16[16,128,128]{2,1,0:T(8,128)(2,1)S(1)} collective-permute-done((bf16[16,128,128]{2,1,0:T(8,128)(2,1)S(1)}, bf16[16,128,128]{2,1,0:T(8,128)(2,1)S(1)}, u32[]{:S(2)}, u32[]{:S(2)}) %collective-permute-start.16) | collective-permute-done | bytes 524320 | tf_op jit(solution)/shard_map/ppermute | solution.py:491
  190.7 6.7 %all-to-all-start.1 = ((bf16[8,2,128,128]{3,2,1,0:T(8,128)(2,1)}), bf16[8,2,128,128]{3,2,1,0:T(8,128)(2,1)S(1)}, u32[]{:S(2)}, u32[]{:S(2)}) async-start(bf16[8,2,128,128]{3,2,1,0:T(8,128)(2,1)} %bitcast.9), calls=%async_computation.1 | async-start | bytes 1048576 | tf_op jit(solution)/shard_map/all_to_all | solution.py:494
  197.4 18.1 %all-to-all-done.1.xa = bf16[8,2,128,128]{3,2,1,0:T(8,128)(2,1)S(1)} async-done(((bf16[8,2,128,128]{3,2,1,0:T(8,128)(2,1)}), bf16[8,2,128,128]{3,2,1,0:T(8,128)(2,1)S(1)}, u32[]{:S(2)}, u32[]{:S(2)}) %all-to-all-start.1) | async-done | bytes 524320 | tf_op jit(solution)/shard_map/all_to_all | solution.py:494
  215.4 4.1 %project.1 = bf16[8,256,128]{2,1,0:T(8,128)(2,1)S(1)} custom-call(s32[1]{0:T(128)} %bitcast.me, s32[1]{0:T(128)} %bitcast.1.column, bf16[8,2,128,128]{3,2,1,0:T(8,128)(2,1)S(1)} %all-to-all-done.xs, bf16[8,2,128,128]{3,2,1,0:T(8,128)(2,1)S(1)} %all-to-all-done.1.xa, bf16[8,1024,128]{2,1,0:T(8,128)(2,1)S(1)} %gather_weights.1.w_mine, ...), custom_call_target="tpu_custom_call" | custom-call | flops 1000000000 | bytes 5000000 | tf_op jit(solution)/shard_map/project/pallas_call | solution.py:450
  219.5 20.3 %all_to_all.15 = bf16[8,256,128]{2,1,0:T(8,128)(2,1)S(1)} all-to-all(bf16[8,256,128]{2,1,0:T(8,128)(2,1)S(1)} %project.1), channel_id=1, replica_groups=mesh['dom'=32,'col'=8] {'col'}, dimensions={0} | all-to-all | bytes 1048576 | tf_op jit(solution)/shard_map/all_to_all | solution.py:499
  (80 shorter events, 24.6 us)
Async XLA Ops:
  4.3 24.3 %collective-permute-start.19 = (bf16[1024,128]{1,0:T(8,128)(2,1)S(1)}, bf16[1024,128]{1,0:T(8,128)(2,1)S(1)}, u32[]{:S(2)}, u32[]{:S(2)}) collective-permute-start(bf16[1024,128]{1,0:T(8,128)(2,1)S(1)} %get-tuple-element.40.refs_0_), channel_id=1, source_target_pairs={{0,1},{1,2},{2,3},{3,4},{4,5},{5,6},{6,7},{7,0},{8,9},{9,10},{10,1... | collective-permute-start | bytes 786440 | tf_op jit(solution)/shard_map/ppermute | solution.py:479
  8.9 70.4 %collective-permute-start.3 = (bf16[32,128,128]{2,1,0:T(8,128)(2,1)S(1)}, bf16[32,128,128]{2,1,0:T(8,128)(2,1)S(1)}, u32[]{:S(2)}, u32[]{:S(2)}) collective-permute-start(bf16[32,128,128]{2,1,0:T(8,128)(2,1)S(1)} %get-tuple-element.24), channel_id=1, source_target_pairs={{0,8},{8,0},{16,24},{24,16},{32,40},{40,32},{48,56},{56,48},{64,72... | collective-permute-start | bytes 3145736 | tf_op jit(solution)/shard_map/ppermute | solution.py:469
  10.0 70.6 %collective-permute-start.4 = (bf16[32,128,128]{2,1,0:T(8,128)(2,1)S(1)}, bf16[32,128,128]{2,1,0:T(8,128)(2,1)S(1)}, u32[]{:S(2)}, u32[]{:S(2)}) collective-permute-start(bf16[32,128,128]{2,1,0:T(8,128)(2,1)S(1)} %get-tuple-element.25), channel_id=1, source_target_pairs={{0,64},{8,24},{16,80},{24,40},{32,96},{40,56},{48,112},{56,8},{64,... | collective-permute-start | bytes 3145736 | tf_op jit(solution)/shard_map/ppermute | solution.py:469
  16.0 3.1 %collective-permute-start = (s32[3200]{0:T(1024)S(1)}, s32[3200]{0:T(1024)S(1)}, u32[]{:S(2)}, u32[]{:S(2)}) collective-permute-start(s32[3200]{0:T(1024)S(1)} %plan.1.refs_0_), channel_id=1, source_target_pairs={{0,16},{8,72},{16,32},{24,88},{32,48},{40,104},{48,0},{56,120},{64... | collective-permute-start | bytes 38408 | tf_op jit(solution)/shard_map/ppermute | solution.py:475
  16.4 4.1 %collective-permute-start.1 = (s32[3200]{0:T(1024)S(1)}, s32[3200]{0:T(1024)S(1)}, u32[]{:S(2)}, u32[]{:S(2)}) collective-permute-start(s32[3200]{0:T(1024)S(1)} %plan.1.refs_0_), channel_id=1, source_target_pairs={{0,32},{8,136},{16,48},{24,152},{32,0},{40,168},{48,16},{56,184},{... | collective-permute-start | bytes 38408 | tf_op jit(solution)/shard_map/ppermute | solution.py:475
  19.2 4.3 %collective-permute-start.2 = (s32[3200]{0:T(1024)S(1)}, s32[3200]{0:T(1024)S(1)}, u32[]{:S(2)}, u32[]{:S(2)}) collective-permute-start(s32[3200]{0:T(1024)S(1)} %plan.1.refs_0_), channel_id=1, source_target_pairs={{0,48},{8,200},{16,0},{24,216},{32,16},{40,232},{48,32},{56,248},{... | collective-permute-start | bytes 38408 | tf_op jit(solution)/shard_map/ppermute | solution.py:475
  20.5 15.5 %collective-permute-start.20 = (bf16[1024,128]{1,0:T(8,128)(2,1)S(1)}, bf16[1024,128]{1,0:T(8,128)(2,1)S(1)}, u32[]{:S(2)}, u32[]{:S(2)}) collective-permute-start(bf16[1024,128]{1,0:T(8,128)(2,1)S(1)} %get-tuple-element.40.refs_0_), channel_id=1, source_target_pairs={{0,2},{1,3},{2,4},{3,5},{4,6},{5,7},{6,0},{7,1},{8,10},{9,11},{10,... | collective-permute-start | bytes 786440 | tf_op jit(solution)/shard_map/ppermute | solution.py:479
  23.5 25.6 %collective-permute-start.21 = (bf16[1024,128]{1,0:T(8,128)(2,1)S(1)}, bf16[1024,128]{1,0:T(8,128)(2,1)S(1)}, u32[]{:S(2)}, u32[]{:S(2)}) collective-permute-start(bf16[1024,128]{1,0:T(8,128)(2,1)S(1)} %get-tuple-element.40.refs_0_), channel_id=1, source_target_pairs={{0,3},{1,4},{2,5},{3,6},{4,7},{5,0},{6,1},{7,2},{8,11},{9,12},{10,... | collective-permute-start | bytes 786440 | tf_op jit(solution)/shard_map/ppermute | solution.py:479
  28.5 33.6 %collective-permute-start.22 = (bf16[1024,128]{1,0:T(8,128)(2,1)S(1)}, bf16[1024,128]{1,0:T(8,128)(2,1)S(1)}, u32[]{:S(2)}, u32[]{:S(2)}) collective-permute-start(bf16[1024,128]{1,0:T(8,128)(2,1)S(1)} %get-tuple-element.40.refs_0_), channel_id=1, source_target_pairs={{0,4},{1,5},{2,6},{3,7},{4,0},{5,1},{6,2},{7,3},{8,12},{9,13},{10,... | collective-permute-start | bytes 786440 | tf_op jit(solution)/shard_map/ppermute | solution.py:479
  36.0 26.1 %collective-permute-start.23 = (bf16[1024,128]{1,0:T(8,128)(2,1)S(1)}, bf16[1024,128]{1,0:T(8,128)(2,1)S(1)}, u32[]{:S(2)}, u32[]{:S(2)}) collective-permute-start(bf16[1024,128]{1,0:T(8,128)(2,1)S(1)} %get-tuple-element.40.refs_0_), channel_id=1, source_target_pairs={{0,5},{1,6},{2,7},{3,0},{4,1},{5,2},{6,3},{7,4},{8,13},{9,14},{10,... | collective-permute-start | bytes 786440 | tf_op jit(solution)/shard_map/ppermute | solution.py:479
  49.1 21.8 %collective-permute-start.24 = (bf16[1024,128]{1,0:T(8,128)(2,1)S(1)}, bf16[1024,128]{1,0:T(8,128)(2,1)S(1)}, u32[]{:S(2)}, u32[]{:S(2)}) collective-permute-start(bf16[1024,128]{1,0:T(8,128)(2,1)S(1)} %get-tuple-element.40.refs_0_), channel_id=1, source_target_pairs={{0,6},{1,7},{2,0},{3,1},{4,2},{5,3},{6,4},{7,5},{8,14},{9,15},{10,... | collective-permute-start | bytes 786440 | tf_op jit(solution)/shard_map/ppermute | solution.py:479
  62.1 12.3 %collective-permute-start.25 = (bf16[1024,128]{1,0:T(8,128)(2,1)S(1)}, bf16[1024,128]{1,0:T(8,128)(2,1)S(1)}, u32[]{:S(2)}, u32[]{:S(2)}) collective-permute-start(bf16[1024,128]{1,0:T(8,128)(2,1)S(1)} %get-tuple-element.40.refs_0_), channel_id=1, source_target_pairs={{0,7},{1,0},{2,1},{3,2},{4,3},{5,4},{6,5},{7,6},{8,15},{9,8},{10,9... | collective-permute-start | bytes 786440 | tf_op jit(solution)/shard_map/ppermute | solution.py:479
  62.1 39.7 %collective-permute-start.5 = (bf16[32,128,128]{2,1,0:T(8,128)(2,1)S(1)}, bf16[32,128,128]{2,1,0:T(8,128)(2,1)S(1)}, u32[]{:S(2)}, u32[]{:S(2)}) collective-permute-start(bf16[32,128,128]{2,1,0:T(8,128)(2,1)S(1)} %get-tuple-element.26), channel_id=1, source_target_pairs={{0,24},{8,64},{16,40},{24,80},{32,56},{40,96},{48,8},{56,112},{64,... | collective-permute-start | bytes 3145736 | tf_op jit(solution)/shard_map/ppermute | solution.py:469
  70.8 31.0 %collective-permute-start.6 = (bf16[32,128,128]{2,1,0:T(8,128)(2,1)S(1)}, bf16[32,128,128]{2,1,0:T(8,128)(2,1)S(1)}, u32[]{:S(2)}, u32[]{:S(2)}) collective-permute-start(bf16[32,128,128]{2,1,0:T(8,128)(2,1)S(1)} %get-tuple-element.27), channel_id=1, source_target_pairs={{0,128},{8,40},{16,144},{24,56},{32,160},{40,8},{48,176},{56,24},{... | collective-permute-start | bytes 3145736 | tf_op jit(solution)/shard_map/ppermute | solution.py:469
  74.4 28.2 %collective-permute-start.7 = (bf16[32,128,128]{2,1,0:T(8,128)(2,1)S(1)}, bf16[32,128,128]{2,1,0:T(8,128)(2,1)S(1)}, u32[]{:S(2)}, u32[]{:S(2)}) collective-permute-start(bf16[32,128,128]{2,1,0:T(8,128)(2,1)S(1)} %get-tuple-element.28), channel_id=1, source_target_pairs={{0,40},{8,128},{16,56},{24,144},{32,8},{40,160},{48,24},{56,176},{... | collective-permute-start | bytes 3145736 | tf_op jit(solution)/shard_map/ppermute | solution.py:469
  79.4 37.5 %collective-permute-start.8 = (bf16[32,128,128]{2,1,0:T(8,128)(2,1)S(1)}, bf16[32,128,128]{2,1,0:T(8,128)(2,1)S(1)}, u32[]{:S(2)}, u32[]{:S(2)}) collective-permute-start(bf16[32,128,128]{2,1,0:T(8,128)(2,1)S(1)} %get-tuple-element.29), channel_id=1, source_target_pairs={{0,192},{8,56},{16,208},{24,8},{32,224},{40,24},{48,240},{56,40},{... | collective-permute-start | bytes 3145736 | tf_op jit(solution)/shard_map/ppermute | solution.py:469
  80.6 41.8 %collective-permute-start.9 = (bf16[32,128,128]{2,1,0:T(8,128)(2,1)S(1)}, bf16[32,128,128]{2,1,0:T(8,128)(2,1)S(1)}, u32[]{:S(2)}, u32[]{:S(2)}) collective-permute-start(bf16[32,128,128]{2,1,0:T(8,128)(2,1)S(1)} %get-tuple-element.30), channel_id=1, source_target_pairs={{0,56},{8,192},{16,8},{24,208},{32,24},{40,224},{48,40},{56,240},{... | collective-permute-start | bytes 3145736 | tf_op jit(solution)/shard_map/ppermute | solution.py:469
  101.8 24.7 %collective-permute-start.13 = (s32[1024,128]{1,0:T(8,128)S(1)}, s32[1024,128]{1,0:T(8,128)S(1)}, u32[]{:S(2)}, u32[]{:S(2)}) collective-permute-start(s32[1024,128]{1,0:T(8,128)S(1)} %get-tuple-element.35.refs_10_.refs_6_), channel_id=1, source_target_pairs={{0,16},{8,72},{16,32},{24,88},{32,48},{40,104},{48,0},{56,120},{64... | collective-permute-start | bytes 1572872 | tf_op jit(solution)/shard_map/ppermute | solution.py:476
  101.8 20.5 %copy-start = (bf16[32,128,128]{2,1,0:T(8,128)(2,1)}, bf16[32,128,128]{2,1,0:T(8,128)(2,1)S(1)}, u32[]{:S(2)}) copy-start(bf16[32,128,128]{2,1,0:T(8,128)(2,1)S(1)} %collective-permute-done.6.refs_8_.refs_4_) | copy-start | bytes 3145732
  101.8 29.6 %collective-permute-start.14 = (s32[1024,128]{1,0:T(8,128)S(1)}, s32[1024,128]{1,0:T(8,128)S(1)}, u32[]{:S(2)}, u32[]{:S(2)}) collective-permute-start(s32[1024,128]{1,0:T(8,128)S(1)} %get-tuple-element.35.refs_10_.refs_6_), channel_id=1, source_target_pairs={{0,32},{8,136},{16,48},{24,152},{32,0},{40,168},{48,16},{56,184},{... | collective-permute-start | bytes 1572872 | tf_op jit(solution)/shard_map/ppermute | solution.py:476
  102.6 19.8 %copy-start.2 = (bf16[32,128,128]{2,1,0:T(8,128)(2,1)}, bf16[32,128,128]{2,1,0:T(8,128)(2,1)S(1)}, u32[]{:S(2)}) copy-start(bf16[32,128,128]{2,1,0:T(8,128)(2,1)S(1)} %collective-permute-done.7.refs_9_.refs_5_) | copy-start | bytes 3145732
  102.6 30.4 %collective-permute-start.15 = (s32[1024,128]{1,0:T(8,128)S(1)}, s32[1024,128]{1,0:T(8,128)S(1)}, u32[]{:S(2)}, u32[]{:S(2)}) collective-permute-start(s32[1024,128]{1,0:T(8,128)S(1)} %get-tuple-element.35.refs_10_.refs_6_), channel_id=1, source_target_pairs={{0,48},{8,200},{16,0},{24,216},{32,16},{40,232},{48,32},{56,248},{... | collective-permute-start | bytes 1572872 | tf_op jit(solution)/shard_map/ppermute | solution.py:476
  116.9 80.5 %collective-permute-start.26 = (bf16[8,1024,128]{2,1,0:T(8,128)(2,1)S(1)}, bf16[8,1024,128]{2,1,0:T(8,128)(2,1)}, u32[]{:S(2)}, u32[]{:S(2)}) collective-permute-start(bf16[8,1024,128]{2,1,0:T(8,128)(2,1)S(1)} %gather_weights.1.w_mine), channel_id=1, source_target_pairs={{0,8},{8,0},{16,24},{24,16},{32,40},{40,32},{48,56},{56,48},{64,72... | collective-permute-start | bytes 6291464 | tf_op jit(solution)/shard_map/ppermute | solution.py:481
  125.9 22.8 %collective-permute-start.10 = (bf16[16,128,128]{2,1,0:T(8,128)(2,1)S(1)}, bf16[16,128,128]{2,1,0:T(8,128)(2,1)S(1)}, u32[]{:S(2)}, u32[]{:S(2)}) collective-permute-start(bf16[16,128,128]{2,1,0:T(8,128)(2,1)S(1)} %get-tuple-element.32), channel_id=1, source_target_pairs={{0,48},{8,200},{16,0},{24,216},{32,16},{40,232},{48,32},{56,248},{... | collective-permute-start | bytes 1572872 | tf_op jit(solution)/shard_map/ppermute | solution.py:486
  126.6 20.2 %copy-start.7 = (s32[1024,128]{1,0:T(8,128)}, s32[1024,128]{1,0:T(8,128)S(1)}, u32[]{:S(2)}) copy-start(s32[1024,128]{1,0:T(8,128)S(1)} %collective-permute-done.13.refs_11_.refs_7_) | copy-start | bytes 1572868
  126.6 22.2 %collective-permute-start.11 = (bf16[16,128,128]{2,1,0:T(8,128)(2,1)S(1)}, bf16[16,128,128]{2,1,0:T(8,128)(2,1)S(1)}, u32[]{:S(2)}, u32[]{:S(2)}) collective-permute-start(bf16[16,128,128]{2,1,0:T(8,128)(2,1)S(1)} %get-tuple-element.33), channel_id=1, source_target_pairs={{0,32},{8,136},{16,48},{24,152},{32,0},{40,168},{48,16},{56,184},{... | collective-permute-start | bytes 1572872 | tf_op jit(solution)/shard_map/ppermute | solution.py:486
  131.4 17.3 %collective-permute-start.12 = (bf16[16,128,128]{2,1,0:T(8,128)(2,1)S(1)}, bf16[16,128,128]{2,1,0:T(8,128)(2,1)S(1)}, u32[]{:S(2)}, u32[]{:S(2)}) collective-permute-start(bf16[16,128,128]{2,1,0:T(8,128)(2,1)S(1)} %get-tuple-element.34), channel_id=1, source_target_pairs={{0,16},{8,72},{16,32},{24,88},{32,48},{40,104},{48,0},{56,120},{64... | collective-permute-start | bytes 1572872 | tf_op jit(solution)/shard_map/ppermute | solution.py:486
  149.8 40.9 %all-to-all-start = ((bf16[8,2,128,128]{3,2,1,0:T(8,128)(2,1)}), bf16[8,2,128,128]{3,2,1,0:T(8,128)(2,1)S(1)}, u32[]{:S(2)}, u32[]{:S(2)}) async-start(bf16[8,2,128,128]{3,2,1,0:T(8,128)(2,1)} %bitcast.5), calls=%async_computation | async-start | bytes 1048576 | tf_op jit(solution)/shard_map/all_to_all | solution.py:494
  173.5 14.9 %collective-permute-start.16 = (bf16[16,128,128]{2,1,0:T(8,128)(2,1)S(1)}, bf16[16,128,128]{2,1,0:T(8,128)(2,1)S(1)}, u32[]{:S(2)}, u32[]{:S(2)}) collective-permute-start(bf16[16,128,128]{2,1,0:T(8,128)(2,1)S(1)} %get-tuple-element.37), channel_id=1, source_target_pairs={{0,48},{8,200},{16,0},{24,216},{32,16},{40,232},{48,32},{56,248},{... | collective-permute-start | bytes 1572872 | tf_op jit(solution)/shard_map/ppermute | solution.py:491
  173.6 14.8 %collective-permute-start.17 = (bf16[16,128,128]{2,1,0:T(8,128)(2,1)S(1)}, bf16[16,128,128]{2,1,0:T(8,128)(2,1)S(1)}, u32[]{:S(2)}, u32[]{:S(2)}) collective-permute-start(bf16[16,128,128]{2,1,0:T(8,128)(2,1)S(1)} %get-tuple-element.38), channel_id=1, source_target_pairs={{0,32},{8,136},{16,48},{24,152},{32,0},{40,168},{48,16},{56,184},{... | collective-permute-start | bytes 1572872 | tf_op jit(solution)/shard_map/ppermute | solution.py:491
  173.7 15.4 %collective-permute-start.18 = (bf16[16,128,128]{2,1,0:T(8,128)(2,1)S(1)}, bf16[16,128,128]{2,1,0:T(8,128)(2,1)S(1)}, u32[]{:S(2)}, u32[]{:S(2)}) collective-permute-start(bf16[16,128,128]{2,1,0:T(8,128)(2,1)S(1)} %get-tuple-element.39), channel_id=1, source_target_pairs={{0,16},{8,72},{16,32},{24,88},{32,48},{40,104},{48,0},{56,120},{64... | collective-permute-start | bytes 1572872 | tf_op jit(solution)/shard_map/ppermute | solution.py:491
  190.7 24.7 %all-to-all-start.1 = ((bf16[8,2,128,128]{3,2,1,0:T(8,128)(2,1)}), bf16[8,2,128,128]{3,2,1,0:T(8,128)(2,1)S(1)}, u32[]{:S(2)}, u32[]{:S(2)}) async-start(bf16[8,2,128,128]{3,2,1,0:T(8,128)(2,1)} %bitcast.9), calls=%async_computation.1 | async-start | bytes 1048576 | tf_op jit(solution)/shard_map/all_to_all | solution.py:494
  (18 other events, 72.4 us)

commit v4 on v3

--- a/solution.py
+++ b/solution.py
@@ -15,6 +15,8 @@
 RING = 4
 N_SRC = 2 * RING
 DST = 16
+N_COL = 8
+ROW_BLK = DST // N_COL
 N_ITEMS = DST * TILES
 SECTION = N_ITEMS + ROWS
 UNROLL = 4
@@ -59,6 +61,10 @@
             pairs.append((dom_of(y, x, 0), dom_of(y, (x + m) % RING, 0)))
             pairs.append((dom_of(y, x, 1), dom_of((y + m) % RING, x, 1)))
     return pairs
+
+
+def col_pairs(k):
+    return [(i, (i + k) % N_COL) for i in range(N_COL)]
 
 
 def wrapped(v):
@@ -110,36 +116,46 @@
     )(me, requests, features)
 
 
-def tables_kernel(me, nbr, ws, wn, nbr_t, w_t):
+def turn_nbr_kernel(nbr, out):
     half = ROWS // 2
-
-    def turn_nbr(i, _):
-        turned = nbr[pl.ds(i * ROWS, ROWS), :].T
-        nbr_t[pl.ds(i * half, half), :] = turned[:half] + turned[half:] * 65536
-        return 0
-
-    lax.fori_loop(0, nbr.shape[0] // ROWS, turn_nbr, 0, unroll=2)
+    for i in range(nbr.shape[0] // ROWS):
+        turned = nbr[i * ROWS : (i + 1) * ROWS, :].T
+        out[i * half : (i + 1) * half, :] = turned[:half] + turned[half:] * 65536
+
+
+def turn_nbr(local_nbr):
+    some = 4 * ROWS
+    return pl.pallas_call(
+        turn_nbr_kernel,
+        grid=(local_nbr.shape[0] // some,),
+        out_shape=jax.ShapeDtypeStruct((local_nbr.shape[0] // 2, ROWS), I32),
+        in_specs=[pl.BlockSpec((some, ROWS), lambda g: (g, 0))],
+        out_specs=pl.BlockSpec((some // 2, ROWS), lambda g: (g, 0)),
+        cost_estimate=pl.CostEstimate(flops=10**9, bytes_accessed=10**7, transcendentals=0),
+        compiler_params=LIMIT,
+        name="turn_nbr",
+    )(local_nbr)
+
+
+def turn_weights_kernel(me, ws, wn, w_t):
     for core, w in enumerate((ws, wn)):
 
-        @pl.when(lax.rem(me[0], 2) == core)
+        @pl.when(me[0] & 1 == core)
         def _():
             for j in range(D // ROWS):
                 w_t[j * ROWS : (j + 1) * ROWS, :] = w[:, j * ROWS : (j + 1) * ROWS].T
 
 
-def tables(me, local_nbr, w_self, w_neigh):
-    return pl.pallas_call(
-        tables_kernel,
-        out_shape=(
-            jax.ShapeDtypeStruct((local_nbr.shape[0] // 2, ROWS), I32),
-            jax.ShapeDtypeStruct((D, ROWS), BF),
-        ),
-        in_specs=[SMEM] + [VMEM] * 3,
-        out_specs=(VMEM, VMEM),
+def turn_weights(me, w_self, w_neigh):
+    return pl.pallas_call(
+        turn_weights_kernel,
+        out_shape=jax.ShapeDtypeStruct((D, ROWS), BF),
+        in_specs=[SMEM] + [VMEM] * 2,
+        out_specs=VMEM,
         cost_estimate=pl.CostEstimate(flops=10**9, bytes_accessed=10**7, transcendentals=0),
         compiler_params=LIMIT,
-        name="tables",
-    )(me, local_nbr, w_self, w_neigh)
+        name="turn_weights",
+    )(me, w_self, w_neigh)
 
 
 def plan_kernel(me, cnt, tile_block, tile_count, todo, slot, size):
@@ -206,16 +222,15 @@
 
 
 def own_kernel(*refs):
-    lists, src, outs = refs[:RING], refs[RING : RING + N_SRC], refs[RING + N_SRC : 2 * RING + N_SRC]
-    stage, sem, sem_out = refs[2 * RING + N_SRC :]
-
-    def copy_of(q, n, v):
-        return pltpu.make_async_copy(src[q].at[v & 31], stage.at[n], sem)
-
+    lists, src, outs = refs[:RING], refs[RING : RING + N_SRC], refs[RING + N_SRC :]
     for m in range(RING):
 
-        def start(i, _):
+        def place(i, _, m=m):
             v = lists[m][m * SECTION + N_ITEMS + 2 + i]
+
+            @pl.when(v < 0)
+            def _():
+                outs[m][i] = jnp.zeros((ROWS, ROWS), BF)
 
             @pl.when(v >= 0)
             def _():
@@ -223,52 +238,26 @@
 
                     @pl.when(v >> 5 == q)
                     def _():
-                        copy_of(q, m * DST + i, v).start()
-
-            @pl.when(v < 0)
-            def _():
-                stage[m * DST + i] = jnp.zeros((ROWS, ROWS), BF)
+                        outs[m][i] = src[q][v & 31]
 
             return 0
 
-        lax.fori_loop(0, DST, start, 0)
-    for m in range(RING):
-
-        def finish(i, _):
-            @pl.when(lists[m][m * SECTION + N_ITEMS + 2 + i] >= 0)
-            def _():
-                copy_of(0, 0, 0).wait()
-
-            return 0
-
-        lax.fori_loop(0, DST, finish, 0)
-    copies = [
-        pltpu.make_async_copy(stage.at[pl.ds(m * DST, DST)], outs[m], sem_out.at[m]) for m in range(RING)
-    ]
-    for copy in copies:
-        copy.start()
-    for copy in copies:
-        copy.wait()
+        lax.fori_loop(0, DST, place, 0)
 
 
 def own_rows(lists, sources):
     return pl.pallas_call(
         own_kernel,
         out_shape=[jax.ShapeDtypeStruct((DST, ROWS, ROWS), BF)] * RING,
-        in_specs=[SMEM] * RING + [ANY] * N_SRC,
-        out_specs=[ANY] * RING,
-        scratch_shapes=[
-            pltpu.VMEM((RING * DST, ROWS, ROWS), BF),
-            pltpu.SemaphoreType.DMA,
-            pltpu.SemaphoreType.DMA((RING,)),
-        ],
+        in_specs=[SMEM] * RING + [VMEM] * N_SRC,
+        out_specs=[VMEM] * RING,
         cost_estimate=pl.CostEstimate(flops=10**9, bytes_accessed=10**7, transcendentals=0),
-        compiler_params=LIMIT,
+        compiler_params=grant(12),
         name="own_rows",
     )(*lists, *sources)
 
 
-def add_sums(lists, nbr, blocks, acc, late):
+def add_sums(lists, nbr, block_of, acc, late):
     iota = lax.broadcasted_iota(I32, (ROWS, ROWS), 0).astype(F32).astype(BF)
     one, zero = jnp.ones((), BF), jnp.zeros((), BF)
     for m in range(RING):
@@ -281,9 +270,7 @@
                 n = h * UNROLL + u
                 place = m * SECTION + (N_ITEMS - 1 - n if late else n)
                 item = jnp.where(n < n_item, todo[place], 128 * late)
-                q = (item >> 5) & 7
-                q = q - 4 if late else jnp.where(q > 3, q - 2, q)
-                blk = q * (RING * CAP) + (item & 31)
+                block = block_of((item >> 5) & 7, item & 31)
                 i = (item >> 8) & 15
                 t = item >> 12
                 row0 = i * (ROWS // 2) + (t & 15) * FAN_T
@@ -294,7 +281,7 @@
                     hit = jnp.where(iota == row.astype(F32).astype(BF), one, zero)
                     total = hit if total is None else total + hit
                 dst = jnp.where(n < n_item, m * DST + i, RING * DST)
-                parts.append((dst, jnp.dot(blocks[blk], total, preferred_element_type=F32)))
+                parts.append((dst, jnp.dot(block, total, preferred_element_type=F32)))
             for dst, part in parts:
                 acc[dst] += part
             return 0
@@ -312,7 +299,7 @@
 
 def early_kernel(*refs):
     lists, src, nbr = refs[:RING], refs[RING : RING + len(EARLY)], refs[RING + len(EARLY) : 2 * RING + len(EARLY)]
-    out, blocks, acc, sem, sem_out = refs[2 * RING + len(EARLY) :]
+    acc, blocks, sem = refs[2 * RING + len(EARLY) :]
     copies = fetched(src, blocks, sem)
 
     def clear(n, _):
@@ -322,23 +309,22 @@
     lax.fori_loop(0, RING * DST + 1, clear, 0)
     for copy in copies:
         copy.wait()
-    add_sums(lists, nbr, blocks, acc, 0)
-    leave = pltpu.make_async_copy(acc.at[pl.ds(0, RING * DST)], out, sem_out)
-    leave.start()
-    leave.wait()
+
+    def block_of(q, b):
+        return blocks[jnp.where(q > 3, q - 2, q) * (RING * CAP) + b]
+
+    add_sums(lists, nbr, block_of, acc, 0)
 
 
 def early_sums(lists, sources, nbrs):
     return pl.pallas_call(
         early_kernel,
-        out_shape=jax.ShapeDtypeStruct((RING * DST, ROWS, ROWS), F32),
+        out_shape=jax.ShapeDtypeStruct((RING * DST + 1, ROWS, ROWS), F32),
         in_specs=[SMEM] * RING + [ANY] * len(EARLY) + [VMEM] * RING,
-        out_specs=ANY,
+        out_specs=VMEM,
         scratch_shapes=[
             pltpu.VMEM((len(EARLY) * RING * CAP, ROWS, ROWS), BF),
-            pltpu.VMEM((RING * DST + 1, ROWS, ROWS), F32),
             pltpu.SemaphoreType.DMA((len(EARLY),)),
-            pltpu.SemaphoreType.DMA,
         ],
         cost_estimate=pl.CostEstimate(flops=10**10, bytes_accessed=2 * 10**7, transcendentals=0),
         compiler_params=grant(15),
@@ -348,17 +334,15 @@
 
 def late_kernel(*refs):
     lists, src, nbr = refs[:RING], refs[RING : RING + len(LATE)], refs[RING + len(LATE) : 2 * RING + len(LATE)]
-    early, outs = refs[2 * RING + len(LATE)], refs[2 * RING + len(LATE) + 1 : 3 * RING + len(LATE) + 1]
-    blocks, acc, sem, sem_in = refs[3 * RING + len(LATE) + 1 :]
-    begin = pltpu.make_async_copy(early, acc.at[pl.ds(0, RING * DST)], sem_in)
-    begin.start()
-    for copy in fetched(src, blocks, sem):
-        copy.wait()
-    begin.wait()
-    add_sums(lists, nbr, blocks, acc, 1)
+    _, *outs, acc = refs[2 * RING + len(LATE) :]
+
+    def block_of(q, b):
+        return jnp.where(q == LATE[0], src[0][b], src[1][b])
+
+    add_sums(lists, nbr, block_of, acc, 1)
     for m in range(RING):
 
-        def leave(n, _):
+        def leave(n, _, m=m):
             outs[m][n] = acc[m * DST + n].astype(BF)
             return 0
 
@@ -366,41 +350,38 @@
 
 
 def late_sums(lists, sources, nbrs, early):
+    n_in = 2 * RING + len(LATE)
     return pl.pallas_call(
         late_kernel,
-        out_shape=[jax.ShapeDtypeStruct((DST, ROWS, ROWS), BF)] * RING,
-        in_specs=[SMEM] * RING + [ANY] * len(LATE) + [VMEM] * RING + [ANY],
-        out_specs=[VMEM] * RING,
-        scratch_shapes=[
-            pltpu.VMEM((len(LATE) * RING * CAP, ROWS, ROWS), BF),
-            pltpu.VMEM((RING * DST + 1, ROWS, ROWS), F32),
-            pltpu.SemaphoreType.DMA((len(LATE),)),
-            pltpu.SemaphoreType.DMA,
-        ],
+        out_shape=[jax.ShapeDtypeStruct((DST, ROWS, ROWS), BF)] * RING + [jax.ShapeDtypeStruct(early.shape, F32)],
+        in_specs=[SMEM] * RING + [VMEM] * (len(LATE) + RING + 1),
+        out_specs=[VMEM] * (RING + 1),
+        input_output_aliases={n_in: RING},
         cost_estimate=pl.CostEstimate(flops=10**10, bytes_accessed=2 * 10**7, transcendentals=0),
         compiler_params=grant(12),
         name="late",
-    )(*lists, *sources, *nbrs, early)
+    )(*lists, *sources, *nbrs, early)[:RING]
 
 
 def join_own_kernel(a, b, c, d, out):
     for n in range(DST):
-        total = a[n].astype(F32) + b[n].astype(F32) + c[n].astype(F32) + d[n].astype(F32)
-        out[n] = total.astype(BF)
-
-
-def join_agg_kernel(tile_count, a, b, c, d, out):
-    for n in range(DST):
-        total = a[n].astype(F32) + b[n].astype(F32) + c[n].astype(F32) + d[n].astype(F32)
-        out[n] = (total / (tile_count[n] * FAN_T).astype(F32)).astype(BF)
-
-
-def join(kernel, scalars, parts):
+        out[n] = (a[n].astype(F32) + b[n].astype(F32) + c[n].astype(F32) + d[n].astype(F32)).astype(BF)
+
+
+def join_agg_kernel(column, tile_count, a, b, c, d, *outs):
+    for k, out in enumerate(outs):
+        for j in range(ROW_BLK):
+            n = ((column[0] + k) & (N_COL - 1)) * ROW_BLK + j
+            total = a[n].astype(F32) + b[n].astype(F32) + c[n].astype(F32) + d[n].astype(F32)
+            out[j] = (total / (tile_count[n] * FAN_T).astype(F32)).astype(BF)
+
+
+def join(kernel, scalars, parts, shapes):
     return pl.pallas_call(
         kernel,
-        out_shape=jax.ShapeDtypeStruct((DST, ROWS, ROWS), BF),
+        out_shape=[jax.ShapeDtypeStruct(shape, BF) for shape in shapes],
         in_specs=[SMEM] * len(scalars) + [VMEM] * RING,
-        out_specs=VMEM,
+        out_specs=[VMEM] * len(shapes),
         cost_estimate=pl.CostEstimate(flops=10**9, bytes_accessed=5 * 10**6, transcendentals=0),
         compiler_params=LIMIT,
     )(*scalars, *parts)
@@ -424,15 +405,14 @@
     )(*parts)
 
 
-def project_kernel(me, column, xs, xa, w_mine, w_other, out, hid):
-    n_col = xs.shape[0]
+def project_kernel(me, column, xs, *refs):
+    xa, (w_mine, w_other, out, hid) = refs[:N_COL], refs[N_COL:]
     self_first = me[0] & 1 == 0
-    for b in range(xs.shape[1]):
+    for b in range(ROW_BLK):
         for n0 in range(0, D, 256):
             total = None
-            for k in range(n_col):
-                group = (column[0] + n_col - k) & (n_col - 1)
-                s, a = xs[group, b], xa[group, b]
+            for k in range(N_COL):
+                s, a = xs[(column[0] - k) & (N_COL - 1), b], xa[k][b]
                 x = jnp.concatenate([jnp.where(self_first, s, a), jnp.where(self_first, a, s)], axis=0)
                 w = jnp.concatenate([w_mine[k, n0 : n0 + 256, :], w_other[k, n0 : n0 + 256, :]], axis=1)
                 part = jnp.dot(w, x, preferred_element_type=F32)
@@ -440,27 +420,25 @@
             hid[n0 : n0 + 256, :] = jnp.maximum(total, 0.0)
         h = hid[...]
         scale = jnp.sqrt(0.25 + jnp.sum(h * h, axis=0, keepdims=True) / D)
-        for j in range(n_col):
+        for j in range(N_COL):
             piece = hid[j * ROWS : (j + 1) * ROWS, :] / scale
             out[j, b * ROWS : (b + 1) * ROWS, :] = piece.T.astype(BF)
 
 
 def project(me, column, xs, xa, w_mine, w_other):
-    n_col, n_blk = xs.shape[:2]
     return pl.pallas_call(
         project_kernel,
-        out_shape=jax.ShapeDtypeStruct((n_col, n_blk * ROWS, ROWS), BF),
-        in_specs=[SMEM] * 2 + [VMEM] * 4,
+        out_shape=jax.ShapeDtypeStruct((N_COL, ROW_BLK * ROWS, ROWS), BF),
+        in_specs=[SMEM] * 2 + [VMEM] * (N_COL + 3),
         out_specs=VMEM,
         scratch_shapes=[pltpu.VMEM((D, ROWS), F32)],
         cost_estimate=pl.CostEstimate(flops=10**9, bytes_accessed=5 * 10**6, transcendentals=0),
         compiler_params=LIMIT,
         name="project",
-    )(me, column, xs, xa, w_mine, w_other)
+    )(me, column, xs, *xa, w_mine, w_other)
 
 
 def body(features, requests, counts, tile_block, local_nbr, tile_count, w_self, w_neigh):
-    n_col = lax.axis_size("col")
     me = lax.axis_index("dom").reshape(1).astype(I32)
     column = lax.axis_index("col").reshape(1).astype(I32)
     packed = pack(me, requests[0].T, features)
@@ -469,14 +447,15 @@
         sources.append(lax.ppermute(packed[q], "dom", meet_pairs(q // 2, q % 2)))
 
     todo = plan(me, counts[:, 0], tile_block, tile_count)
-    nbr_t, w_t = tables(me, local_nbr, w_self, w_neigh)
+    nbr_t = turn_nbr(local_nbr)
+    w_t = turn_weights(me, w_self, w_neigh)
     lists, nbrs = [todo], [nbr_t]
     for m in range(1, RING):
         lists.append(lax.ppermute(todo, "dom", ring_pairs(m)))
         nbrs.append(lax.ppermute(nbr_t, "dom", ring_pairs(m)))
     w_all = [w_t]
-    for k in range(1, n_col):
-        w_all.append(lax.ppermute(w_t, "col", [(i, (i + k) % n_col) for i in range(n_col)]))
+    for k in range(1, N_COL):
+        w_all.append(lax.ppermute(w_t, "col", col_pairs(k)))
     w_mine = gather_weights(w_all)
     w_other = lax.ppermute(w_mine, "dom", [(i, i ^ 1) for i in range(lax.axis_size("dom"))])
 
@@ -490,11 +469,10 @@
     for m in range(1, RING):
         agg_here.append(lax.ppermute(agg_parts[m], "dom", ring_pairs(RING - m)))
 
-    def to_rows(x):
-        return lax.all_to_all(x.reshape(n_col, DST // n_col, ROWS, ROWS), "col", 0, 0, tiled=True)
-
-    xs = to_rows(join(join_own_kernel, (), own_here))
-    xa = to_rows(join(join_agg_kernel, (tile_count,), agg_here))
+    (own_sum,) = join(join_own_kernel, (), own_here, [(DST, ROWS, ROWS)])
+    xs = lax.all_to_all(own_sum.reshape(N_COL, ROW_BLK, ROWS, ROWS), "col", 0, 0, tiled=True)
+    parts = join(join_agg_kernel, (column, tile_count), agg_here, [(ROW_BLK, ROWS, ROWS)] * N_COL)
+    xa = [parts[0]] + [lax.ppermute(parts[k], "col", col_pairs(k)) for k in range(1, N_COL)]
     y = project(me, column, xs, xa, w_mine, w_other)
     return lax.all_to_all(y, "col", 0, 0, tiled=True).reshape(-1, ROWS)
 

time: 241 us -> 241 us (level)
  the two profiles are of different devices: /device:TPU:25 before, /device:TPU:1 now
where the time goes in v4:
time: 241 us; the launch traced here: 240 us
  waiting for transfers between devices  85.2 us (35%)
  starting transfers between devices  80.8 us (34%)
  Pallas kernels  37.4 us (16%)
  blocking collectives  22.1 us (9%)
  local copies, waits for them, and re-layouts  14.5 us (6%)
    ppermute x7, waiting for transfers between devices, body(): w_all.append(lax.ppermute(w_t, 'col', col_pairs(k)))  34 us
    ppermute x7, waiting for transfers between devices, body(): sources.append(lax.ppermute(packed[q], 'dom', meet_pairs(q // 2, q % 2)))  28.9 us
    all_to_all x1, blocking collectives, body(): return lax.all_to_all(y, 'col', 0, 0, tiled=True).reshape(-1, ROWS)  22.1 us
    ppermute x7, starting transfers between devices, body(): w_all.append(lax.ppermute(w_t, 'col', col_pairs(k)))  16.5 us
    ppermute x7, starting transfers between devices, body(): sources.append(lax.ppermute(packed[q], 'dom', meet_pairs(q // 2, q % 2)))  14.9 us
    ppermute x3, waiting for transfers between devices, body(): agg_here.append(lax.ppermute(agg_parts[m], 'dom', ring_pairs(RING - m)))  14.6 us
    unnamed x45, local copies, waits for them, and re-layouts  14.5 us
    ppermute x7, starting transfers between devices, body(): lax.ppermute(parts[k], 'col', col_pairs(k))  14.4 us
  transfers between devices with their start and end apart: 35, of which 16 were waited for; matrix products, arithmetic and copies ran while one was open for 0% of the time, Pallas kernels for 14%

profile of v4, /device:TPU:1, one launch (start us, length us, event | category | flops | bytes accessed | tf_op | source)
XLA Modules:
  0.0 240.2 jit_solution(346824925644489635)
XLA Ops:
  2.2 2.5 %collective-permute-start.26 = (bf16[1024,128]{1,0:T(8,128)(2,1)S(1)}, bf16[1024,128]{1,0:T(8,128)(2,1)S(1)}, u32[]{:S(2)}, u32[]{:S(2)}) collective-permute-start(bf16[1024,128]{1,0:T(8,128)(2,1)S(1)} %turn_weights.1.refs_0_), channel_id=1, source_target_pairs={{0,1},{1,2},{2,3},{3,4},{4,5},{5,6},{6,7},{7,0},{8,9},{9,10},{10,1... | collective-permute-start | bytes 786440 | tf_op jit(solution)/shard_map/ppermute | solution.py:458
  4.8 2.9 %pack.1 = (bf16[32,128,128]{2,1,0:T(8,128)(2,1)S(1)}, bf16[32,128,128]{2,1,0:T(8,128)(2,1)S(1)}, bf16[32,128,128]{2,1,0:T(8,128)(2,1)S(1)}, bf16[32,128,128]{2,1...) custom-call(s32[1]{0:T(128)} %bitcast.me, ...), custom_call_target="tpu_custom_call" | custom-call | flops 1000000000 | bytes 10000000 | tf_op jit(solution)/shard_map/pack/pallas_call | solution.py:103
  10.0 5.2 %plan.1.refs_0_ = s32[3200]{0:T(1024)S(1)} custom-call(s32[1]{0:T(128)} %bitcast.me, s32[32]{0:T(128)S(1)} %bitcast.9, s32[16,32]{1,0:T(8,128)S(1)} %copy-done.14, s32[16]{0:T(128)S(1)} %copy-done.17), custom_call_target="tpu_custom_call" | custom-call | flops 2000000000 | bytes 1000000 | tf_op jit(solution)/shard_map/plan/pallas_call | solution.py:212
  21.3 3.0 %collective-permute-start.27 = (bf16[1024,128]{1,0:T(8,128)(2,1)S(1)}, bf16[1024,128]{1,0:T(8,128)(2,1)S(1)}, u32[]{:S(2)}, u32[]{:S(2)}) collective-permute-start(bf16[1024,128]{1,0:T(8,128)(2,1)S(1)} %turn_weights.1.refs_0_), channel_id=1, source_target_pairs={{0,2},{1,3},{2,4},{3,5},{4,6},{5,7},{6,0},{7,1},{8,10},{9,11},{10,... | collective-permute-start | bytes 786440 | tf_op jit(solution)/shard_map/ppermute | solution.py:458
  24.3 3.8 %collective-permute-start.28 = (bf16[1024,128]{1,0:T(8,128)(2,1)S(1)}, bf16[1024,128]{1,0:T(8,128)(2,1)S(1)}, u32[]{:S(2)}, u32[]{:S(2)}) collective-permute-start(bf16[1024,128]{1,0:T(8,128)(2,1)S(1)} %turn_weights.1.refs_0_), channel_id=1, source_target_pairs={{0,3},{1,4},{2,5},{3,6},{4,7},{5,0},{6,1},{7,2},{8,11},{9,12},{10,... | collective-permute-start | bytes 786440 | tf_op jit(solution)/shard_map/ppermute | solution.py:458
  29.4 6.0 %collective-permute-done.27.refs_2_ = bf16[1024,128]{1,0:T(8,128)(2,1)S(1)} collective-permute-done((bf16[1024,128]{1,0:T(8,128)(2,1)S(1)}, bf16[1024,128]{1,0:T(8,128)(2,1)S(1)}, u32[]{:S(2)}, u32[]{:S(2)}) %collective-permute-start.27) | collective-permute-done | bytes 262176 | tf_op jit(solution)/shard_map/ppermute | solution.py:458
  35.4 5.5 %collective-permute-start.30 = (bf16[1024,128]{1,0:T(8,128)(2,1)S(1)}, bf16[1024,128]{1,0:T(8,128)(2,1)S(1)}, u32[]{:S(2)}, u32[]{:S(2)}) collective-permute-start(bf16[1024,128]{1,0:T(8,128)(2,1)S(1)} %turn_weights.1.refs_0_), channel_id=1, source_target_pairs={{0,5},{1,6},{2,7},{3,0},{4,1},{5,2},{6,3},{7,4},{8,13},{9,14},{10,... | collective-permute-start | bytes 786440 | tf_op jit(solution)/shard_map/ppermute | solution.py:458
  40.9 13.7 %collective-permute-done.28.refs_3_ = bf16[1024,128]{1,0:T(8,128)(2,1)S(1)} collective-permute-done((bf16[1024,128]{1,0:T(8,128)(2,1)S(1)}, bf16[1024,128]{1,0:T(8,128)(2,1)S(1)}, u32[]{:S(2)}, u32[]{:S(2)}) %collective-permute-start.28) | collective-permute-done | bytes 262176 | tf_op jit(solution)/shard_map/ppermute | solution.py:458
  54.9 8.2 %collective-permute-done.29.refs_4_ = bf16[1024,128]{1,0:T(8,128)(2,1)S(1)} collective-permute-done((bf16[1024,128]{1,0:T(8,128)(2,1)S(1)}, bf16[1024,128]{1,0:T(8,128)(2,1)S(1)}, u32[]{:S(2)}, u32[]{:S(2)}) %collective-permute-start.29) | collective-permute-done | bytes 262176 | tf_op jit(solution)/shard_map/ppermute | solution.py:458
  63.2 4.3 %collective-permute-start.5 = (bf16[32,128,128]{2,1,0:T(8,128)(2,1)S(1)}, bf16[32,128,128]{2,1,0:T(8,128)(2,1)S(1)}, u32[]{:S(2)}, u32[]{:S(2)}) collective-permute-start(bf16[32,128,128]{2,1,0:T(8,128)(2,1)S(1)} %get-tuple-element.32), channel_id=1, source_target_pairs={{0,24},{8,64},{16,40},{24,80},{32,56},{40,96},{48,8},{56,112},{64,... | collective-permute-start | bytes 3145736 | tf_op jit(solution)/shard_map/ppermute | solution.py:447
  67.4 3.0 %collective-permute-done.31.refs_6_ = bf16[1024,128]{1,0:T(8,128)(2,1)S(1)} collective-permute-done((bf16[1024,128]{1,0:T(8,128)(2,1)S(1)}, bf16[1024,128]{1,0:T(8,128)(2,1)S(1)}, u32[]{:S(2)}, u32[]{:S(2)}) %collective-permute-start.31) | collective-permute-done | bytes 262176 | tf_op jit(solution)/shard_map/ppermute | solution.py:458
  70.4 2.8 %collective-permute-start.6 = (bf16[32,128,128]{2,1,0:T(8,128)(2,1)S(1)}, bf16[32,128,128]{2,1,0:T(8,128)(2,1)S(1)}, u32[]{:S(2)}, u32[]{:S(2)}) collective-permute-start(bf16[32,128,128]{2,1,0:T(8,128)(2,1)S(1)} %get-tuple-element.33), channel_id=1, source_target_pairs={{0,128},{8,40},{16,144},{24,56},{32,160},{40,8},{48,176},{56,24},{... | collective-permute-start | bytes 3145736 | tf_op jit(solution)/shard_map/ppermute | solution.py:447
  73.3 3.2 %collective-permute-done.32.refs_7_ = bf16[1024,128]{1,0:T(8,128)(2,1)S(1)} collective-permute-done((bf16[1024,128]{1,0:T(8,128)(2,1)S(1)}, bf16[1024,128]{1,0:T(8,128)(2,1)S(1)}, u32[]{:S(2)}, u32[]{:S(2)}) %collective-permute-start.32) | collective-permute-done | bytes 262176 | tf_op jit(solution)/shard_map/ppermute | solution.py:458
  76.4 4.9 %collective-permute-start.7 = (bf16[32,128,128]{2,1,0:T(8,128)(2,1)S(1)}, bf16[32,128,128]{2,1,0:T(8,128)(2,1)S(1)}, u32[]{:S(2)}, u32[]{:S(2)}) collective-permute-start(bf16[32,128,128]{2,1,0:T(8,128)(2,1)S(1)} %get-tuple-element.34), channel_id=1, source_target_pairs={{0,40},{8,128},{16,56},{24,144},{32,8},{40,160},{48,24},{56,176},{... | collective-permute-start | bytes 3145736 | tf_op jit(solution)/shard_map/ppermute | solution.py:447
  84.6 12.5 %collective-permute-done.6.refs_8_.refs_4_ = bf16[32,128,128]{2,1,0:T(8,128)(2,1)S(1)} collective-permute-done((bf16[32,128,128]{2,1,0:T(8,128)(2,1)S(1)}, bf16[32,128,128]{2,1,0:T(8,128)(2,1)S(1)}, u32[]{:S(2)}, u32[]{:S(2)}) %collective-permute-start.6) | collective-permute-done | bytes 1048608 | tf_op jit(solution)/shard_map/ppermute | solution.py:447
  97.1 6.8 %collective-permute-start.14 = (s32[1024,128]{1,0:T(8,128)S(1)}, s32[1024,128]{1,0:T(8,128)S(1)}, u32[]{:S(2)}, u32[]{:S(2)}) collective-permute-start(s32[1024,128]{1,0:T(8,128)S(1)} %turn_nbr.1.refs_10_.refs_6_), channel_id=1, source_target_pairs={{0,32},{8,136},{16,48},{24,152},{32,0},{40,168},{48,16},{56,184},{... | collective-permute-start | bytes 1572872 | tf_op jit(solution)/shard_map/ppermute | solution.py:455
  104.5 14.3 %collective-permute-done.8.refs_10_.refs_8_ = bf16[32,128,128]{2,1,0:T(8,128)(2,1)S(1)} collective-permute-done((bf16[32,128,128]{2,1,0:T(8,128)(2,1)S(1)}, bf16[32,128,128]{2,1,0:T(8,128)(2,1)S(1)}, u32[]{:S(2)}, u32[]{:S(2)}) %collective-permute-start.8) | collective-permute-done | bytes 1048608 | tf_op jit(solution)/shard_map/ppermute | solution.py:447
  120.1 5.1 %own_rows.1 = (bf16[16,128,128]{2,1,0:T(8,128)(2,1)S(1)}, bf16[16,128,128]{2,1,0:T(8,128)(2,1)S(1)}, bf16[16,128,128]{2,1,0:T(8,128)(2,1)S(1)}, bf16[16,128,128]{2,1,0:T(8,128)(2,1)S(1)}) custom-call(s32[3200]{0:T(1024)S(1)} %plan.1.refs_0_, s32[3200]{0:T(1024)S(1)} %collective-permute-done.refs_1_, s32[3200]{0:T(1024)S(1)} %collective-permute-done.1.refs_2_, ...), custom_call_target="tpu_custom_call" | custom-call | flops 1000000000 | bytes 10000000 | tf_op jit(solution)/shard_map/own_rows/pallas_call | solution.py:249
  126.3 2.6 %collective-permute-start.11 = (bf16[16,128,128]{2,1,0:T(8,128)(2,1)S(1)}, bf16[16,128,128]{2,1,0:T(8,128)(2,1)S(1)}, u32[]{:S(2)}, u32[]{:S(2)}) collective-permute-start(bf16[16,128,128]{2,1,0:T(8,128)(2,1)S(1)} %get-tuple-element.39), channel_id=1, source_target_pairs={{0,32},{8,136},{16,48},{24,152},{32,0},{40,168},{48,16},{56,184},{... | collective-permute-start | bytes 1572872 | tf_op jit(solution)/shard_map/ppermute | solution.py:465
  129.5 2.6 %collective-permute-done.15.refs_13_.refs_9_ = s32[1024,128]{1,0:T(8,128)S(1)} collective-permute-done((s32[1024,128]{1,0:T(8,128)S(1)}, s32[1024,128]{1,0:T(8,128)S(1)}, u32[]{:S(2)}, u32[]{:S(2)}) %collective-permute-start.15) | collective-permute-done | bytes 524320 | tf_op jit(solution)/shard_map/ppermute | solution.py:455
  132.1 10.3 %early.1.refs_10_ = f32[65,128,128]{2,1,0:T(8,128)S(1)} custom-call(s32[3200]{0:T(1024)S(1)} %plan.1.refs_0_, s32[3200]{0:T(1024)S(1)} %collective-permute-done.refs_1_, s32[3200]{0:T(1024)S(1)} %collective-permute-done.1.refs_2_, s32[3200]{0:T(1024)S(1)} %collective-permute-done.2.refs_3_, bf16[32,128,128]{2,1,0:T(8,128)(2,1)S(1)} %get-tuple-element.29.refs_4_, ...), custom_call_target="tpu_custom_call" | custom-call | flops 10000000000 | bytes 20000000 | tf_op jit(solution)/shard_map/early/pallas_call | solution.py:320
  145.6 10.2 %all-to-all-start = ((bf16[8,2,128,128]{3,2,1,0:T(8,128)(2,1)}), bf16[8,2,128,128]{3,2,1,0:T(8,128)(2,1)S(1)}, u32[]{:S(2)}, u32[]{:S(2)}) async-start(bf16[8,2,128,128]{3,2,1,0:T(8,128)(2,1)} %bitcast.5), calls=%async_computation | async-start | bytes 1048576 | tf_op jit(solution)/shard_map/all_to_all | solution.py:473
  163.6 6.4 %late.1 = (bf16[16,128,128]{2,1,0:T(8,128)(2,1)S(1)}, bf16[16,128,128]{2,1,0:T(8,128)(2,1)}, bf16[16,128,128]{2,1,0:T(8,128)(2,1)}, bf16[16,128,128]{2,1,0:T(8,128)(2,1)}, f32[65,128,128]{2,1,0:T(8,128)S(1)}) custom-call(s32[3200]{0:T(1024)S(1)} %plan.1.refs_0_, s32[3200]{0:T(1024)S(1)} %collective-permute-done.refs_1_, ...), custom_call_target="tpu_custom_call", output_to_operand_aliasing={{4}: (10, {})} | custom-call | flops 10000000000 | bytes 20000000 | tf_op jit(solution)/shard_map/late/pallas_call | solution.py:354
  170.7 6.5 %collective-permute-start.16 = (bf16[16,128,128]{2,1,0:T(8,128)(2,1)}, bf16[16,128,128]{2,1,0:T(8,128)(2,1)S(1)}, u32[]{:S(2)}, u32[]{:S(2)}) collective-permute-start(bf16[16,128,128]{2,1,0:T(8,128)(2,1)} %get-tuple-element.42), channel_id=1, source_target_pairs={{0,48},{8,200},{16,0},{24,216},{32,16},{40,232},{48,32},{56,248},{... | collective-permute-start | bytes 1572872 | tf_op jit(solution)/shard_map/ppermute | solution.py:470
  177.8 11.5 %collective-permute-done.16.b = bf16[16,128,128]{2,1,0:T(8,128)(2,1)S(1)} collective-permute-done((bf16[16,128,128]{2,1,0:T(8,128)(2,1)}, bf16[16,128,128]{2,1,0:T(8,128)(2,1)S(1)}, u32[]{:S(2)}, u32[]{:S(2)}) %collective-permute-start.16) | collective-permute-done | bytes 524320 | tf_op jit(solution)/shard_map/ppermute | solution.py:470
  189.3 3.1 %collective-permute-done.18.d = bf16[16,128,128]{2,1,0:T(8,128)(2,1)} collective-permute-done((bf16[16,128,128]{2,1,0:T(8,128)(2,1)}, bf16[16,128,128]{2,1,0:T(8,128)(2,1)}, u32[]{:S(2)}, u32[]{:S(2)}) %collective-permute-start.18) | collective-permute-done | bytes 524320 | tf_op jit(solution)/shard_map/ppermute | solution.py:470
  198.6 2.4 %collective-permute-start.21 = (bf16[2,128,128]{2,1,0:T(8,128)(2,1)S(1)}, bf16[2,128,128]{2,1,0:T(8,128)(2,1)S(1)}, u32[]{:S(2)}, u32[]{:S(2)}) collective-permute-start(bf16[2,128,128]{2,1,0:T(8,128)(2,1)S(1)} %get-tuple-element.48), channel_id=1, source_target_pairs={{0,3},{1,4},{2,5},{3,6},{4,7},{5,0},{6,1},{7,2},{8,11},{9,12},{10,... | collective-permute-start | bytes 196616 | tf_op jit(solution)/shard_map/ppermute | solution.py:475
  203.0 2.4 %collective-permute-start.23 = (bf16[2,128,128]{2,1,0:T(8,128)(2,1)S(1)}, bf16[2,128,128]{2,1,0:T(8,128)(2,1)S(1)}, u32[]{:S(2)}, u32[]{:S(2)}) collective-permute-start(bf16[2,128,128]{2,1,0:T(8,128)(2,1)S(1)} %get-tuple-element.50), channel_id=1, source_target_pairs={{0,5},{1,6},{2,7},{3,0},{4,1},{5,2},{6,3},{7,4},{8,13},{9,14},{10,... | collective-permute-start | bytes 196616 | tf_op jit(solution)/shard_map/ppermute | solution.py:475
  206.0 2.7 %collective-permute-start.24 = (bf16[2,128,128]{2,1,0:T(8,128)(2,1)S(1)}, bf16[2,128,128]{2,1,0:T(8,128)(2,1)S(1)}, u32[]{:S(2)}, u32[]{:S(2)}) collective-permute-start(bf16[2,128,128]{2,1,0:T(8,128)(2,1)S(1)} %get-tuple-element.51), channel_id=1, source_target_pairs={{0,6},{1,7},{2,0},{3,1},{4,2},{5,3},{6,4},{7,5},{8,14},{9,15},{10,... | collective-permute-start | bytes 196616 | tf_op jit(solution)/shard_map/ppermute | solution.py:475
  210.8 2.4 collective-permute-done.24.refs_6_
  213.2 4.1 %project.1 = bf16[8,256,128]{2,1,0:T(8,128)(2,1)S(1)} custom-call(s32[1]{0:T(128)} %bitcast.me, s32[1]{0:T(128)} %bitcast.1.column, bf16[8,2,128,128]{3,2,1,0:T(8,128)(2,1)S(1)} %all-to-all-done.xs, bf16[2,128,128]{2,1,0:T(8,128)(2,1)S(1)} %get-tuple-element.45.refs_0_, bf16[2,128,128]{2,1,0:T(8,128)(2,1)S(1)} %collective-permute-done.19.refs_1_, ...), custom_call_target="tpu_custom_call" | custom-call | flops 1000000000 | bytes 5000000 | tf_op jit(solution)/shard_map/project/pallas_call | solution.py:429
  217.3 22.1 %all_to_all.10 = bf16[8,256,128]{2,1,0:T(8,128)(2,1)S(1)} all-to-all(bf16[8,256,128]{2,1,0:T(8,128)(2,1)S(1)} %project.1), channel_id=1, replica_groups=mesh['dom'=32,'col'=8] {'col'}, dimensions={0} | all-to-all | bytes 1048576 | tf_op jit(solution)/shard_map/all_to_all | solution.py:477
  (95 shorter events, 42.9 us)
Async XLA Ops:
  2.2 25.9 %collective-permute-start.26 = (bf16[1024,128]{1,0:T(8,128)(2,1)S(1)}, bf16[1024,128]{1,0:T(8,128)(2,1)S(1)}, u32[]{:S(2)}, u32[]{:S(2)}) collective-permute-start(bf16[1024,128]{1,0:T(8,128)(2,1)S(1)} %turn_weights.1.refs_0_), channel_id=1, source_target_pairs={{0,1},{1,2},{2,3},{3,4},{4,5},{5,6},{6,7},{7,0},{8,9},{9,10},{10,1... | collective-permute-start | bytes 786440 | tf_op jit(solution)/shard_map/ppermute | solution.py:458
  7.7 73.7 %collective-permute-start.3 = (bf16[32,128,128]{2,1,0:T(8,128)(2,1)S(1)}, bf16[32,128,128]{2,1,0:T(8,128)(2,1)S(1)}, u32[]{:S(2)}, u32[]{:S(2)}) collective-permute-start(bf16[32,128,128]{2,1,0:T(8,128)(2,1)S(1)} %get-tuple-element.30), channel_id=1, source_target_pairs={{0,8},{8,0},{16,24},{24,16},{32,40},{40,32},{48,56},{56,48},{64,72... | collective-permute-start | bytes 3145736 | tf_op jit(solution)/shard_map/ppermute | solution.py:447
  9.0 72.8 %collective-permute-start.4 = (bf16[32,128,128]{2,1,0:T(8,128)(2,1)S(1)}, bf16[32,128,128]{2,1,0:T(8,128)(2,1)S(1)}, u32[]{:S(2)}, u32[]{:S(2)}) collective-permute-start(bf16[32,128,128]{2,1,0:T(8,128)(2,1)S(1)} %get-tuple-element.31), channel_id=1, source_target_pairs={{0,64},{8,24},{16,80},{24,40},{32,96},{40,56},{48,112},{56,8},{64,... | collective-permute-start | bytes 3145736 | tf_op jit(solution)/shard_map/ppermute | solution.py:447
  19.5 4.8 %collective-permute-start.2 = (s32[3200]{0:T(1024)S(1)}, s32[3200]{0:T(1024)S(1)}, u32[]{:S(2)}, u32[]{:S(2)}) collective-permute-start(s32[3200]{0:T(1024)S(1)} %plan.1.refs_0_), channel_id=1, source_target_pairs={{0,48},{8,200},{16,0},{24,216},{32,16},{40,232},{48,32},{56,248},{... | collective-permute-start | bytes 38408 | tf_op jit(solution)/shard_map/ppermute | solution.py:454
  21.3 14.1 %collective-permute-start.27 = (bf16[1024,128]{1,0:T(8,128)(2,1)S(1)}, bf16[1024,128]{1,0:T(8,128)(2,1)S(1)}, u32[]{:S(2)}, u32[]{:S(2)}) collective-permute-start(bf16[1024,128]{1,0:T(8,128)(2,1)S(1)} %turn_weights.1.refs_0_), channel_id=1, source_target_pairs={{0,2},{1,3},{2,4},{3,5},{4,6},{5,7},{6,0},{7,1},{8,10},{9,11},{10,... | collective-permute-start | bytes 786440 | tf_op jit(solution)/shard_map/ppermute | solution.py:458
  24.3 30.3 %collective-permute-start.28 = (bf16[1024,128]{1,0:T(8,128)(2,1)S(1)}, bf16[1024,128]{1,0:T(8,128)(2,1)S(1)}, u32[]{:S(2)}, u32[]{:S(2)}) collective-permute-start(bf16[1024,128]{1,0:T(8,128)(2,1)S(1)} %turn_weights.1.refs_0_), channel_id=1, source_target_pairs={{0,3},{1,4},{2,5},{3,6},{4,7},{5,0},{6,1},{7,2},{8,11},{9,12},{10,... | collective-permute-start | bytes 786440 | tf_op jit(solution)/shard_map/ppermute | solution.py:458
  28.1 35.1 %collective-permute-start.29 = (bf16[1024,128]{1,0:T(8,128)(2,1)S(1)}, bf16[1024,128]{1,0:T(8,128)(2,1)S(1)}, u32[]{:S(2)}, u32[]{:S(2)}) collective-permute-start(bf16[1024,128]{1,0:T(8,128)(2,1)S(1)} %turn_weights.1.refs_0_), channel_id=1, source_target_pairs={{0,4},{1,5},{2,6},{3,7},{4,0},{5,1},{6,2},{7,3},{8,12},{9,13},{10,... | collective-permute-start | bytes 786440 | tf_op jit(solution)/shard_map/ppermute | solution.py:458
  35.4 27.8 %collective-permute-start.30 = (bf16[1024,128]{1,0:T(8,128)(2,1)S(1)}, bf16[1024,128]{1,0:T(8,128)(2,1)S(1)}, u32[]{:S(2)}, u32[]{:S(2)}) collective-permute-start(bf16[1024,128]{1,0:T(8,128)(2,1)S(1)} %turn_weights.1.refs_0_), channel_id=1, source_target_pairs={{0,5},{1,6},{2,7},{3,0},{4,1},{5,2},{6,3},{7,4},{8,13},{9,14},{10,... | collective-permute-start | bytes 786440 | tf_op jit(solution)/shard_map/ppermute | solution.py:458
  54.6 15.8 %collective-permute-start.31 = (bf16[1024,128]{1,0:T(8,128)(2,1)S(1)}, bf16[1024,128]{1,0:T(8,128)(2,1)S(1)}, u32[]{:S(2)}, u32[]{:S(2)}) collective-permute-start(bf16[1024,128]{1,0:T(8,128)(2,1)S(1)} %turn_weights.1.refs_0_), channel_id=1, source_target_pairs={{0,6},{1,7},{2,0},{3,1},{4,2},{5,3},{6,4},{7,5},{8,14},{9,15},{10,... | collective-permute-start | bytes 786440 | tf_op jit(solution)/shard_map/ppermute | solution.py:458
  63.2 13.3 %collective-permute-start.32 = (bf16[1024,128]{1,0:T(8,128)(2,1)S(1)}, bf16[1024,128]{1,0:T(8,128)(2,1)S(1)}, u32[]{:S(2)}, u32[]{:S(2)}) collective-permute-start(bf16[1024,128]{1,0:T(8,128)(2,1)S(1)} %turn_weights.1.refs_0_), channel_id=1, source_target_pairs={{0,7},{1,0},{2,1},{3,2},{4,3},{5,4},{6,5},{7,6},{8,15},{9,8},{10,9... | collective-permute-start | bytes 786440 | tf_op jit(solution)/shard_map/ppermute | solution.py:458
  63.2 21.4 %collective-permute-start.5 = (bf16[32,128,128]{2,1,0:T(8,128)(2,1)S(1)}, bf16[32,128,128]{2,1,0:T(8,128)(2,1)S(1)}, u32[]{:S(2)}, u32[]{:S(2)}) collective-permute-start(bf16[32,128,128]{2,1,0:T(8,128)(2,1)S(1)} %get-tuple-element.32), channel_id=1, source_target_pairs={{0,24},{8,64},{16,40},{24,80},{32,56},{40,96},{48,8},{56,112},{64,... | collective-permute-start | bytes 3145736 | tf_op jit(solution)/shard_map/ppermute | solution.py:447
  70.4 26.7 %collective-permute-start.6 = (bf16[32,128,128]{2,1,0:T(8,128)(2,1)S(1)}, bf16[32,128,128]{2,1,0:T(8,128)(2,1)S(1)}, u32[]{:S(2)}, u32[]{:S(2)}) collective-permute-start(bf16[32,128,128]{2,1,0:T(8,128)(2,1)S(1)} %get-tuple-element.33), channel_id=1, source_target_pairs={{0,128},{8,40},{16,144},{24,56},{32,160},{40,8},{48,176},{56,24},{... | collective-permute-start | bytes 3145736 | tf_op jit(solution)/shard_map/ppermute | solution.py:447
  76.4 27.5 %collective-permute-start.7 = (bf16[32,128,128]{2,1,0:T(8,128)(2,1)S(1)}, bf16[32,128,128]{2,1,0:T(8,128)(2,1)S(1)}, u32[]{:S(2)}, u32[]{:S(2)}) collective-permute-start(bf16[32,128,128]{2,1,0:T(8,128)(2,1)S(1)} %get-tuple-element.34), channel_id=1, source_target_pairs={{0,40},{8,128},{16,56},{24,144},{32,8},{40,160},{48,24},{56,176},{... | collective-permute-start | bytes 3145736 | tf_op jit(solution)/shard_map/ppermute | solution.py:447
  81.4 37.4 %collective-permute-start.8 = (bf16[32,128,128]{2,1,0:T(8,128)(2,1)S(1)}, bf16[32,128,128]{2,1,0:T(8,128)(2,1)S(1)}, u32[]{:S(2)}, u32[]{:S(2)}) collective-permute-start(bf16[32,128,128]{2,1,0:T(8,128)(2,1)S(1)} %get-tuple-element.35), channel_id=1, source_target_pairs={{0,192},{8,56},{16,208},{24,8},{32,224},{40,24},{48,240},{56,40},{... | collective-permute-start | bytes 3145736 | tf_op jit(solution)/shard_map/ppermute | solution.py:447
  81.8 38.3 %collective-permute-start.9 = (bf16[32,128,128]{2,1,0:T(8,128)(2,1)S(1)}, bf16[32,128,128]{2,1,0:T(8,128)(2,1)S(1)}, u32[]{:S(2)}, u32[]{:S(2)}) collective-permute-start(bf16[32,128,128]{2,1,0:T(8,128)(2,1)S(1)} %get-tuple-element.36), channel_id=1, source_target_pairs={{0,56},{8,192},{16,8},{24,208},{32,24},{40,224},{48,40},{56,240},{... | collective-permute-start | bytes 3145736 | tf_op jit(solution)/shard_map/ppermute | solution.py:447
  84.6 41.7 %collective-permute-start.13 = (s32[1024,128]{1,0:T(8,128)S(1)}, s32[1024,128]{1,0:T(8,128)S(1)}, u32[]{:S(2)}, u32[]{:S(2)}) collective-permute-start(s32[1024,128]{1,0:T(8,128)S(1)} %turn_nbr.1.refs_10_.refs_6_), channel_id=1, source_target_pairs={{0,16},{8,72},{16,32},{24,88},{32,48},{40,104},{48,0},{56,120},{64... | collective-permute-start | bytes 1572872 | tf_op jit(solution)/shard_map/ppermute | solution.py:455
  97.1 31.9 %collective-permute-start.14 = (s32[1024,128]{1,0:T(8,128)S(1)}, s32[1024,128]{1,0:T(8,128)S(1)}, u32[]{:S(2)}, u32[]{:S(2)}) collective-permute-start(s32[1024,128]{1,0:T(8,128)S(1)} %turn_nbr.1.refs_10_.refs_6_), channel_id=1, source_target_pairs={{0,32},{8,136},{16,48},{24,152},{32,0},{40,168},{48,16},{56,184},{... | collective-permute-start | bytes 1572872 | tf_op jit(solution)/shard_map/ppermute | solution.py:455
  103.9 28.2 %collective-permute-start.15 = (s32[1024,128]{1,0:T(8,128)S(1)}, s32[1024,128]{1,0:T(8,128)S(1)}, u32[]{:S(2)}, u32[]{:S(2)}) collective-permute-start(s32[1024,128]{1,0:T(8,128)S(1)} %turn_nbr.1.refs_10_.refs_6_), channel_id=1, source_target_pairs={{0,48},{8,200},{16,0},{24,216},{32,16},{40,232},{48,32},{56,248},{... | collective-permute-start | bytes 1572872 | tf_op jit(solution)/shard_map/ppermute | solution.py:455
  118.8 94.4 %collective-permute-start.33 = (bf16[8,1024,128]{2,1,0:T(8,128)(2,1)S(1)}, bf16[8,1024,128]{2,1,0:T(8,128)(2,1)}, u32[]{:S(2)}, u32[]{:S(2)}) collective-permute-start(bf16[8,1024,128]{2,1,0:T(8,128)(2,1)S(1)} %gather_weights.1.refs_8_), channel_id=1, source_target_pairs={{0,8},{8,0},{16,24},{24,16},{32,40},{40,32},{48,56},{56,48},{64,72... | collective-permute-start | bytes 6291464 | tf_op jit(solution)/shard_map/ppermute | solution.py:460
  125.2 19.3 %collective-permute-start.10 = (bf16[16,128,128]{2,1,0:T(8,128)(2,1)S(1)}, bf16[16,128,128]{2,1,0:T(8,128)(2,1)S(1)}, u32[]{:S(2)}, u32[]{:S(2)}) collective-permute-start(bf16[16,128,128]{2,1,0:T(8,128)(2,1)S(1)} %get-tuple-element.38), channel_id=1, source_target_pairs={{0,48},{8,200},{16,0},{24,216},{32,16},{40,232},{48,32},{56,248},{... | collective-permute-start | bytes 1572872 | tf_op jit(solution)/shard_map/ppermute | solution.py:465
  126.3 18.2 %collective-permute-start.11 = (bf16[16,128,128]{2,1,0:T(8,128)(2,1)S(1)}, bf16[16,128,128]{2,1,0:T(8,128)(2,1)S(1)}, u32[]{:S(2)}, u32[]{:S(2)}) collective-permute-start(bf16[16,128,128]{2,1,0:T(8,128)(2,1)S(1)} %get-tuple-element.39), channel_id=1, source_target_pairs={{0,32},{8,136},{16,48},{24,152},{32,0},{40,168},{48,16},{56,184},{... | collective-permute-start | bytes 1572872 | tf_op jit(solution)/shard_map/ppermute | solution.py:465
  129.0 15.6 %collective-permute-start.12 = (bf16[16,128,128]{2,1,0:T(8,128)(2,1)S(1)}, bf16[16,128,128]{2,1,0:T(8,128)(2,1)S(1)}, u32[]{:S(2)}, u32[]{:S(2)}) collective-permute-start(bf16[16,128,128]{2,1,0:T(8,128)(2,1)S(1)} %get-tuple-element.40), channel_id=1, source_target_pairs={{0,16},{8,72},{16,32},{24,88},{32,48},{40,104},{48,0},{56,120},{64... | collective-permute-start | bytes 1572872 | tf_op jit(solution)/shard_map/ppermute | solution.py:465
  145.6 67.6 %all-to-all-start = ((bf16[8,2,128,128]{3,2,1,0:T(8,128)(2,1)}), bf16[8,2,128,128]{3,2,1,0:T(8,128)(2,1)S(1)}, u32[]{:S(2)}, u32[]{:S(2)}) async-start(bf16[8,2,128,128]{3,2,1,0:T(8,128)(2,1)} %bitcast.5), calls=%async_computation | async-start | bytes 1048576 | tf_op jit(solution)/shard_map/all_to_all | solution.py:473
  170.7 18.5 %collective-permute-start.16 = (bf16[16,128,128]{2,1,0:T(8,128)(2,1)}, bf16[16,128,128]{2,1,0:T(8,128)(2,1)S(1)}, u32[]{:S(2)}, u32[]{:S(2)}) collective-permute-start(bf16[16,128,128]{2,1,0:T(8,128)(2,1)} %get-tuple-element.42), channel_id=1, source_target_pairs={{0,48},{8,200},{16,0},{24,216},{32,16},{40,232},{48,32},{56,248},{... | collective-permute-start | bytes 1572872 | tf_op jit(solution)/shard_map/ppermute | solution.py:470
  177.2 12.1 %collective-permute-start.17 = (bf16[16,128,128]{2,1,0:T(8,128)(2,1)}, bf16[16,128,128]{2,1,0:T(8,128)(2,1)}, u32[]{:S(2)}, u32[]{:S(2)}) collective-permute-start(bf16[16,128,128]{2,1,0:T(8,128)(2,1)} %get-tuple-element.43), channel_id=1, source_target_pairs={{0,32},{8,136},{16,48},{24,152},{32,0},{40,168},{48,16},{56,184},{... | collective-permute-start | bytes 1572872 | tf_op jit(solution)/shard_map/ppermute | solution.py:470
  177.2 15.2 %collective-permute-start.18 = (bf16[16,128,128]{2,1,0:T(8,128)(2,1)}, bf16[16,128,128]{2,1,0:T(8,128)(2,1)}, u32[]{:S(2)}, u32[]{:S(2)}) collective-permute-start(bf16[16,128,128]{2,1,0:T(8,128)(2,1)} %get-tuple-element.44), channel_id=1, source_target_pairs={{0,16},{8,72},{16,32},{24,88},{32,48},{40,104},{48,0},{56,120},{64... | collective-permute-start | bytes 1572872 | tf_op jit(solution)/shard_map/ppermute | solution.py:470
  194.9 8.1 %collective-permute-start.19 = (bf16[2,128,128]{2,1,0:T(8,128)(2,1)S(1)}, bf16[2,128,128]{2,1,0:T(8,128)(2,1)S(1)}, u32[]{:S(2)}, u32[]{:S(2)}) collective-permute-start(bf16[2,128,128]{2,1,0:T(8,128)(2,1)S(1)} %get-tuple-element.46), channel_id=1, source_target_pairs={{0,1},{1,2},{2,3},{3,4},{4,5},{5,6},{6,7},{7,0},{8,9},{9,10},{10,1... | collective-permute-start | bytes 196616 | tf_op jit(solution)/shard_map/ppermute | solution.py:475
  196.5 9.5 %collective-permute-start.20 = (bf16[2,128,128]{2,1,0:T(8,128)(2,1)S(1)}, bf16[2,128,128]{2,1,0:T(8,128)(2,1)S(1)}, u32[]{:S(2)}, u32[]{:S(2)}) collective-permute-start(bf16[2,128,128]{2,1,0:T(8,128)(2,1)S(1)} %get-tuple-element.47), channel_id=1, source_target_pairs={{0,2},{1,3},{2,4},{3,5},{4,6},{5,7},{6,0},{7,1},{8,10},{9,11},{10,... | collective-permute-start | bytes 196616 | tf_op jit(solution)/shard_map/ppermute | solution.py:475
  198.6 10.2 %collective-permute-start.21 = (bf16[2,128,128]{2,1,0:T(8,128)(2,1)S(1)}, bf16[2,128,128]{2,1,0:T(8,128)(2,1)S(1)}, u32[]{:S(2)}, u32[]{:S(2)}) collective-permute-start(bf16[2,128,128]{2,1,0:T(8,128)(2,1)S(1)} %get-tuple-element.48), channel_id=1, source_target_pairs={{0,3},{1,4},{2,5},{3,6},{4,7},{5,0},{6,1},{7,2},{8,11},{9,12},{10,... | collective-permute-start | bytes 196616 | tf_op jit(solution)/shard_map/ppermute | solution.py:475
  201.0 8.9 %collective-permute-start.22 = (bf16[2,128,128]{2,1,0:T(8,128)(2,1)S(1)}, bf16[2,128,128]{2,1,0:T(8,128)(2,1)S(1)}, u32[]{:S(2)}, u32[]{:S(2)}) collective-permute-start(bf16[2,128,128]{2,1,0:T(8,128)(2,1)S(1)} %get-tuple-element.49), channel_id=1, source_target_pairs={{0,4},{1,5},{2,6},{3,7},{4,0},{5,1},{6,2},{7,3},{8,12},{9,13},{10,... | collective-permute-start | bytes 196616 | tf_op jit(solution)/shard_map/ppermute | solution.py:475
  203.0 7.7 %collective-permute-start.23 = (bf16[2,128,128]{2,1,0:T(8,128)(2,1)S(1)}, bf16[2,128,128]{2,1,0:T(8,128)(2,1)S(1)}, u32[]{:S(2)}, u32[]{:S(2)}) collective-permute-start(bf16[2,128,128]{2,1,0:T(8,128)(2,1)S(1)} %get-tuple-element.50), channel_id=1, source_target_pairs={{0,5},{1,6},{2,7},{3,0},{4,1},{5,2},{6,3},{7,4},{8,13},{9,14},{10,... | collective-permute-start | bytes 196616 | tf_op jit(solution)/shard_map/ppermute | solution.py:475
  206.0 7.1 %collective-permute-start.24 = (bf16[2,128,128]{2,1,0:T(8,128)(2,1)S(1)}, bf16[2,128,128]{2,1,0:T(8,128)(2,1)S(1)}, u32[]{:S(2)}, u32[]{:S(2)}) collective-permute-start(bf16[2,128,128]{2,1,0:T(8,128)(2,1)S(1)} %get-tuple-element.51), channel_id=1, source_target_pairs={{0,6},{1,7},{2,0},{3,1},{4,2},{5,3},{6,4},{7,5},{8,14},{9,15},{10,... | collective-permute-start | bytes 196616 | tf_op jit(solution)/shard_map/ppermute | solution.py:475
  (25 other events, 208.7 us)

commit v5 on v4

--- a/solution.py
+++ b/solution.py
@@ -444,7 +444,12 @@
     packed = pack(me, requests[0].T, features)
     sources = [packed[0]]
     for q in range(1, N_SRC):
-        sources.append(lax.ppermute(packed[q], "dom", meet_pairs(q // 2, q % 2)))
+        if q in LATE:
+            d = 1 if q % 2 == 0 else RING - 1
+            hop = lax.ppermute(packed[q], "dom", meet_pairs(d, q % 2))
+            sources.append(lax.ppermute(hop, "dom", meet_pairs(d, 0)))
+        else:
+            sources.append(lax.ppermute(packed[q], "dom", meet_pairs(q // 2, q % 2)))
 
     todo = plan(me, counts[:, 0], tile_block, tile_count)
     nbr_t = turn_nbr(local_nbr)

time: 241 us -> 249 us (1.033)
  waiting for transfers between devices: 85.2 us -> 98.1 us
  starting transfers between devices: 80.8 us -> 76.9 us
    ppermute x0 -> x4, waiting for transfers between devices: none -> 15 us  [the longest x2 15 us: body(): sources.append(lax.ppermute(hop, 'dom', meet_pairs(d, 0)))]
    ppermute x7, starting transfers between devices: 16.5 us -> 26.7 us  [body(): w_all.append(lax.ppermute(w_t, 'col', col_pairs(k)))]
    ppermute x7 -> x5, waiting for transfers between devices: 28.9 us -> 18.8 us  [body(): sources.append(lax.ppermute(packed[q], 'dom', meet_pairs(q // 2, q % 2)))]
    ppermute x7 -> x5, starting transfers between devices: 14.9 us -> 6.01 us  [body(): sources.append(lax.ppermute(packed[q], 'dom', meet_pairs(q // 2, q % 2)))]
    ppermute x0 -> x4, starting transfers between devices: none -> 6.18 us  [the longest x2 3.51 us: body(): hop = lax.ppermute(packed[q], 'dom', meet_pairs(d, q % 2))]
    all_to_all x1, starting transfers between devices: 10.2 us -> 4.69 us  [body(): lax.all_to_all(own_sum.reshape(N_COL, ROW_BLK, ROWS, ROWS), 'col', 0, 0,...]
    ppermute x3, waiting for transfers between devices: 1.34 us -> 6.55 us  [body(): lists.append(lax.ppermute(todo, 'dom', ring_pairs(m)))]
    ppermute x7, waiting for transfers between devices: 3.79 us -> 6.59 us  [body(): lax.ppermute(parts[k], 'col', col_pairs(k))]
  transfers between devices with their start and end apart: 35 -> 37, of which waited for: 16 -> 17; matrix products, arithmetic and copies ran while one was open for 0% -> 0% of each run, Pallas kernels for 14% -> 13%
where the time goes in v5:
time: 249 us; the launch traced here: 248 us
  waiting for transfers between devices  98.1 us (39%)
  starting transfers between devices  76.9 us (31%)
  Pallas kernels  37.4 us (15%)
  blocking collectives  21.1 us (8%)
  local copies, waits for them, and re-layouts  14.5 us (6%)
    ppermute x7, waiting for transfers between devices, body(): w_all.append(lax.ppermute(w_t, 'col', col_pairs(k)))  34.3 us
    ppermute x7, starting transfers between devices, body(): w_all.append(lax.ppermute(w_t, 'col', col_pairs(k)))  26.7 us
    all_to_all x1, blocking collectives, body(): return lax.all_to_all(y, 'col', 0, 0, tiled=True).reshape(-1, ROWS)  21.1 us
    ppermute x5, waiting for transfers between devices, body(): sources.append(lax.ppermute(packed[q], 'dom', meet_pairs(q // 2, q % 2)))  18.8 us
    ppermute x2, waiting for transfers between devices, body(): sources.append(lax.ppermute(hop, 'dom', meet_pairs(d, 0)))  15 us
    ppermute x7, starting transfers between devices, body(): lax.ppermute(parts[k], 'col', col_pairs(k))  15 us
    ppermute x3, waiting for transfers between devices, body(): agg_here.append(lax.ppermute(agg_parts[m], 'dom', ring_pairs(RING - m)))  14.6 us
    unnamed x45, local copies, waits for them, and re-layouts  14.5 us
  transfers between devices with their start and end apart: 37, of which 17 were waited for; matrix products, arithmetic and copies ran while one was open for 0% of the time, Pallas kernels for 13%

profile of v5, /device:TPU:1, one launch (start us, length us, event | category | flops | bytes accessed | tf_op | source)
XLA Modules:
  0.0 248.3 jit_solution(2729208642985202037)
XLA Ops:
  2.2 2.5 %collective-permute-start.28 = (bf16[1024,128]{1,0:T(8,128)(2,1)S(1)}, bf16[1024,128]{1,0:T(8,128)(2,1)S(1)}, u32[]{:S(2)}, u32[]{:S(2)}) collective-permute-start(bf16[1024,128]{1,0:T(8,128)(2,1)S(1)} %turn_weights.1.refs_0_), channel_id=1, source_target_pairs={{0,1},{1,2},{2,3},{3,4},{4,5},{5,6},{6,7},{7,0},{8,9},{9,10},{10,1... | collective-permute-start | bytes 786440 | tf_op jit(solution)/shard_map/ppermute | solution.py:463
  4.7 3.0 %collective-permute-start.29 = (bf16[1024,128]{1,0:T(8,128)(2,1)S(1)}, bf16[1024,128]{1,0:T(8,128)(2,1)S(1)}, u32[]{:S(2)}, u32[]{:S(2)}) collective-permute-start(bf16[1024,128]{1,0:T(8,128)(2,1)S(1)} %turn_weights.1.refs_0_), channel_id=1, source_target_pairs={{0,2},{1,3},{2,4},{3,5},{4,6},{5,7},{6,0},{7,1},{8,10},{9,11},{10,... | collective-permute-start | bytes 786440 | tf_op jit(solution)/shard_map/ppermute | solution.py:463
  7.7 2.9 %pack.1 = (bf16[32,128,128]{2,1,0:T(8,128)(2,1)S(1)}, bf16[32,128,128]{2,1,0:T(8,128)(2,1)S(1)}, bf16[32,128,128]{2,1,0:T(8,128)(2,1)S(1)}, bf16[32,128,128]{2,1...) custom-call(s32[1]{0:T(128)} %bitcast.me, ...), custom_call_target="tpu_custom_call" | custom-call | flops 1000000000 | bytes 10000000 | tf_op jit(solution)/shard_map/pack/pallas_call | solution.py:103
  13.2 5.2 %plan.1.refs_0_ = s32[3200]{0:T(1024)S(1)} custom-call(s32[1]{0:T(128)} %bitcast.me, s32[32]{0:T(128)S(1)} %bitcast.9, s32[16,32]{1,0:T(8,128)S(1)} %copy-done.14, s32[16]{0:T(128)S(1)} %copy-done.17), custom_call_target="tpu_custom_call" | custom-call | flops 2000000000 | bytes 1000000 | tf_op jit(solution)/shard_map/plan/pallas_call | solution.py:212
  20.3 2.4 collective-permute-done.refs_1_
  24.5 2.5 %collective-permute-done.1.refs_2_ = s32[3200]{0:T(1024)S(1)} collective-permute-done((s32[3200]{0:T(1024)S(1)}, s32[3200]{0:T(1024)S(1)}, u32[]{:S(2)}, u32[]{:S(2)}) %collective-permute-start.1) | collective-permute-done | bytes 12832 | tf_op jit(solution)/shard_map/ppermute | solution.py:459
  29.6 3.8 %collective-permute-start.30 = (bf16[1024,128]{1,0:T(8,128)(2,1)S(1)}, bf16[1024,128]{1,0:T(8,128)(2,1)S(1)}, u32[]{:S(2)}, u32[]{:S(2)}) collective-permute-start(bf16[1024,128]{1,0:T(8,128)(2,1)S(1)} %turn_weights.1.refs_0_), channel_id=1, source_target_pairs={{0,3},{1,4},{2,5},{3,6},{4,7},{5,0},{6,1},{7,2},{8,11},{9,12},{10,... | collective-permute-start | bytes 786440 | tf_op jit(solution)/shard_map/ppermute | solution.py:463
  33.8 4.5 %collective-permute-start.32 = (bf16[1024,128]{1,0:T(8,128)(2,1)S(1)}, bf16[1024,128]{1,0:T(8,128)(2,1)S(1)}, u32[]{:S(2)}, u32[]{:S(2)}) collective-permute-start(bf16[1024,128]{1,0:T(8,128)(2,1)S(1)} %turn_weights.1.refs_0_), channel_id=1, source_target_pairs={{0,5},{1,6},{2,7},{3,0},{4,1},{5,2},{6,3},{7,4},{8,13},{9,14},{10,... | collective-permute-start | bytes 786440 | tf_op jit(solution)/shard_map/ppermute | solution.py:463
  38.3 20.1 %collective-permute-done.30.refs_3_ = bf16[1024,128]{1,0:T(8,128)(2,1)S(1)} collective-permute-done((bf16[1024,128]{1,0:T(8,128)(2,1)S(1)}, bf16[1024,128]{1,0:T(8,128)(2,1)S(1)}, u32[]{:S(2)}, u32[]{:S(2)}) %collective-permute-start.30) | collective-permute-done | bytes 262176 | tf_op jit(solution)/shard_map/ppermute | solution.py:463
  58.4 3.5 %collective-permute-start.8 = (bf16[32,128,128]{2,1,0:T(8,128)(2,1)S(1)}, bf16[32,128,128]{2,1,0:T(8,128)(2,1)S(1)}, u32[]{:S(2)}, u32[]{:S(2)}) collective-permute-start(bf16[32,128,128]{2,1,0:T(8,128)(2,1)S(1)} %get-tuple-element.34), channel_id=1, source_target_pairs={{0,56},{8,192},{16,8},{24,208},{32,24},{40,224},{48,40},{56,240},{... | collective-permute-start | bytes 3145736 | tf_op jit(solution)/shard_map/ppermute | solution.py:449
  61.9 7.2 %collective-permute-start.33 = (bf16[1024,128]{1,0:T(8,128)(2,1)S(1)}, bf16[1024,128]{1,0:T(8,128)(2,1)S(1)}, u32[]{:S(2)}, u32[]{:S(2)}) collective-permute-start(bf16[1024,128]{1,0:T(8,128)(2,1)S(1)} %turn_weights.1.refs_0_), channel_id=1, source_target_pairs={{0,6},{1,7},{2,0},{3,1},{4,2},{5,3},{6,4},{7,5},{8,14},{9,15},{10,... | collective-permute-start | bytes 786440 | tf_op jit(solution)/shard_map/ppermute | solution.py:463
  69.2 9.3 %collective-permute-done.33.refs_6_ = bf16[1024,128]{1,0:T(8,128)(2,1)S(1)} collective-permute-done((bf16[1024,128]{1,0:T(8,128)(2,1)S(1)}, bf16[1024,128]{1,0:T(8,128)(2,1)S(1)}, u32[]{:S(2)}, u32[]{:S(2)}) %collective-permute-start.33) | collective-permute-done | bytes 262176 | tf_op jit(solution)/shard_map/ppermute | solution.py:463
  78.4 5.3 %collective-permute-start.34 = (bf16[1024,128]{1,0:T(8,128)(2,1)S(1)}, bf16[1024,128]{1,0:T(8,128)(2,1)S(1)}, u32[]{:S(2)}, u32[]{:S(2)}) collective-permute-start(bf16[1024,128]{1,0:T(8,128)(2,1)S(1)} %turn_weights.1.refs_0_), channel_id=1, source_target_pairs={{0,7},{1,0},{2,1},{3,2},{4,3},{5,4},{6,5},{7,6},{8,15},{9,8},{10,9... | collective-permute-start | bytes 786440 | tf_op jit(solution)/shard_map/ppermute | solution.py:463
  83.7 4.9 %collective-permute-done.34.refs_7_ = bf16[1024,128]{1,0:T(8,128)(2,1)S(1)} collective-permute-done((bf16[1024,128]{1,0:T(8,128)(2,1)S(1)}, bf16[1024,128]{1,0:T(8,128)(2,1)S(1)}, u32[]{:S(2)}, u32[]{:S(2)}) %collective-permute-start.34) | collective-permute-done | bytes 262176 | tf_op jit(solution)/shard_map/ppermute | solution.py:463
  95.3 18.1 %collective-permute-done.5.refs_7_ = bf16[32,128,128]{2,1,0:T(8,128)(2,1)S(1)} collective-permute-done((bf16[32,128,128]{2,1,0:T(8,128)(2,1)S(1)}, bf16[32,128,128]{2,1,0:T(8,128)(2,1)S(1)}, u32[]{:S(2)}, u32[]{:S(2)}) %collective-permute-start.5) | collective-permute-done | bytes 1048608 | tf_op jit(solution)/shard_map/ppermute | solution.py:452
  113.7 2.9 %collective-permute-start.16 = (s32[1024,128]{1,0:T(8,128)S(1)}, s32[1024,128]{1,0:T(8,128)S(1)}, u32[]{:S(2)}, u32[]{:S(2)}) collective-permute-start(s32[1024,128]{1,0:T(8,128)S(1)} %turn_nbr.1.refs_10_.refs_6_), channel_id=1, source_target_pairs={{0,32},{8,136},{16,48},{24,152},{32,0},{40,168},{48,16},{56,184},{... | collective-permute-start | bytes 1572872 | tf_op jit(solution)/shard_map/ppermute | solution.py:460
  117.0 3.3 %collective-permute-start.17 = (s32[1024,128]{1,0:T(8,128)S(1)}, s32[1024,128]{1,0:T(8,128)S(1)}, u32[]{:S(2)}, u32[]{:S(2)}) collective-permute-start(s32[1024,128]{1,0:T(8,128)S(1)} %turn_nbr.1.refs_10_.refs_6_), channel_id=1, source_target_pairs={{0,48},{8,200},{16,0},{24,216},{32,16},{40,232},{48,32},{56,248},{... | collective-permute-start | bytes 1572872 | tf_op jit(solution)/shard_map/ppermute | solution.py:460
  120.6 15.0 %collective-permute-done.9.refs_9_.refs_5_ = bf16[32,128,128]{2,1,0:T(8,128)(2,1)S(1)} collective-permute-done((bf16[32,128,128]{2,1,0:T(8,128)(2,1)S(1)}, bf16[32,128,128]{2,1,0:T(8,128)(2,1)S(1)}, u32[]{:S(2)}, u32[]{:S(2)}) %collective-permute-start.9) | collective-permute-done | bytes 1048608 | tf_op jit(solution)/shard_map/ppermute | solution.py:450
  135.7 5.1 %own_rows.1 = (bf16[16,128,128]{2,1,0:T(8,128)(2,1)S(1)}, bf16[16,128,128]{2,1,0:T(8,128)(2,1)S(1)}, bf16[16,128,128]{2,1,0:T(8,128)(2,1)S(1)}, bf16[16,128,128]{2,1,0:T(8,128)(2,1)S(1)}) custom-call(s32[3200]{0:T(1024)S(1)} %plan.1.refs_0_, s32[3200]{0:T(1024)S(1)} %collective-permute-done.refs_1_, s32[3200]{0:T(1024)S(1)} %collective-permute-done.1.refs_2_, ...), custom_call_target="tpu_custom_call" | custom-call | flops 1000000000 | bytes 10000000 | tf_op jit(solution)/shard_map/own_rows/pallas_call | solution.py:249
  143.6 10.3 %early.1.refs_10_ = f32[65,128,128]{2,1,0:T(8,128)S(1)} custom-call(s32[3200]{0:T(1024)S(1)} %plan.1.refs_0_, s32[3200]{0:T(1024)S(1)} %collective-permute-done.refs_1_, s32[3200]{0:T(1024)S(1)} %collective-permute-done.1.refs_2_, s32[3200]{0:T(1024)S(1)} %collective-permute-done.2.refs_3_, bf16[32,128,128]{2,1,0:T(8,128)(2,1)S(1)} %get-tuple-element.29.refs_4_, ...), custom_call_target="tpu_custom_call" | custom-call | flops 10000000000 | bytes 20000000 | tf_op jit(solution)/shard_map/early/pallas_call | solution.py:320
  159.2 4.7 %all-to-all-start = ((bf16[8,2,128,128]{3,2,1,0:T(8,128)(2,1)}), bf16[8,2,128,128]{3,2,1,0:T(8,128)(2,1)S(1)}, u32[]{:S(2)}, u32[]{:S(2)}) async-start(bf16[8,2,128,128]{3,2,1,0:T(8,128)(2,1)} %bitcast.5), calls=%async_computation | async-start | bytes 1048576 | tf_op jit(solution)/shard_map/all_to_all | solution.py:478
  169.5 2.2 copy-done.21
  171.7 6.4 %late.1 = (bf16[16,128,128]{2,1,0:T(8,128)(2,1)S(1)}, bf16[16,128,128]{2,1,0:T(8,128)(2,1)}, bf16[16,128,128]{2,1,0:T(8,128)(2,1)}, bf16[16,128,128]{2,1,0:T(8,128)(2,1)}, f32[65,128,128]{2,1,0:T(8,128)S(1)}) custom-call(s32[3200]{0:T(1024)S(1)} %plan.1.refs_0_, s32[3200]{0:T(1024)S(1)} %collective-permute-done.refs_1_, ...), custom_call_target="tpu_custom_call", output_to_operand_aliasing={{4}: (10, {})} | custom-call | flops 10000000000 | bytes 20000000 | tf_op jit(solution)/shard_map/late/pallas_call | solution.py:354
  178.8 4.1 %collective-permute-start.18 = (bf16[16,128,128]{2,1,0:T(8,128)(2,1)}, bf16[16,128,128]{2,1,0:T(8,128)(2,1)S(1)}, u32[]{:S(2)}, u32[]{:S(2)}) collective-permute-start(bf16[16,128,128]{2,1,0:T(8,128)(2,1)} %get-tuple-element.42), channel_id=1, source_target_pairs={{0,48},{8,200},{16,0},{24,216},{32,16},{40,232},{48,32},{56,248},{... | collective-permute-start | bytes 1572872 | tf_op jit(solution)/shard_map/ppermute | solution.py:475
  183.5 11.5 %collective-permute-done.18.b = bf16[16,128,128]{2,1,0:T(8,128)(2,1)S(1)} collective-permute-done((bf16[16,128,128]{2,1,0:T(8,128)(2,1)}, bf16[16,128,128]{2,1,0:T(8,128)(2,1)S(1)}, u32[]{:S(2)}, u32[]{:S(2)}) %collective-permute-start.18) | collective-permute-done | bytes 524320 | tf_op jit(solution)/shard_map/ppermute | solution.py:475
  195.0 3.1 %collective-permute-done.20.d = bf16[16,128,128]{2,1,0:T(8,128)(2,1)} collective-permute-done((bf16[16,128,128]{2,1,0:T(8,128)(2,1)}, bf16[16,128,128]{2,1,0:T(8,128)(2,1)}, u32[]{:S(2)}, u32[]{:S(2)}) %collective-permute-start.20) | collective-permute-done | bytes 524320 | tf_op jit(solution)/shard_map/ppermute | solution.py:475
  204.3 2.4 collective-permute-start.23
  208.8 2.4 collective-permute-start.25
  211.2 3.3 %collective-permute-start.26 = (bf16[2,128,128]{2,1,0:T(8,128)(2,1)S(1)}, bf16[2,128,128]{2,1,0:T(8,128)(2,1)S(1)}, u32[]{:S(2)}, u32[]{:S(2)}) collective-permute-start(bf16[2,128,128]{2,1,0:T(8,128)(2,1)S(1)} %get-tuple-element.51), channel_id=1, source_target_pairs={{0,6},{1,7},{2,0},{3,1},{4,2},{5,3},{6,4},{7,5},{8,14},{9,15},{10,... | collective-permute-start | bytes 196616 | tf_op jit(solution)/shard_map/ppermute | solution.py:480
  217.1 3.6 %collective-permute-done.25.refs_5_ = bf16[2,128,128]{2,1,0:T(8,128)(2,1)S(1)} collective-permute-done((bf16[2,128,128]{2,1,0:T(8,128)(2,1)S(1)}, bf16[2,128,128]{2,1,0:T(8,128)(2,1)S(1)}, u32[]{:S(2)}, u32[]{:S(2)}) %collective-permute-start.25) | collective-permute-done | bytes 65568 | tf_op jit(solution)/shard_map/ppermute | solution.py:480
  222.2 4.1 %project.1 = bf16[8,256,128]{2,1,0:T(8,128)(2,1)S(1)} custom-call(s32[1]{0:T(128)} %bitcast.me, s32[1]{0:T(128)} %bitcast.1.column, bf16[8,2,128,128]{3,2,1,0:T(8,128)(2,1)S(1)} %all-to-all-done.xs, bf16[2,128,128]{2,1,0:T(8,128)(2,1)S(1)} %get-tuple-element.45.refs_0_, bf16[2,128,128]{2,1,0:T(8,128)(2,1)S(1)} %collective-permute-done.21.refs_1_, ...), custom_call_target="tpu_custom_call" | custom-call | flops 1000000000 | bytes 5000000 | tf_op jit(solution)/shard_map/project/pallas_call | solution.py:429
  226.3 21.1 %all_to_all.10 = bf16[8,256,128]{2,1,0:T(8,128)(2,1)S(1)} all-to-all(bf16[8,256,128]{2,1,0:T(8,128)(2,1)S(1)} %project.1), channel_id=1, replica_groups=mesh['dom'=32,'col'=8] {'col'}, dimensions={0} | all-to-all | bytes 1048576 | tf_op jit(solution)/shard_map/all_to_all | solution.py:482
  (99 shorter events, 47.3 us)
Async XLA Ops:
  2.2 31.2 %collective-permute-start.28 = (bf16[1024,128]{1,0:T(8,128)(2,1)S(1)}, bf16[1024,128]{1,0:T(8,128)(2,1)S(1)}, u32[]{:S(2)}, u32[]{:S(2)}) collective-permute-start(bf16[1024,128]{1,0:T(8,128)(2,1)S(1)} %turn_weights.1.refs_0_), channel_id=1, source_target_pairs={{0,1},{1,2},{2,3},{3,4},{4,5},{5,6},{6,7},{7,0},{8,9},{9,10},{10,1... | collective-permute-start | bytes 786440 | tf_op jit(solution)/shard_map/ppermute | solution.py:463
  4.7 29.1 %collective-permute-start.29 = (bf16[1024,128]{1,0:T(8,128)(2,1)S(1)}, bf16[1024,128]{1,0:T(8,128)(2,1)S(1)}, u32[]{:S(2)}, u32[]{:S(2)}) collective-permute-start(bf16[1024,128]{1,0:T(8,128)(2,1)S(1)} %turn_weights.1.refs_0_), channel_id=1, source_target_pairs={{0,2},{1,3},{2,4},{3,5},{4,6},{5,7},{6,0},{7,1},{8,10},{9,11},{10,... | collective-permute-start | bytes 786440 | tf_op jit(solution)/shard_map/ppermute | solution.py:463
  10.7 79.5 %collective-permute-start.3 = (bf16[32,128,128]{2,1,0:T(8,128)(2,1)S(1)}, bf16[32,128,128]{2,1,0:T(8,128)(2,1)S(1)}, u32[]{:S(2)}, u32[]{:S(2)}) collective-permute-start(bf16[32,128,128]{2,1,0:T(8,128)(2,1)S(1)} %get-tuple-element.30), channel_id=1, source_target_pairs={{0,8},{8,0},{16,24},{24,16},{32,40},{40,32},{48,56},{56,48},{64,72... | collective-permute-start | bytes 3145736 | tf_op jit(solution)/shard_map/ppermute | solution.py:452
  12.0 78.4 %collective-permute-start.4 = (bf16[32,128,128]{2,1,0:T(8,128)(2,1)S(1)}, bf16[32,128,128]{2,1,0:T(8,128)(2,1)S(1)}, u32[]{:S(2)}, u32[]{:S(2)}) collective-permute-start(bf16[32,128,128]{2,1,0:T(8,128)(2,1)S(1)} %get-tuple-element.31), channel_id=1, source_target_pairs={{0,64},{8,24},{16,80},{24,40},{32,96},{40,56},{48,112},{56,8},{64,... | collective-permute-start | bytes 3145736 | tf_op jit(solution)/shard_map/ppermute | solution.py:452
  29.6 28.8 %collective-permute-start.30 = (bf16[1024,128]{1,0:T(8,128)(2,1)S(1)}, bf16[1024,128]{1,0:T(8,128)(2,1)S(1)}, u32[]{:S(2)}, u32[]{:S(2)}) collective-permute-start(bf16[1024,128]{1,0:T(8,128)(2,1)S(1)} %turn_weights.1.refs_0_), channel_id=1, source_target_pairs={{0,3},{1,4},{2,5},{3,6},{4,7},{5,0},{6,1},{7,2},{8,11},{9,12},{10,... | collective-permute-start | bytes 786440 | tf_op jit(solution)/shard_map/ppermute | solution.py:463
  33.4 25.1 %collective-permute-start.31 = (bf16[1024,128]{1,0:T(8,128)(2,1)S(1)}, bf16[1024,128]{1,0:T(8,128)(2,1)S(1)}, u32[]{:S(2)}, u32[]{:S(2)}) collective-permute-start(bf16[1024,128]{1,0:T(8,128)(2,1)S(1)} %turn_weights.1.refs_0_), channel_id=1, source_target_pairs={{0,4},{1,5},{2,6},{3,7},{4,0},{5,1},{6,2},{7,3},{8,12},{9,13},{10,... | collective-permute-start | bytes 786440 | tf_op jit(solution)/shard_map/ppermute | solution.py:463
  33.8 28.1 %collective-permute-start.32 = (bf16[1024,128]{1,0:T(8,128)(2,1)S(1)}, bf16[1024,128]{1,0:T(8,128)(2,1)S(1)}, u32[]{:S(2)}, u32[]{:S(2)}) collective-permute-start(bf16[1024,128]{1,0:T(8,128)(2,1)S(1)} %turn_weights.1.refs_0_), channel_id=1, source_target_pairs={{0,5},{1,6},{2,7},{3,0},{4,1},{5,2},{6,3},{7,4},{8,13},{9,14},{10,... | collective-permute-start | bytes 786440 | tf_op jit(solution)/shard_map/ppermute | solution.py:463
  58.4 33.6 %collective-permute-start.6 = (bf16[32,128,128]{2,1,0:T(8,128)(2,1)S(1)}, bf16[32,128,128]{2,1,0:T(8,128)(2,1)S(1)}, u32[]{:S(2)}, u32[]{:S(2)}) collective-permute-start(bf16[32,128,128]{2,1,0:T(8,128)(2,1)S(1)} %get-tuple-element.33), channel_id=1, source_target_pairs={{0,64},{8,24},{16,80},{24,40},{32,96},{40,56},{48,112},{56,8},{64,... | collective-permute-start | bytes 3145736 | tf_op jit(solution)/shard_map/ppermute | solution.py:449
  58.4 34.4 %collective-permute-start.8 = (bf16[32,128,128]{2,1,0:T(8,128)(2,1)S(1)}, bf16[32,128,128]{2,1,0:T(8,128)(2,1)S(1)}, u32[]{:S(2)}, u32[]{:S(2)}) collective-permute-start(bf16[32,128,128]{2,1,0:T(8,128)(2,1)S(1)} %get-tuple-element.34), channel_id=1, source_target_pairs={{0,56},{8,192},{16,8},{24,208},{32,24},{40,224},{48,40},{56,240},{... | collective-permute-start | bytes 3145736 | tf_op jit(solution)/shard_map/ppermute | solution.py:449
  61.9 16.5 %collective-permute-start.33 = (bf16[1024,128]{1,0:T(8,128)(2,1)S(1)}, bf16[1024,128]{1,0:T(8,128)(2,1)S(1)}, u32[]{:S(2)}, u32[]{:S(2)}) collective-permute-start(bf16[1024,128]{1,0:T(8,128)(2,1)S(1)} %turn_weights.1.refs_0_), channel_id=1, source_target_pairs={{0,6},{1,7},{2,0},{3,1},{4,2},{5,3},{6,4},{7,5},{8,14},{9,15},{10,... | collective-permute-start | bytes 786440 | tf_op jit(solution)/shard_map/ppermute | solution.py:463
  88.6 24.8 %collective-permute-start.5 = (bf16[32,128,128]{2,1,0:T(8,128)(2,1)S(1)}, bf16[32,128,128]{2,1,0:T(8,128)(2,1)S(1)}, u32[]{:S(2)}, u32[]{:S(2)}) collective-permute-start(bf16[32,128,128]{2,1,0:T(8,128)(2,1)S(1)} %get-tuple-element.32), channel_id=1, source_target_pairs={{0,24},{8,64},{16,40},{24,80},{32,56},{40,96},{48,8},{56,112},{64,... | collective-permute-start | bytes 3145736 | tf_op jit(solution)/shard_map/ppermute | solution.py:452
  90.2 23.5 %collective-permute-start.10 = (bf16[32,128,128]{2,1,0:T(8,128)(2,1)S(1)}, bf16[32,128,128]{2,1,0:T(8,128)(2,1)S(1)}, u32[]{:S(2)}, u32[]{:S(2)}) collective-permute-start(bf16[32,128,128]{2,1,0:T(8,128)(2,1)S(1)} %get-tuple-element.35), channel_id=1, source_target_pairs={{0,192},{8,56},{16,208},{24,8},{32,224},{40,24},{48,240},{56,40},{... | collective-permute-start | bytes 3145736 | tf_op jit(solution)/shard_map/ppermute | solution.py:452
  90.4 26.6 %collective-permute-start.11 = (bf16[32,128,128]{2,1,0:T(8,128)(2,1)S(1)}, bf16[32,128,128]{2,1,0:T(8,128)(2,1)S(1)}, u32[]{:S(2)}, u32[]{:S(2)}) collective-permute-start(bf16[32,128,128]{2,1,0:T(8,128)(2,1)S(1)} %get-tuple-element.36), channel_id=1, source_target_pairs={{0,56},{8,192},{16,8},{24,208},{32,24},{40,224},{48,40},{56,240},{... | collective-permute-start | bytes 3145736 | tf_op jit(solution)/shard_map/ppermute | solution.py:452
  92.1 28.4 %collective-permute-start.7 = (bf16[32,128,128]{2,1,0:T(8,128)(2,1)S(1)}, bf16[32,128,128]{2,1,0:T(8,128)(2,1)S(1)}, u32[]{:S(2)}, u32[]{:S(2)}) collective-permute-start(bf16[32,128,128]{2,1,0:T(8,128)(2,1)S(1)} %collective-permute-done.6), channel_id=1, source_target_pairs={{0,64},{8,24},{16,80},{24,40},{32,96},{40,56},{48,112},{56,8},{64,... | collective-permute-start | bytes 3145736 | tf_op jit(solution)/shard_map/ppermute | solution.py:450
  92.8 42.8 %collective-permute-start.9 = (bf16[32,128,128]{2,1,0:T(8,128)(2,1)S(1)}, bf16[32,128,128]{2,1,0:T(8,128)(2,1)S(1)}, u32[]{:S(2)}, u32[]{:S(2)}) collective-permute-start(bf16[32,128,128]{2,1,0:T(8,128)(2,1)S(1)} %collective-permute-done.8), channel_id=1, source_target_pairs={{0,192},{8,56},{16,208},{24,8},{32,224},{40,24},{48,240},{56,40},{... | collective-permute-start | bytes 3145736 | tf_op jit(solution)/shard_map/ppermute | solution.py:450
  113.4 29.4 %collective-permute-start.15 = (s32[1024,128]{1,0:T(8,128)S(1)}, s32[1024,128]{1,0:T(8,128)S(1)}, u32[]{:S(2)}, u32[]{:S(2)}) collective-permute-start(s32[1024,128]{1,0:T(8,128)S(1)} %turn_nbr.1.refs_10_.refs_6_), channel_id=1, source_target_pairs={{0,16},{8,72},{16,32},{24,88},{32,48},{40,104},{48,0},{56,120},{64... | collective-permute-start | bytes 1572872 | tf_op jit(solution)/shard_map/ppermute | solution.py:460
  113.7 29.2 %collective-permute-start.16 = (s32[1024,128]{1,0:T(8,128)S(1)}, s32[1024,128]{1,0:T(8,128)S(1)}, u32[]{:S(2)}, u32[]{:S(2)}) collective-permute-start(s32[1024,128]{1,0:T(8,128)S(1)} %turn_nbr.1.refs_10_.refs_6_), channel_id=1, source_target_pairs={{0,32},{8,136},{16,48},{24,152},{32,0},{40,168},{48,16},{56,184},{... | collective-permute-start | bytes 1572872 | tf_op jit(solution)/shard_map/ppermute | solution.py:460
  117.0 26.5 %collective-permute-start.17 = (s32[1024,128]{1,0:T(8,128)S(1)}, s32[1024,128]{1,0:T(8,128)S(1)}, u32[]{:S(2)}, u32[]{:S(2)}) collective-permute-start(s32[1024,128]{1,0:T(8,128)S(1)} %turn_nbr.1.refs_10_.refs_6_), channel_id=1, source_target_pairs={{0,48},{8,200},{16,0},{24,216},{32,16},{40,232},{48,32},{56,248},{... | collective-permute-start | bytes 1572872 | tf_op jit(solution)/shard_map/ppermute | solution.py:460
  120.5 88.2 %collective-permute-start.35 = (bf16[8,1024,128]{2,1,0:T(8,128)(2,1)S(1)}, bf16[8,1024,128]{2,1,0:T(8,128)(2,1)}, u32[]{:S(2)}, u32[]{:S(2)}) collective-permute-start(bf16[8,1024,128]{2,1,0:T(8,128)(2,1)S(1)} %gather_weights.1.refs_8_), channel_id=1, source_target_pairs={{0,8},{8,0},{16,24},{24,16},{32,40},{40,32},{48,56},{56,48},{64,72... | collective-permute-start | bytes 6291464 | tf_op jit(solution)/shard_map/ppermute | solution.py:465
  140.8 15.2 %collective-permute-start.12 = (bf16[16,128,128]{2,1,0:T(8,128)(2,1)S(1)}, bf16[16,128,128]{2,1,0:T(8,128)(2,1)S(1)}, u32[]{:S(2)}, u32[]{:S(2)}) collective-permute-start(bf16[16,128,128]{2,1,0:T(8,128)(2,1)S(1)} %get-tuple-element.38), channel_id=1, source_target_pairs={{0,48},{8,200},{16,0},{24,216},{32,16},{40,232},{48,32},{56,248},{... | collective-permute-start | bytes 1572872 | tf_op jit(solution)/shard_map/ppermute | solution.py:470
  142.9 13.1 %collective-permute-start.13 = (bf16[16,128,128]{2,1,0:T(8,128)(2,1)S(1)}, bf16[16,128,128]{2,1,0:T(8,128)(2,1)S(1)}, u32[]{:S(2)}, u32[]{:S(2)}) collective-permute-start(bf16[16,128,128]{2,1,0:T(8,128)(2,1)S(1)} %get-tuple-element.39), channel_id=1, source_target_pairs={{0,32},{8,136},{16,48},{24,152},{32,0},{40,168},{48,16},{56,184},{... | collective-permute-start | bytes 1572872 | tf_op jit(solution)/shard_map/ppermute | solution.py:470
  142.9 15.2 %collective-permute-start.14 = (bf16[16,128,128]{2,1,0:T(8,128)(2,1)S(1)}, bf16[16,128,128]{2,1,0:T(8,128)(2,1)S(1)}, u32[]{:S(2)}, u32[]{:S(2)}) collective-permute-start(bf16[16,128,128]{2,1,0:T(8,128)(2,1)S(1)} %get-tuple-element.40), channel_id=1, source_target_pairs={{0,16},{8,72},{16,32},{24,88},{32,48},{40,104},{48,0},{56,120},{64... | collective-permute-start | bytes 1572872 | tf_op jit(solution)/shard_map/ppermute | solution.py:470
  159.2 63.0 %all-to-all-start = ((bf16[8,2,128,128]{3,2,1,0:T(8,128)(2,1)}), bf16[8,2,128,128]{3,2,1,0:T(8,128)(2,1)S(1)}, u32[]{:S(2)}, u32[]{:S(2)}) async-start(bf16[8,2,128,128]{3,2,1,0:T(8,128)(2,1)} %bitcast.5), calls=%async_computation | async-start | bytes 1048576 | tf_op jit(solution)/shard_map/all_to_all | solution.py:478
  178.8 16.1 %collective-permute-start.18 = (bf16[16,128,128]{2,1,0:T(8,128)(2,1)}, bf16[16,128,128]{2,1,0:T(8,128)(2,1)S(1)}, u32[]{:S(2)}, u32[]{:S(2)}) collective-permute-start(bf16[16,128,128]{2,1,0:T(8,128)(2,1)} %get-tuple-element.42), channel_id=1, source_target_pairs={{0,48},{8,200},{16,0},{24,216},{32,16},{40,232},{48,32},{56,248},{... | collective-permute-start | bytes 1572872 | tf_op jit(solution)/shard_map/ppermute | solution.py:475
  182.9 12.1 %collective-permute-start.19 = (bf16[16,128,128]{2,1,0:T(8,128)(2,1)}, bf16[16,128,128]{2,1,0:T(8,128)(2,1)}, u32[]{:S(2)}, u32[]{:S(2)}) collective-permute-start(bf16[16,128,128]{2,1,0:T(8,128)(2,1)} %get-tuple-element.43), channel_id=1, source_target_pairs={{0,32},{8,136},{16,48},{24,152},{32,0},{40,168},{48,16},{56,184},{... | collective-permute-start | bytes 1572872 | tf_op jit(solution)/shard_map/ppermute | solution.py:475
  182.9 15.2 %collective-permute-start.20 = (bf16[16,128,128]{2,1,0:T(8,128)(2,1)}, bf16[16,128,128]{2,1,0:T(8,128)(2,1)}, u32[]{:S(2)}, u32[]{:S(2)}) collective-permute-start(bf16[16,128,128]{2,1,0:T(8,128)(2,1)} %get-tuple-element.44), channel_id=1, source_target_pairs={{0,16},{8,72},{16,32},{24,88},{32,48},{40,104},{48,0},{56,120},{64... | collective-permute-start | bytes 1572872 | tf_op jit(solution)/shard_map/ppermute | solution.py:475
  200.7 10.5 %collective-permute-start.21 = (bf16[2,128,128]{2,1,0:T(8,128)(2,1)S(1)}, bf16[2,128,128]{2,1,0:T(8,128)(2,1)S(1)}, u32[]{:S(2)}, u32[]{:S(2)}) collective-permute-start(bf16[2,128,128]{2,1,0:T(8,128)(2,1)S(1)} %get-tuple-element.46), channel_id=1, source_target_pairs={{0,1},{1,2},{2,3},{3,4},{4,5},{5,6},{6,7},{7,0},{8,9},{9,10},{10,1... | collective-permute-start | bytes 196616 | tf_op jit(solution)/shard_map/ppermute | solution.py:480
  202.2 12.3 %collective-permute-start.22 = (bf16[2,128,128]{2,1,0:T(8,128)(2,1)S(1)}, bf16[2,128,128]{2,1,0:T(8,128)(2,1)S(1)}, u32[]{:S(2)}, u32[]{:S(2)}) collective-permute-start(bf16[2,128,128]{2,1,0:T(8,128)(2,1)S(1)} %get-tuple-element.47), channel_id=1, source_target_pairs={{0,2},{1,3},{2,4},{3,5},{4,6},{5,7},{6,0},{7,1},{8,10},{9,11},{10,... | collective-permute-start | bytes 196616 | tf_op jit(solution)/shard_map/ppermute | solution.py:480
  204.3 11.4 %collective-permute-start.23 = (bf16[2,128,128]{2,1,0:T(8,128)(2,1)S(1)}, bf16[2,128,128]{2,1,0:T(8,128)(2,1)S(1)}, u32[]{:S(2)}, u32[]{:S(2)}) collective-permute-start(bf16[2,128,128]{2,1,0:T(8,128)(2,1)S(1)} %get-tuple-element.48), channel_id=1, source_target_pairs={{0,3},{1,4},{2,5},{3,6},{4,7},{5,0},{6,1},{7,2},{8,11},{9,12},{10,... | collective-permute-start | bytes 196616 | tf_op jit(solution)/shard_map/ppermute | solution.py:480
  206.7 10.5 %collective-permute-start.24 = (bf16[2,128,128]{2,1,0:T(8,128)(2,1)S(1)}, bf16[2,128,128]{2,1,0:T(8,128)(2,1)S(1)}, u32[]{:S(2)}, u32[]{:S(2)}) collective-permute-start(bf16[2,128,128]{2,1,0:T(8,128)(2,1)S(1)} %get-tuple-element.49), channel_id=1, source_target_pairs={{0,4},{1,5},{2,6},{3,7},{4,0},{5,1},{6,2},{7,3},{8,12},{9,13},{10,... | collective-permute-start | bytes 196616 | tf_op jit(solution)/shard_map/ppermute | solution.py:480
  208.8 12.0 %collective-permute-start.25 = (bf16[2,128,128]{2,1,0:T(8,128)(2,1)S(1)}, bf16[2,128,128]{2,1,0:T(8,128)(2,1)S(1)}, u32[]{:S(2)}, u32[]{:S(2)}) collective-permute-start(bf16[2,128,128]{2,1,0:T(8,128)(2,1)S(1)} %get-tuple-element.50), channel_id=1, source_target_pairs={{0,5},{1,6},{2,7},{3,0},{4,1},{5,2},{6,3},{7,4},{8,13},{9,14},{10,... | collective-permute-start | bytes 196616 | tf_op jit(solution)/shard_map/ppermute | solution.py:480
  211.2 10.6 %collective-permute-start.26 = (bf16[2,128,128]{2,1,0:T(8,128)(2,1)S(1)}, bf16[2,128,128]{2,1,0:T(8,128)(2,1)S(1)}, u32[]{:S(2)}, u32[]{:S(2)}) collective-permute-start(bf16[2,128,128]{2,1,0:T(8,128)(2,1)S(1)} %get-tuple-element.51), channel_id=1, source_target_pairs={{0,6},{1,7},{2,0},{3,1},{4,2},{5,3},{6,4},{7,5},{8,14},{9,15},{10,... | collective-permute-start | bytes 196616 | tf_op jit(solution)/shard_map/ppermute | solution.py:480
  (27 other events, 228.7 us)
